TPU v7x, 32 devices: a whole 2x2x4 slice. The times are simulated.
32 devices in a mesh: seq: 2 (over y), dp: 16 (over z, x, core).
Axes of the slice: x: 2, y: 2, z: 4, core: 2. Of those that a mesh axis runs over, the one named last changes fastest.
Arguments:
- inputs: bfloat16 [32, 128, 2304], P('dp', 'seq'), may hold values from -6 to 6
- lengths: int32 [32], P('dp'), may hold values from 32 to 128, as said below
- query_weight: bfloat16 [2304, 2304], P(('seq', 'dp')), may hold values from -0.1875 to 0.1875
- key_weight: bfloat16 [2304, 2304], P(('seq', 'dp')), may hold values from -0.1875 to 0.1875
- value_weight: bfloat16 [2304, 2304], P(('seq', 'dp')), may hold values from -0.125 to 0.125
- out_weight: bfloat16 [2304, 2304], P(('seq', 'dp')), may hold values from -2 to 2
- gate_weight: bfloat16 [2304, 5760], P(('seq', 'dp')), may hold values from -0.125 to 0.125
- up_weight: bfloat16 [2304, 5760], P(('seq', 'dp')), may hold values from -0.125 to 0.125
- down_weight: bfloat16 [5760, 2304], P(('seq', 'dp')), may hold values from -0.3125 to 0.3125
- attn_gain: bfloat16 [2304], P(('seq', 'dp')), may hold values from 0.5 to 1.5
- ffn_gain: bfloat16 [2304], P(('seq', 'dp')), may hold values from 0.5 to 1.5
- cotangent: bfloat16 [32, 128, 2304], P('dp', 'seq'), may hold values from -6 to 6
Outputs:
- output: bfloat16 [32, 128, 2304], P('dp', 'seq')
- input_grad: bfloat16 [32, 128, 2304], P('dp', 'seq')
- query_grad: float32 [2304, 2304], P(('seq', 'dp'))
- key_grad: float32 [2304, 2304], P(('seq', 'dp'))
- value_grad: float32 [2304, 2304], P(('seq', 'dp'))
- out_grad: float32 [2304, 2304], P(('seq', 'dp'))
- gate_grad: float32 [2304, 5760], P(('seq', 'dp'))
- up_grad: float32 [2304, 5760], P(('seq', 'dp'))
- down_grad: float32 [5760, 2304], P(('seq', 'dp'))
- attn_gain_grad: float32 [2304], P(('seq', 'dp'))
- ffn_gain_grad: float32 [2304], P(('seq', 'dp'))
Inputs may be any that keep to these rules, and one draw needn't show every extreme that they name: `lengths`: every sequence's valid tokens come first; one sequence has 128 valid tokens and one has 32.
All inputs are finite; a program needn't handle non-finite values.
Results may differ from a plain program's by a relative error of at most 0.015.
Values may be sent and summed in bfloat16 or wider, within the bound.
A program may use at most 576 MiB of HBM per device.

v0:
```python
import math

import jax
import jax.numpy as jnp
from jax import lax
from jax.sharding import Mesh
from jax.sharding import PartitionSpec as P


HEADS = 36
HEAD_DIM = 64

NORM_EPS = 1e-05
BRANCH_SCALE = 1.4 / math.sqrt(40.0)
SCORE_SCALE = 0.125
MASK_FILL = -1e30

BF16 = jnp.bfloat16
F32 = jnp.float32


PLANE = ("y", "l")
LINE = ("x", "c")
FLIPS = (0, 2, 1, 3)


def dot(left, right, contract=((1,), (0,))):
    return lax.dot_general(left, right, (contract, ((), ())), preferred_element_type=F32)


NT = ((1,), (1,))
TN = ((0,), (0,))


def flip_send(block, flip):
    return lax.ppermute(block, PLANE, [(p, p ^ flip) for p in range(4)])


def plane_gather(block):
    return jnp.concatenate([block] + [flip_send(block, f) for f in FLIPS[1:]], axis=0)


def plane_scatter(partial):
    rows = partial.shape[0] // 4
    total = partial[:rows].astype(F32)
    for k, f in enumerate(FLIPS[1:], 1):
        total = total + flip_send(partial[k * rows : (k + 1) * rows].astype(BF16), f).astype(F32)
    return total


def reorder(blocks):
    pairs = blocks.reshape((2, 2) + blocks.shape[1:])
    pairs = jnp.where(lax.axis_index("y") == 1, pairs[::-1], pairs)
    pairs = jnp.where(lax.axis_index("l") == 1, pairs[:, ::-1], pairs)
    return pairs.reshape(blocks.shape)


def plane_exchange(blocks):
    mine = reorder(blocks)
    got = [mine[0]] + [flip_send(mine[f], f) for f in (1, 2, 3)]
    return reorder(jnp.stack(got))


def after(value, *others):
    return lax.optimization_barrier((value,) + others)[0]


def line_gather(block):
    return lax.all_gather(block, LINE, axis=0, tiled=True)


def in_order(own, other):
    return jnp.where(
        lax.axis_index("h") == 0,
        jnp.concatenate([own, other], axis=0),
        jnp.concatenate([other, own], axis=0),
    )


def half_gather(block):
    if lax.axis_size("h") == 2:
        return in_order(block, lax.ppermute(block, "h", [(0, 1), (1, 0)]))
    return lax.all_gather(block, "h", axis=0, tiled=True)


def line_scatter(partial):
    return lax.psum_scatter(partial, LINE, scatter_dimension=0, tiled=True)


def half_scatter(partial):
    if lax.axis_size("h") == 2:
        rows = partial.shape[0] // 2
        h = lax.axis_index("h")
        other = lax.dynamic_slice_in_dim(partial, (1 - h) * rows, rows)
        own = lax.dynamic_slice_in_dim(partial, h * rows, rows)
        return own.astype(F32) + lax.ppermute(other, "h", [(0, 1), (1, 0)]).astype(F32)
    return lax.psum_scatter(partial, "h", scatter_dimension=0, tiled=True).astype(F32)


def column_block(blocks):
    four, rows, n = blocks.shape
    return half_gather(plane_exchange(blocks).reshape(four * rows, n))


def column_grad(scattered, rows):
    mine = half_scatter(scattered).astype(BF16)
    return plane_exchange(mine.reshape(4, rows, mine.shape[1]))


def to_line(tokens, rows):
    count = tokens.shape[0]
    blocks = tokens.reshape(count, 2, -1, 2, 2, 2, rows)
    return blocks.transpose(0, 4, 5, 2, 1, 3, 6).reshape(tokens.shape)


def from_line(tokens, rows):
    count = tokens.shape[0]
    blocks = tokens.reshape(count, 2, 2, -1, 2, 2, rows)
    return blocks.transpose(0, 4, 3, 5, 1, 2, 6).reshape(tokens.shape)


def head_order(flip):
    h = lax.axis_size("h")
    pairs = []
    for hi in range(h):
        for li in range(2):
            for xc in range(4):
                source = li * 4 * h + xc * h + hi
                pairs.append((source, ((hi ^ flip) * 2 + li) * 4 + xc))
    return pairs


def angle_tables(positions):
    inverse = 10000.0 ** (-jnp.arange(32, dtype=F32) / 32.0)
    phase = positions[:, None] * inverse[None, :]
    phase = jnp.concatenate([phase, phase], axis=-1)
    return jnp.cos(phase), jnp.sin(phase)


def rotate(tensor, cosine, sine):
    half = HEAD_DIM // 2
    turned = jnp.concatenate([-tensor[..., half:], tensor[..., :half]], axis=-1)
    return tensor * cosine[:, None, :] + turned * sine[:, None, :]


def rotate_back(grad, cosine, sine):
    half = HEAD_DIM // 2
    scaled = grad * sine[:, None, :]
    turned = jnp.concatenate([scaled[..., half:], -scaled[..., :half]], axis=-1)
    return grad * cosine[:, None, :] + turned


def norm_factor(values):
    return lax.rsqrt(jnp.mean(values * values, axis=-1, keepdims=True) + NORM_EPS)


def norm_back(values, factor, grad):
    mean = jnp.mean(values * grad, axis=-1, keepdims=True)
    return factor * (grad - values * (factor * factor) * mean)


def einsum(spec, left, right):
    return jnp.einsum(spec, left, right, preferred_element_type=F32)


def body(
    inputs,
    lengths,
    query_weight,
    key_weight,
    value_weight,
    out_weight,
    gate_weight,
    up_weight,
    down_weight,
    attn_gain,
    ffn_gain,
    cotangent,
):
    count, tokens, width = inputs.shape
    rows = query_weight.shape[0]
    units = down_weight.shape[0]
    halves = lax.axis_size("h")
    heads = HEADS // 4
    part = heads * HEAD_DIM
    padded = -(-units // 8) * 8
    hidden = padded * 4 * halves
    y = lax.axis_index("y")

    spare = -3 * part % 128
    spare = spare if spare >= 2 else spare + 128
    extra = jnp.concatenate(
        [attn_gain[:, None], ffn_gain[:, None], jnp.zeros((rows, spare - 2), BF16)], axis=1
    )
    extra = jnp.broadcast_to(extra[None], (4, rows, spare))

    def split_heads(weight):
        return weight.reshape(rows, 4, part).transpose(1, 0, 2)

    def split_units(weight):
        blocks = weight.reshape(rows, 2, halves, 2, 2, 2, units)
        blocks = jnp.pad(blocks, ((0, 0),) * 6 + ((0, padded - units),))
        return blocks.transpose(1, 3, 0, 4, 5, 2, 6).reshape(4, rows, hidden)

    def join_units(blocks):
        blocks = blocks.reshape(2, 2, rows, 2, 2, halves, padded)[..., :units]
        return blocks.transpose(2, 0, 5, 1, 3, 4, 6).reshape(rows, 16 * halves * units)

    HLXC = ("h", "l", "x", "c")
    if halves == 2:
        out_block = in_order(
            lax.ppermute(out_weight, HLXC, head_order(0)),
            lax.ppermute(out_weight, HLXC, head_order(1)),
        )
    else:
        out_block = half_gather(lax.ppermute(out_weight, HLXC, head_order(0)))
    qkv_columns = jnp.concatenate(
        [split_heads(w) for w in (query_weight, key_weight, value_weight)] + [extra], axis=2
    )
    qkv_block = column_block(qkv_columns)
    late_gate, late_up, late_down, qkv_columns = lax.optimization_barrier(
        (gate_weight, up_weight, down_weight, qkv_columns)
    )
    gu_block = column_block(
        jnp.concatenate([split_units(late_gate), split_units(late_up)], axis=2)
    )
    down_block = half_gather(jnp.pad(late_down, ((0, padded - units), (0, 0))))
    w_out = line_gather(out_block)
    w_qkv = line_gather(qkv_block)
    w_gu = line_gather(gu_block)
    w_down = line_gather(down_block)

    own = jnp.arange(tokens, dtype=jnp.int32)
    place = jnp.concatenate([y * tokens + own, (1 - y) * tokens + own])
    local_place = place[:tokens]
    cosine, sine = angle_tables(place.astype(F32))
    lengths_two = jnp.stack(
        [lengths, lax.ppermute(lengths, "l", [(0, 1), (1, 0)])], axis=1
    )

    x_float = [inputs[s].astype(F32) for s in range(count)]
    gathered = [plane_gather(to_line(inputs[s], rows)) for s in range(count)]
    grad_y = []
    branch2 = []
    for s in range(count):
        live = (local_place < lengths[s]).astype(F32)
        grad_y.append(cotangent[s].astype(F32) * live[:, None])
        branch2.append(plane_gather((BRANCH_SCALE * grad_y[s]).astype(BF16)))

    pick = (
        lax.broadcasted_iota(jnp.int32, (8, spare), 0)
        == lax.broadcasted_iota(jnp.int32, (8, spare), 1)
    ).astype(BF16)
    gains = dot(pick, w_qkv[:, 3 * part :], NT)
    gain_one_line = gains[0:1]
    gain_one = from_line(gain_one_line, rows)
    gain_two = from_line(gains[1:2], rows)

    kept = []
    mids = []
    normed = []
    for s in range(count):
        whole = gathered[s].astype(F32)
        normed.append((whole * norm_factor(whole) * gain_one_line).astype(BF16))
        visible = (place[None, :] <= place[:, None])[None] & (
            place[None, None, :] < lengths_two[s][:, None, None]
        )
        visible = visible[:, None, :, :]
        lin = dot(normed[s], w_qkv)[:, : 3 * part].reshape(2, 2 * tokens, 3, heads, HEAD_DIM)
        queries = rotate(lin[:, :, 0], cosine, sine).astype(BF16)
        keys = rotate(lin[:, :, 1], cosine, sine).astype(BF16)
        values = lin[:, :, 2].astype(BF16)
        scores = einsum("bqhe,bkhe->bhqk", queries, keys) * SCORE_SCALE
        scores = jnp.where(visible, scores, MASK_FILL)
        expo = jnp.exp(scores - jnp.max(scores, axis=-1, keepdims=True))
        probs = expo / jnp.sum(expo, axis=-1, keepdims=True)
        attended = einsum("bhqk,bkhe->bqhe", probs.astype(BF16), values)
        attended = attended.astype(BF16).reshape(4 * tokens, part)
        mid = x_float[s] + BRANCH_SCALE * plane_scatter(dot(attended, w_out))
        kept.append((queries, keys, values, probs, attended))
        mids.append(mid)

    factor_two = [norm_factor(v) for v in mids]
    normed_ffn = [
        plane_gather(to_line((v * f * gain_two).astype(BF16), rows))
        for v, f in zip(mids, factor_two)
    ]
    mixes = []
    acts = []
    for s in range(count):
        both = dot(normed_ffn[s], w_gu)
        gate_pre, up_pre = both[:, :hidden], both[:, hidden:]
        sigmoid = 1.0 / (1.0 + jnp.exp(-gate_pre))
        mixes.append((gate_pre * sigmoid * up_pre).astype(BF16))
        acts.append((gate_pre, up_pre, sigmoid))
    all_mixed = jnp.concatenate(mixes, axis=0)
    all_branch2 = jnp.concatenate(branch2, axis=0)
    down_terms = dot(all_mixed, all_branch2, TN).astype(BF16)
    down_part = line_scatter(down_terms)

    grad_boths = []
    for s in range(count):
        gate_pre, up_pre, sigmoid = acts[s]
        grad_mixed = dot(after(branch2[s], down_terms), w_down, NT)
        grad_gate = grad_mixed * up_pre * (sigmoid + gate_pre * sigmoid * (1.0 - sigmoid))
        grad_up = grad_mixed * gate_pre * sigmoid
        grad_boths.append(jnp.concatenate([grad_gate.astype(BF16), grad_up.astype(BF16)], axis=1))
    norm_terms = [dot(g, w_gu, NT).astype(BF16) for g in grad_boths]
    all_ffn = after(jnp.concatenate(normed_ffn, axis=0), *norm_terms)
    gu_terms = dot(all_ffn, jnp.concatenate(grad_boths, axis=0), TN).astype(BF16)
    gu_part = line_scatter(gu_terms)

    grad_mids = []
    branch1 = []
    for s in range(count):
        grad_norm = from_line(plane_scatter(norm_terms[s]), rows) * gain_two
        grad_mid = grad_y[s] + norm_back(mids[s], factor_two[s], grad_norm)
        grad_mids.append(grad_mid)
        branch1.append(plane_gather((BRANCH_SCALE * grad_mid).astype(BF16)))

    outputs = [
        (mids[s] + BRANCH_SCALE * plane_scatter(dot(after(mixes[s], gu_terms), w_down))).astype(BF16)
        for s in range(count)
    ]

    grad_qkv = []
    input_grads = []
    for s in range(count):
        queries, keys, values, probs, attended = kept[s]
        grad_att = dot(branch1[s], w_out, NT).astype(BF16).reshape(2, 2 * tokens, heads, HEAD_DIM)
        grad_probs = einsum("bqhe,bkhe->bhqk", grad_att, values)
        delta = jnp.sum(probs * grad_probs, axis=-1, keepdims=True)
        grad_scores = (probs * (grad_probs - delta)).astype(BF16)
        grad_q = einsum("bhqk,bkhe->bqhe", grad_scores, keys) * SCORE_SCALE
        grad_k = einsum("bhqk,bqhe->bkhe", grad_scores, queries) * SCORE_SCALE
        grad_v = einsum("bhqk,bqhe->bkhe", probs.astype(BF16), grad_att)
        grads = jnp.stack(
            [
                rotate_back(grad_q, cosine, sine).astype(BF16),
                rotate_back(grad_k, cosine, sine).astype(BF16),
                grad_v.astype(BF16),
            ],
            axis=2,
        ).reshape(4 * tokens, 3 * part)
        grad_qkv.append(jnp.pad(grads, ((0, 0), (0, spare))))
    qkv_terms = dot(
        jnp.concatenate(normed, axis=0), jnp.concatenate(grad_qkv, axis=0), TN
    ).astype(BF16)
    qkv_part = line_scatter(qkv_terms)
    all_attended = after(jnp.concatenate([k[4] for k in kept], axis=0), qkv_terms)
    out_terms = dot(all_attended, jnp.concatenate(branch1, axis=0), TN).astype(BF16)
    out_part = line_scatter(out_terms)
    out_grad = lax.ppermute(
        half_scatter(out_part).astype(BF16), HLXC, [(b, a) for a, b in head_order(0)]
    ).astype(F32)
    gu_raw = column_grad(gu_part, rows)
    qkv_raw = column_grad(qkv_part, rows)
    factor_one = [norm_factor(v) for v in x_float]
    for s in range(count):
        grad_norm = from_line(plane_scatter(dot(grad_qkv[s], w_qkv, NT)), rows) * gain_one
        input_grads.append(
            (grad_mids[s] + norm_back(x_float[s], factor_one[s], grad_norm)).astype(BF16)
        )

    gate_grad = join_units(gu_raw[:, :, :hidden]).astype(F32)
    up_grad = join_units(gu_raw[:, :, hidden:]).astype(F32)
    ffn_gain_grad = jnp.sum(
        gate_grad * gate_weight.astype(F32) + up_grad * up_weight.astype(F32), axis=1
    ) / ffn_gain.astype(F32)
    qkv_grads = [
        qkv_raw[:, :, i * part : (i + 1) * part].transpose(1, 0, 2).reshape(rows, width).astype(F32)
        for i in range(3)
    ]
    attn_gain_grad = jnp.sum(
        qkv_grads[0] * query_weight.astype(F32)
        + qkv_grads[1] * key_weight.astype(F32)
        + qkv_grads[2] * value_weight.astype(F32),
        axis=1,
    ) / attn_gain.astype(F32)
    return (
        jnp.stack(outputs, axis=0),
        jnp.stack(input_grads, axis=0),
        *qkv_grads,
        out_grad,
        gate_grad,
        up_grad,
        half_scatter(down_part)[:units],
        attn_gain_grad,
        ffn_gain_grad,
    )


def solution(mesh):
    seq, dp = mesh.devices.shape
    fine = Mesh(mesh.devices.reshape(seq, dp // 8, 2, 2, 2), ("y", "h", "l", "x", "c"))
    owners = ("y", "h", "l", "x", "c")
    acts = P(owners[1:], "y", None)
    weight = P(owners, None)
    gain = P(owners)
    return jax.shard_map(
        body,
        mesh=fine,
        in_specs=(acts, P(owners[1:])) + (weight,) * 7 + (gain, gain, acts),
        out_specs=(acts, acts) + (weight,) * 7 + (gain, gain),
        check_vma=False,
    )
```

profile of v0, /device:TPU:0, one launch (start us, length us, event | category | flops | bytes accessed | tf_op | source)
XLA Modules:
  0.0 1015.1 jit_solution(7837751459945635750)
XLA Ops:
  34.9 43.8 %collective-permute-done.6 = bf16[288,1792]{1,0:T(8,128)(2,1)S(1)} collective-permute-done((bf16[288,1792]{1,0:T(8,128)(2,1)S(1)}, bf16[288,1792]{1,0:T(8,128)(2,1)S(1)}, u32[]{:S(2)}, u32[]{:S(2)}) %collective-permute-start.6) | collective-permute-done | bytes 1032224 | tf_op jit(solution)/shard_map/ppermute | solution.py:82
  107.8 7.0 collective-permute-done.16
  114.9 8.8 collective-permute-done.17
  127.2 72.4 %collective-permute-done.19 = bf16[288,2944]{1,0:T(8,128)(2,1)S(1)} collective-permute-done((bf16[288,2944]{1,0:T(8,128)(2,1)S(1)}, bf16[288,2944]{1,0:T(8,128)(2,1)S(1)}, u32[]{:S(2)}, u32[]{:S(2)}) %collective-permute-start.19) | collective-permute-done | bytes 1695776 | tf_op jit(solution)/shard_map/ppermute | solution.py:82
  246.6 8.0 collective-permute-done.1
  261.9 12.9 %collective-permute-done.33 = bf16[64,2304]{1,0:T(8,128)(2,1)S(1)} collective-permute-done((bf16[64,2304]{1,0:T(8,128)(2,1)S(1)}, bf16[64,2304]{1,0:T(8,128)(2,1)S(1)}, u32[]{:S(2)}, u32[]{:S(2)}) %collective-permute-start.33) | collective-permute-done | bytes 294944 | tf_op jit(solution)/shard_map/ppermute | solution.py:36
  289.6 6.7 fusion.2
  300.1 8.9 fusion.4
  392.8 7.9 fusion.38
  429.6 8.3 convolution_convert_fusion.4
  437.9 8.3 convolution_convert_fusion.5
  446.2 11.9 %convolution_convert_fusion = bf16[2304,2944]{1,0:T(8,128)(2,1)} fusion(bf16[512,2304]{1,0:T(8,128)(2,1)} %constant_dynamic-update-slice_fusion, bf16[256,2944]{1,0:T(8,128)(2,1)S(1)} %pad_maximum_fusion.4, bf16[256,2944]{1,0:T(8,128)(2,1)S(1)} %pad_maximum_fusion.3), kind=kOutput, calls=%fused_computation.2 | convolution fusion | flops 6958579712 | bytes 18939904 | tf_op jit(solution)/shard_map/dot_general | solution.py:28
  459.8 6.5 fusion.198
  477.7 7.0 collective-permute-done.51
  496.4 8.1 collective-permute-done.42
  545.9 6.7 collective-permute-done.47
  580.8 6.7 convolution_convert_fusion.1
  610.4 7.2 fusion.199
  644.4 60.9 %reduce-scatter.5.cloned.1.call-done = bf16[576,1792]{1,0:T(8,128)(2,1)} async-done(((bf16[2304,1792]{1,0:T(8,128)(2,1)}), bf16[576,1792]{1,0:T(8,128)(2,1)}) %reduce-scatter.5.cloned.1.call-update) | async-done | bytes 2064400 | tf_op jit(solution)/shard_map/reduce_scatter | solution.py:87
  713.5 56.6 %reduce-scatter.11.cloned.1.call-done = bf16[368,2304]{1,0:T(8,128)(2,1)} async-done(((bf16[1472,2304]{1,0:T(8,128)(2,1)}), bf16[368,2304]{1,0:T(8,128)(2,1)}) %reduce-scatter.11.cloned.1.call-update) | async-done | bytes 1695760 | tf_op jit(solution)/shard_map/reduce_scatter | solution.py:87
  784.2 100.9 %reduce-scatter.9.cloned.1.call-done = bf16[576,2944]{1,0:T(8,128)(2,1)} async-done(((bf16[2304,2944]{1,0:T(8,128)(2,1)}), bf16[576,2944]{1,0:T(8,128)(2,1)}) %reduce-scatter.9.cloned.1.call-update) | async-done | bytes 3391504 | tf_op jit(solution)/shard_map/reduce_scatter | solution.py:87
  905.3 58.8 %collective-permute-done.66 = bf16[288,2944]{1,0:T(8,128)(2,1)} collective-permute-done((bf16[288,2944]{1,0:T(8,128)(2,1)}, bf16[288,2944]{1,0:T(8,128)(2,1)}, u32[]{:S(2)}, u32[]{:S(2)}) %collective-permute-start.66) | collective-permute-done | bytes 1695776 | tf_op jit(solution)/shard_map/ppermute | solution.py:96
  971.2 8.2 collective-permute-done.67
  979.4 8.3 collective-permute-done.68
  (592 shorter events, 458.2 us)
Async XLA Ops:
  7.2 276.5 %all-gather.5.cloned.1.call-start = ((), (), s32[]{:S(2)}) async-start(), calls=%async_computation.4 | async-start | bytes 10321920 | tf_op jit(solution)/shard_map/all_gather | solution.py:69
  32.3 46.5 %collective-permute-start.6 = (bf16[288,1792]{1,0:T(8,128)(2,1)S(1)}, bf16[288,1792]{1,0:T(8,128)(2,1)S(1)}, u32[]{:S(2)}, u32[]{:S(2)}) collective-permute-start(bf16[288,1792]{1,0:T(8,128)(2,1)S(1)} %bitcast.291), channel_id=1, source_target_pairs={{0,8},{8,0},{1,9},{9,1},{2,10},{10,2},{3,11},{11,3},{4,12},{12,4},... | collective-permute-start | bytes 3096584 | tf_op jit(solution)/shard_map/ppermute | solution.py:82
  80.9 238.0 %all-gather.7.cloned.1.call-start = ((), (), s32[]{:S(2)}) async-start(), calls=%async_computation.5 | async-start | bytes 3317760 | tf_op jit(solution)/shard_map/all_gather | solution.py:69
  107.8 285.1 %all-gather.9.cloned.1.call-start = ((), (), s32[]{:S(2)}) async-start(), calls=%async_computation.6 | async-start | bytes 16957440 | tf_op jit(solution)/shard_map/all_gather | solution.py:69
  124.5 75.1 %collective-permute-start.19 = (bf16[288,2944]{1,0:T(8,128)(2,1)S(1)}, bf16[288,2944]{1,0:T(8,128)(2,1)S(1)}, u32[]{:S(2)}, u32[]{:S(2)}) collective-permute-start(bf16[288,2944]{1,0:T(8,128)(2,1)S(1)} %bitcast.282), channel_id=1, source_target_pairs={{0,8},{8,0},{1,9},{9,1},{2,10},{10,2},{3,11},{11,3},{4,12},{12,4},... | collective-permute-start | bytes 5087240 | tf_op jit(solution)/shard_map/ppermute | solution.py:82
  202.0 216.4 %all-gather.11.cloned.1.call-start = ((), (), s32[]{:S(2)}) async-start(), calls=%async_computation.7 | async-start | bytes 8478720 | tf_op jit(solution)/shard_map/all_gather | solution.py:69
  205.3 33.9 %collective-permute-start.20 = (bf16[64,2304]{1,0:T(8,128)(2,1)S(1)}, bf16[64,2304]{1,0:T(8,128)(2,1)S(1)}, u32[]{:S(2)}, u32[]{:S(2)}) collective-permute-start(bf16[64,2304]{1,0:T(8,128)(2,1)S(1)} %reshape.455), channel_id=1, source_target_pairs={{0,16},{4,20},{16,0},{20,4},{1,17},{5,21},{17,1},{21,5},{2,18},{6,... | collective-permute-start | bytes 884744 | tf_op jit(solution)/shard_map/ppermute | solution.py:36
  206.2 34.4 %collective-permute-start.21 = (bf16[64,2304]{1,0:T(8,128)(2,1)S(1)}, bf16[64,2304]{1,0:T(8,128)(2,1)S(1)}, u32[]{:S(2)}, u32[]{:S(2)}) collective-permute-start(bf16[64,2304]{1,0:T(8,128)(2,1)S(1)} %reshape.455), channel_id=1, source_target_pairs={{0,4},{4,0},{16,20},{20,16},{1,5},{5,1},{17,21},{21,17},{2,6},{6,2... | collective-permute-start | bytes 884744 | tf_op jit(solution)/shard_map/ppermute | solution.py:36
  206.7 36.5 %collective-permute-start.22 = (bf16[64,2304]{1,0:T(8,128)(2,1)S(1)}, bf16[64,2304]{1,0:T(8,128)(2,1)}, u32[]{:S(2)}, u32[]{:S(2)}) collective-permute-start(bf16[64,2304]{1,0:T(8,128)(2,1)S(1)} %reshape.455), channel_id=1, source_target_pairs={{0,20},{4,16},{16,4},{20,0},{1,21},{5,17},{17,5},{21,1},{2,22},{6,... | collective-permute-start | bytes 884744 | tf_op jit(solution)/shard_map/ppermute | solution.py:36
  240.6 41.0 %collective-permute-start.35 = (bf16[184,2304]{1,0:T(8,128)(2,1)S(1)}, bf16[184,2304]{1,0:T(8,128)(2,1)S(1)}, u32[]{:S(2)}, u32[]{:S(2)}) collective-permute-start(bf16[184,2304]{1,0:T(8,128)(2,1)S(1)} %pad.20), channel_id=1, source_target_pairs={{0,8},{8,0},{1,9},{9,1},{2,10},{10,2},{3,11},{11,3},{4,12},{12,4},... | collective-permute-start | bytes 2543624 | tf_op jit(solution)/shard_map/ppermute | solution.py:82
  245.1 29.7 %collective-permute-start.33 = (bf16[64,2304]{1,0:T(8,128)(2,1)S(1)}, bf16[64,2304]{1,0:T(8,128)(2,1)S(1)}, u32[]{:S(2)}, u32[]{:S(2)}) collective-permute-start(bf16[64,2304]{1,0:T(8,128)(2,1)S(1)} %get-tuple-element.46), channel_id=1, source_target_pairs={{0,4},{4,0},{16,20},{20,16},{1,5},{5,1},{17,21},{21,17},{2,6},{6,2... | collective-permute-start | bytes 884744 | tf_op jit(solution)/shard_map/ppermute | solution.py:36
  283.2 353.5 %reduce-scatter.7.cloned.1.call-start = ((), (), s32[]{:S(2)}) async-start(), calls=%async_computation.9 | async-start | bytes 3317760 | tf_op jit(solution)/shard_map/reduce_scatter | solution.py:87
  468.1 61.8 %collective-permute-start.37 = (bf16[64,2304]{1,0:T(8,128)(2,1)}, bf16[64,2304]{1,0:T(8,128)(2,1)}, u32[]{:S(2)}, u32[]{:S(2)}) collective-permute-start(bf16[64,2304]{1,0:T(8,128)(2,1)} %get-tuple-element.87), channel_id=1, source_target_pairs={{0,4},{4,0},{16,20},{20,16},{1,5},{5,1},{17,21},{21,17},{2,6},{6,2... | collective-permute-start | bytes 884744 | tf_op jit(solution)/shard_map/ppermute | solution.py:36
  495.5 34.5 %collective-permute-start.38 = (bf16[64,2304]{1,0:T(8,128)(2,1)}, bf16[64,2304]{1,0:T(8,128)(2,1)}, u32[]{:S(2)}, u32[]{:S(2)}) collective-permute-start(bf16[64,2304]{1,0:T(8,128)(2,1)} %get-tuple-element.86), channel_id=1, source_target_pairs={{0,20},{4,16},{16,4},{20,0},{1,21},{5,17},{17,5},{21,1},{2,22},{6,... | collective-permute-start | bytes 884744 | tf_op jit(solution)/shard_map/ppermute | solution.py:36
  597.4 107.9 %reduce-scatter.5.cloned.1.call-start = ((), (), s32[]{:S(2)}) async-start(), calls=%async_computation.8 | async-start | bytes 10321920 | tf_op jit(solution)/shard_map/reduce_scatter | solution.py:87
  598.0 172.1 %reduce-scatter.11.cloned.1.call-start = ((), (), s32[]{:S(2)}) async-start(), calls=%async_computation.11 | async-start | bytes 8478720 | tf_op jit(solution)/shard_map/reduce_scatter | solution.py:87
  598.7 286.4 %reduce-scatter.9.cloned.1.call-start = ((), (), s32[]{:S(2)}) async-start(), calls=%async_computation.10 | async-start | bytes 16957440 | tf_op jit(solution)/shard_map/reduce_scatter | solution.py:87
  638.5 71.4 %collective-permute-start.64 = (bf16[72,2304]{1,0:T(8,128)(2,1)}, bf16[72,2304]{1,0:T(8,128)(2,1)}, u32[]{:S(2)}, u32[]{:S(2)}) collective-permute-start(bf16[72,2304]{1,0:T(8,128)(2,1)} %constant_dynamic-slice_fusion.2), channel_id=1, source_target_pairs={{0,8},{8,0},{1,9},{9,1},{2,10},{10,2},{3,11},{11,3},{4,12},{12,4},... | collective-permute-start | bytes 995336 | tf_op jit(solution)/shard_map/ppermute | solution.py:96
  707.5 69.7 %collective-permute-start.60 = (bf16[288,1792]{1,0:T(8,128)(2,1)}, bf16[288,1792]{1,0:T(8,128)(2,1)}, u32[]{:S(2)}, u32[]{:S(2)}) collective-permute-start(bf16[288,1792]{1,0:T(8,128)(2,1)} %constant_dynamic-slice_fusion.3), channel_id=1, source_target_pairs={{0,8},{8,0},{1,9},{9,1},{2,10},{10,2},{3,11},{11,3},{4,12},{12,4},... | collective-permute-start | bytes 3096584 | tf_op jit(solution)/shard_map/ppermute | solution.py:96
  771.3 119.0 %collective-permute-start.70 = (bf16[184,2304]{1,0:T(8,128)(2,1)S(1)}, bf16[184,2304]{1,0:T(8,128)(2,1)}, u32[]{:S(2)}, u32[]{:S(2)}) collective-permute-start(bf16[184,2304]{1,0:T(8,128)(2,1)S(1)} %constant_dynamic-slice_fusion), channel_id=1, source_target_pairs={{0,8},{8,0},{1,9},{9,1},{2,10},{10,2},{3,11},{11,3},{4,12},{12,4},... | collective-permute-start | bytes 2543624 | tf_op jit(solution)/shard_map/ppermute | solution.py:96
  779.9 113.0 %collective-permute-start.61 = (bf16[72,1792]{1,0:T(8,128)(2,1)}, bf16[72,1792]{1,0:T(8,128)(2,1)S(1)}, u32[]{:S(2)}, u32[]{:S(2)}) collective-permute-start(bf16[72,1792]{1,0:T(8,128)(2,1)} %get-tuple-element.103), channel_id=1, source_target_pairs={{0,4},{4,0},{16,20},{20,16},{1,5},{5,1},{17,21},{21,17},{2,6},{6,2... | collective-permute-start | bytes 774152 | tf_op jit(solution)/shard_map/ppermute | solution.py:36
  782.7 110.2 %collective-permute-start.62 = (bf16[72,1792]{1,0:T(8,128)(2,1)}, bf16[72,1792]{1,0:T(8,128)(2,1)}, u32[]{:S(2)}, u32[]{:S(2)}) collective-permute-start(bf16[72,1792]{1,0:T(8,128)(2,1)} %get-tuple-element.102), channel_id=1, source_target_pairs={{0,16},{4,20},{16,0},{20,4},{1,17},{5,21},{17,1},{21,5},{2,18},{6,... | collective-permute-start | bytes 774152 | tf_op jit(solution)/shard_map/ppermute | solution.py:36
  784.2 108.7 %collective-permute-start.63 = (bf16[72,1792]{1,0:T(8,128)(2,1)S(1)}, bf16[72,1792]{1,0:T(8,128)(2,1)}, u32[]{:S(2)}, u32[]{:S(2)}) collective-permute-start(bf16[72,1792]{1,0:T(8,128)(2,1)S(1)} %get-tuple-element.101), channel_id=1, source_target_pairs={{0,20},{4,16},{16,4},{20,0},{1,21},{5,17},{17,5},{21,1},{2,22},{6,... | collective-permute-start | bytes 774152 | tf_op jit(solution)/shard_map/ppermute | solution.py:36
  887.9 76.2 %collective-permute-start.66 = (bf16[288,2944]{1,0:T(8,128)(2,1)}, bf16[288,2944]{1,0:T(8,128)(2,1)}, u32[]{:S(2)}, u32[]{:S(2)}) collective-permute-start(bf16[288,2944]{1,0:T(8,128)(2,1)} %constant_dynamic-slice_fusion.1), channel_id=1, source_target_pairs={{0,8},{8,0},{1,9},{9,1},{2,10},{10,2},{3,11},{11,3},{4,12},{12,4},... | collective-permute-start | bytes 5087240 | tf_op jit(solution)/shard_map/ppermute | solution.py:96
  (153 other events, 1545.9 us)
Sparse Core Ops, SparseCore 0:
  81.1 57.7 all-gather.4
  141.0 30.4 all-gather.6
  202.1 87.0 all-gather.8
  291.2 49.1 all-gather.10
  597.5 34.6 reduce-scatter.6
  634.6 70.6 reduce-scatter.4
  707.9 62.1 reduce-scatter.10
  772.7 112.3 reduce-scatter.8
where the time goes:
time: 1020 us
  waiting for transfers between devices  533 us (52%)
  local copies, waits for them, and re-layouts  162 us (16%)
  matrix products  134 us (13%)
  starting transfers between devices  101 us (10%)
  other arithmetic  68.4 us (7%)
  between operations  16.2 us (2%)
    reduce_scatter x4, waiting for transfers between devices, line_scatter(): return lax.psum_scatter(partial, LINE, scatter_dimension=0, tiled=True)  218 us
    ppermute x60, waiting for transfers between devices, flip_send(): return lax.ppermute(block, PLANE, [(p, p ^ flip) for p in range(4)])  135 us
    dot_general x21, matrix products, dot(): lax.dot_general(left, right, (contract, ((), ())), preferred_element_type...  120 us
    ppermute x3, waiting for transfers between devices, half_gather(): return in_order(block, lax.ppermute(block, 'h', [(0, 1), (1, 0)]))  116 us
    ppermute x60, starting transfers between devices, flip_send(): return lax.ppermute(block, PLANE, [(p, p ^ flip) for p in range(4)])  71.9 us
    ppermute x4, waiting for transfers between devices, half_scatter(): lax.ppermute(other, 'h', [(0, 1), (1, 0)]).astype(F32)  58.8 us
    unnamed x220, local copies, waits for them, and re-layouts  38.9 us
  transfers between devices with their start and end apart: 79, of which 33 were waited for; matrix products, arithmetic and copies ran while one was open for 23% of the time, Pallas kernels for 0%

commit v1 on v0

--- a/solution.py
+++ b/solution.py
@@ -79,7 +79,8 @@
 
 def half_gather(block):
     if lax.axis_size("h") == 2:
-        return in_order(block, lax.ppermute(block, "h", [(0, 1), (1, 0)]))
+        other = lax.ppermute(block, "h", [(0, 1), (1, 0)])
+        return in_order(block, other)
     return lax.all_gather(block, "h", axis=0, tiled=True)
 
 
@@ -93,13 +94,15 @@
         h = lax.axis_index("h")
         other = lax.dynamic_slice_in_dim(partial, (1 - h) * rows, rows)
         own = lax.dynamic_slice_in_dim(partial, h * rows, rows)
-        return own.astype(F32) + lax.ppermute(other, "h", [(0, 1), (1, 0)]).astype(F32)
+        other = lax.ppermute(other, "h", [(0, 1), (1, 0)])
+        return own.astype(F32) + other.astype(F32)
     return lax.psum_scatter(partial, "h", scatter_dimension=0, tiled=True).astype(F32)
 
 
 def column_block(blocks):
     four, rows, n = blocks.shape
-    return half_gather(plane_exchange(blocks).reshape(four * rows, n))
+    mine = plane_exchange(blocks)
+    return half_gather(mine.reshape(four * rows, n))
 
 
 def column_grad(scattered, rows):
@@ -208,38 +211,33 @@
 
     HLXC = ("h", "l", "x", "c")
     if halves == 2:
-        out_block = in_order(
-            lax.ppermute(out_weight, HLXC, head_order(0)),
-            lax.ppermute(out_weight, HLXC, head_order(1)),
-        )
+        pair = [lax.ppermute(out_weight, HLXC, head_order(flip)) for flip in (0, 1)]
+        out_block = in_order(*pair)
     else:
         out_block = half_gather(lax.ppermute(out_weight, HLXC, head_order(0)))
-    qkv_columns = jnp.concatenate(
-        [split_heads(w) for w in (query_weight, key_weight, value_weight)] + [extra], axis=2
-    )
-    qkv_block = column_block(qkv_columns)
-    late_gate, late_up, late_down, qkv_columns = lax.optimization_barrier(
-        (gate_weight, up_weight, down_weight, qkv_columns)
+    other_lengths = lax.ppermute(lengths, "l", [(0, 1), (1, 0)])
+    gathered = [plane_gather(to_line(inputs[s], rows)) for s in range(count)]
+    down_block = half_gather(jnp.pad(down_weight, ((0, padded - units), (0, 0))))
+    qkv_block = column_block(
+        jnp.concatenate(
+            [split_heads(w) for w in (query_weight, key_weight, value_weight)] + [extra], axis=2
+        ),
     )
     gu_block = column_block(
-        jnp.concatenate([split_units(late_gate), split_units(late_up)], axis=2)
-    )
-    down_block = half_gather(jnp.pad(late_down, ((0, padded - units), (0, 0))))
+        jnp.concatenate([split_units(gate_weight), split_units(up_weight)], axis=2)
+    )
     w_out = line_gather(out_block)
     w_qkv = line_gather(qkv_block)
     w_gu = line_gather(gu_block)
     w_down = line_gather(down_block)
 
-    own = jnp.arange(tokens, dtype=jnp.int32)
-    place = jnp.concatenate([y * tokens + own, (1 - y) * tokens + own])
+    step = jnp.arange(tokens, dtype=jnp.int32)
+    place = jnp.concatenate([y * tokens + step, (1 - y) * tokens + step])
     local_place = place[:tokens]
     cosine, sine = angle_tables(place.astype(F32))
-    lengths_two = jnp.stack(
-        [lengths, lax.ppermute(lengths, "l", [(0, 1), (1, 0)])], axis=1
-    )
+    lengths_two = jnp.stack([lengths, other_lengths], axis=1)
 
     x_float = [inputs[s].astype(F32) for s in range(count)]
-    gathered = [plane_gather(to_line(inputs[s], rows)) for s in range(count)]
     grad_y = []
     branch2 = []
     for s in range(count):
@@ -327,7 +325,7 @@
     input_grads = []
     for s in range(count):
         queries, keys, values, probs, attended = kept[s]
-        grad_att = dot(branch1[s], w_out, NT).astype(BF16).reshape(2, 2 * tokens, heads, HEAD_DIM)
+        grad_att = dot(after(branch1[s], down_part), w_out, NT).astype(BF16).reshape(2, 2 * tokens, heads, HEAD_DIM)
         grad_probs = einsum("bqhe,bkhe->bhqk", grad_att, values)
         delta = jnp.sum(probs * grad_probs, axis=-1, keepdims=True)
         grad_scores = (probs * (grad_probs - delta)).astype(BF16)
@@ -350,14 +348,26 @@
     all_attended = after(jnp.concatenate([k[4] for k in kept], axis=0), qkv_terms)
     out_terms = dot(all_attended, jnp.concatenate(branch1, axis=0), TN).astype(BF16)
     out_part = line_scatter(out_terms)
-    out_grad = lax.ppermute(
-        half_scatter(out_part).astype(BF16), HLXC, [(b, a) for a, b in head_order(0)]
-    ).astype(F32)
+    own = out_part.shape[0] // halves
+    if halves == 2:
+        h = lax.axis_index("h")
+        out_grad = sum(
+            lax.ppermute(
+                lax.dynamic_slice_in_dim(out_part, (h ^ flip) * own, own),
+                HLXC,
+                [(b, a) for a, b in head_order(flip)],
+            ).astype(F32)
+            for flip in (0, 1)
+        )
+    else:
+        out_grad = lax.ppermute(half_scatter(out_part), HLXC, [(b, a) for a, b in head_order(0)])
     gu_raw = column_grad(gu_part, rows)
     qkv_raw = column_grad(qkv_part, rows)
     factor_one = [norm_factor(v) for v in x_float]
     for s in range(count):
-        grad_norm = from_line(plane_scatter(dot(grad_qkv[s], w_qkv, NT)), rows) * gain_one
+        in_terms = dot(after(grad_qkv[s], gu_part, out_terms), w_qkv, NT)
+        grad_norm = plane_scatter(in_terms)
+        grad_norm = from_line(grad_norm, rows) * gain_one
         input_grads.append(
             (grad_mids[s] + norm_back(x_float[s], factor_one[s], grad_norm)).astype(BF16)
         )

time: 1020 us -> 954 us (0.935)
  waiting for transfers between devices: 533 us -> 481 us
    reduce_scatter x4, waiting for transfers between devices: 218 us -> 121 us  [line_scatter(): return lax.psum_scatter(partial, LINE, scatter_dimension=0, tiled=True)]
    ppermute x11, waiting for transfers between devices: 178 us -> 203 us  [the longest x3 120 us: half_gather(): other = lax.ppermute(block, 'h', [(0, 1), (1, 0)])]
    ppermute x60, waiting for transfers between devices: 135 us -> 155 us  [flip_send(): return lax.ppermute(block, PLANE, [(p, p ^ flip) for p in range(4)])]
    ppermute x11, starting transfers between devices: 28.2 us -> 15.5 us  [the longest x3 5.5 us: half_scatter(): other = lax.ppermute(other, 'h', [(0, 1), (1, 0)])]
  transfers between devices with their start and end apart: 79 -> 79, of which waited for: 33 -> 38; matrix products, arithmetic and copies ran while one was open for 23% -> 31% of each run, Pallas kernels for 0% -> 0%
where the time goes in v1:
time: 954 us; the launch traced here: 947 us
  waiting for transfers between devices  481 us (50%)
  local copies, waits for them, and re-layouts  153 us (16%)
  matrix products  142 us (15%)
  starting transfers between devices  92.2 us (10%)
  other arithmetic  64 us (7%)
  between operations  16.4 us (2%)
    ppermute x60, waiting for transfers between devices, flip_send(): return lax.ppermute(block, PLANE, [(p, p ^ flip) for p in range(4)])  155 us
    dot_general x21, matrix products, dot(): lax.dot_general(left, right, (contract, ((), ())), preferred_element_type...  127 us
    reduce_scatter x4, waiting for transfers between devices, line_scatter(): return lax.psum_scatter(partial, LINE, scatter_dimension=0, tiled=True)  121 us
    ppermute x3, waiting for transfers between devices, half_gather(): other = lax.ppermute(block, 'h', [(0, 1), (1, 0)])  120 us
    ppermute x60, starting transfers between devices, flip_send(): return lax.ppermute(block, PLANE, [(p, p ^ flip) for p in range(4)])  76.2 us
    ppermute x3, waiting for transfers between devices, half_scatter(): other = lax.ppermute(other, 'h', [(0, 1), (1, 0)])  75.5 us
    unnamed x220, local copies, waits for them, and re-layouts  34 us
    reshape x12, local copies, waits for them, and re-layouts, from_line(): blocks = tokens.reshape(count, 2, 2, -1, 2, 2, rows)  19.4 us
  transfers between devices with their start and end apart: 79, of which 38 were waited for; matrix products, arithmetic and copies ran while one was open for 31% of the time, Pallas kernels for 0%

profile of v1, /device:TPU:0, one launch (start us, length us, event | category | flops | bytes accessed | tf_op | source)
XLA Modules:
  0.0 947.4 jit_solution(16954653124996508212)
XLA Ops:
  34.6 45.0 %collective-permute-done.6 = bf16[288,1792]{1,0:T(8,128)(2,1)S(1)} collective-permute-done((bf16[288,1792]{1,0:T(8,128)(2,1)S(1)}, bf16[288,1792]{1,0:T(8,128)(2,1)S(1)}, u32[]{:S(2)}, u32[]{:S(2)}) %collective-permute-start.6) | collective-permute-done | bytes 1032224 | tf_op jit(solution)/shard_map/ppermute | solution.py:82
  109.1 7.3 collective-permute-done.18
  116.4 9.7 %collective-permute-done.17 = bf16[72,2944]{1,0:T(8,128)(2,1)S(1)} collective-permute-done((bf16[72,2944]{1,0:T(8,128)(2,1)S(1)}, bf16[72,2944]{1,0:T(8,128)(2,1)S(1)}, u32[]{:S(2)}, u32[]{:S(2)}) %collective-permute-start.17) | collective-permute-done | bytes 423968 | tf_op jit(solution)/shard_map/ppermute | solution.py:36
  128.4 75.0 %collective-permute-done.19 = bf16[288,2944]{1,0:T(8,128)(2,1)S(1)} collective-permute-done((bf16[288,2944]{1,0:T(8,128)(2,1)S(1)}, bf16[288,2944]{1,0:T(8,128)(2,1)S(1)}, u32[]{:S(2)}, u32[]{:S(2)}) %collective-permute-start.19) | collective-permute-done | bytes 1695776 | tf_op jit(solution)/shard_map/ppermute | solution.py:82
  228.1 9.9 %collective-permute-done.29 = bf16[64,2304]{1,0:T(8,128)(2,1)S(1)} collective-permute-done((bf16[64,2304]{1,0:T(8,128)(2,1)S(1)}, bf16[64,2304]{1,0:T(8,128)(2,1)S(1)}, u32[]{:S(2)}, u32[]{:S(2)}) %collective-permute-start.29) | collective-permute-done | bytes 294944 | tf_op jit(solution)/shard_map/ppermute | solution.py:36
  238.7 8.2 collective-permute-done.30
  256.1 8.0 collective-permute-done.22
  271.0 14.6 %collective-permute-done.33 = bf16[64,2304]{1,0:T(8,128)(2,1)S(1)} collective-permute-done((bf16[64,2304]{1,0:T(8,128)(2,1)S(1)}, bf16[64,2304]{1,0:T(8,128)(2,1)S(1)}, u32[]{:S(2)}, u32[]{:S(2)}) %collective-permute-start.33) | collective-permute-done | bytes 294944 | tf_op jit(solution)/shard_map/ppermute | solution.py:36
  286.4 6.8 collective-permute-done.34
  301.2 8.0 fusion.4
  312.6 7.8 fusion.2
  404.7 7.9 fusion.38
  436.5 10.5 %convolution_convert_fusion.5 = bf16[256,2304]{1,0:T(8,128)(2,1)} fusion(bf16[256,2944]{1,0:T(8,128)(2,1)S(1)} %pad_maximum_fusion.3, bf16[2304,2944]{1,0:T(8,128)(2,1)} %all-gather.9.cloned.1.call-done), kind=kOutput, calls=%fused_computation.11 | convolution fusion | flops 3473473536 | bytes 16252928 | tf_op jit(solution)/shard_map/dot_general | solution.py:28
  452.7 8.3 convolution_convert_fusion.4
  461.1 11.8 %convolution_convert_fusion = bf16[2304,2944]{1,0:T(8,128)(2,1)} fusion(bf16[512,2304]{1,0:T(8,128)(2,1)} %constant_dynamic-update-slice_fusion, bf16[256,2944]{1,0:T(8,128)(2,1)S(1)} %pad_maximum_fusion.4, bf16[256,2944]{1,0:T(8,128)(2,1)S(1)} %pad_maximum_fusion.3), kind=kOutput, calls=%fused_computation.2 | convolution fusion | flops 6958579712 | bytes 18939904 | tf_op jit(solution)/shard_map/dot_general | solution.py:28
  545.0 8.5 collective-permute-done.45
  563.3 8.1 collective-permute-done.51
  613.1 27.9 %reduce-scatter.11.cloned.1.call-done = bf16[144,2304]{1,0:T(8,128)(2,1)} async-done(((bf16[576,2304]{1,0:T(8,128)(2,1)}), bf16[144,2304]{1,0:T(8,128)(2,1)}) %reduce-scatter.11.cloned.1.call-update) | async-done | bytes 663568 | tf_op jit(solution)/shard_map/reduce_scatter | solution.py:88
  657.3 92.9 %reduce-scatter.7.cloned.1.call-done = bf16[576,2944]{1,0:T(8,128)(2,1)} async-done(((bf16[2304,2944]{1,0:T(8,128)(2,1)}), bf16[576,2944]{1,0:T(8,128)(2,1)}) %reduce-scatter.7.cloned.1.call-update) | async-done | bytes 3391504 | tf_op jit(solution)/shard_map/reduce_scatter | solution.py:88
  759.8 9.5 %fusion.180 = (bf16[256,2304]{1,0:T(8,128)(2,1)S(1)}, f32[256,2304]{1,0:T(8,128)}) fusion(bf16[256,1792]{0,1:T(8,128)(2,1)S(1)} %pad.22, bf16[2304,1792]{1,0:T(8,128)(2,1)} %all-gather.5.cloned.1.call-done), kind=kOutput, calls=%fused_computation.405 | convolution fusion | flops 2114519040 | bytes 12713984 | tf_op jit(solution)/shard_map/dot_general | solution.py:28
  780.9 10.5 %collective-permute-done.59 = bf16[64,2304]{1,0:T(8,128)(2,1)S(1)} collective-permute-done((bf16[64,2304]{1,0:T(8,128)(2,1)S(1)}, bf16[64,2304]{1,0:T(8,128)(2,1)S(1)}, u32[]{:S(2)}, u32[]{:S(2)}) %collective-permute-start.59) | collective-permute-done | bytes 294944 | tf_op jit(solution)/shard_map/ppermute | solution.py:36
  803.0 44.7 %collective-permute-done.66 = bf16[288,2944]{1,0:T(8,128)(2,1)} collective-permute-done((bf16[288,2944]{1,0:T(8,128)(2,1)}, bf16[288,2944]{1,0:T(8,128)(2,1)}, u32[]{:S(2)}, u32[]{:S(2)}) %collective-permute-start.66) | collective-permute-done | bytes 1695776 | tf_op jit(solution)/shard_map/ppermute | solution.py:97
  855.9 8.2 collective-permute-done.69
  894.2 24.4 %collective-permute-done.60 = bf16[288,1792]{1,0:T(8,128)(2,1)} collective-permute-done((bf16[288,1792]{1,0:T(8,128)(2,1)}, bf16[288,1792]{1,0:T(8,128)(2,1)}, u32[]{:S(2)}, u32[]{:S(2)}) %collective-permute-start.60) | collective-permute-done | bytes 1032224 | tf_op jit(solution)/shard_map/ppermute | solution.py:97
  (593 shorter events, 457.5 us)
Async XLA Ops:
  7.2 289.1 %all-gather.5.cloned.1.call-start = ((), (), s32[]{:S(2)}) async-start(), calls=%async_computation.4 | async-start | bytes 10321920 | tf_op jit(solution)/shard_map/all_gather | solution.py:69
  32.0 47.7 %collective-permute-start.6 = (bf16[288,1792]{1,0:T(8,128)(2,1)S(1)}, bf16[288,1792]{1,0:T(8,128)(2,1)S(1)}, u32[]{:S(2)}, u32[]{:S(2)}) collective-permute-start(bf16[288,1792]{1,0:T(8,128)(2,1)S(1)} %bitcast.295), channel_id=1, source_target_pairs={{0,8},{8,0},{1,9},{9,1},{2,10},{10,2},{3,11},{11,3},{4,12},{12,4},... | collective-permute-start | bytes 3096584 | tf_op jit(solution)/shard_map/ppermute | solution.py:82
  81.7 248.2 %all-gather.7.cloned.1.call-start = ((), (), s32[]{:S(2)}) async-start(), calls=%async_computation.5 | async-start | bytes 3317760 | tf_op jit(solution)/shard_map/all_gather | solution.py:69
  81.8 25.2 %collective-permute-start.9 = (bf16[72,2304]{1,0:T(8,128)(2,1)}, bf16[72,2304]{1,0:T(8,128)(2,1)S(1)}, u32[]{:S(2)}, u32[]{:S(2)}) collective-permute-start(bf16[72,2304]{1,0:T(8,128)(2,1)} %param.17), channel_id=1, source_target_pairs={{0,8},{2,9},{4,10},{6,11},{8,12},{10,13},{12,14},{14,15},{1,0},{3,... | collective-permute-start | bytes 995336 | tf_op jit(solution)/shard_map/ppermute | solution.py:214
  81.9 25.2 %collective-permute-start.8 = (bf16[72,2304]{1,0:T(8,128)(2,1)}, bf16[72,2304]{1,0:T(8,128)(2,1)}, u32[]{:S(2)}, u32[]{:S(2)}) collective-permute-start(bf16[72,2304]{1,0:T(8,128)(2,1)} %param.17), channel_id=1, source_target_pairs={{0,0},{2,1},{4,2},{6,3},{8,4},{10,5},{12,6},{14,7},{1,8},{3,9},{5,... | collective-permute-start | bytes 995336 | tf_op jit(solution)/shard_map/ppermute | solution.py:214
  109.1 295.6 %all-gather.9.cloned.1.call-start = ((), (), s32[]{:S(2)}) async-start(), calls=%async_computation.6 | async-start | bytes 16957440 | tf_op jit(solution)/shard_map/all_gather | solution.py:69
  127.0 76.5 %collective-permute-start.19 = (bf16[288,2944]{1,0:T(8,128)(2,1)S(1)}, bf16[288,2944]{1,0:T(8,128)(2,1)S(1)}, u32[]{:S(2)}, u32[]{:S(2)}) collective-permute-start(bf16[288,2944]{1,0:T(8,128)(2,1)S(1)} %bitcast.286), channel_id=1, source_target_pairs={{0,8},{8,0},{1,9},{9,1},{2,10},{10,2},{3,11},{11,3},{4,12},{12,4},... | collective-permute-start | bytes 5087240 | tf_op jit(solution)/shard_map/ppermute | solution.py:82
  205.9 223.9 %all-gather.11.cloned.1.call-start = ((), (), s32[]{:S(2)}) async-start(), calls=%async_computation.7 | async-start | bytes 8478720 | tf_op jit(solution)/shard_map/all_gather | solution.py:69
  209.2 43.4 %collective-permute-start.2 = (bf16[64,2304]{1,0:T(8,128)(2,1)S(1)}, bf16[64,2304]{1,0:T(8,128)(2,1)S(1)}, u32[]{:S(2)}, u32[]{:S(2)}) collective-permute-start(bf16[64,2304]{1,0:T(8,128)(2,1)S(1)} %reshape.439), channel_id=1, source_target_pairs={{0,20},{4,16},{16,4},{20,0},{1,21},{5,17},{17,5},{21,1},{2,22},{6,... | collective-permute-start | bytes 884744 | tf_op jit(solution)/shard_map/ppermute | solution.py:36
  209.2 44.7 %collective-permute-start.1 = (bf16[64,2304]{1,0:T(8,128)(2,1)S(1)}, bf16[64,2304]{1,0:T(8,128)(2,1)S(1)}, u32[]{:S(2)}, u32[]{:S(2)}) collective-permute-start(bf16[64,2304]{1,0:T(8,128)(2,1)S(1)} %reshape.439), channel_id=1, source_target_pairs={{0,4},{4,0},{16,20},{20,16},{1,5},{5,1},{17,21},{21,17},{2,6},{6,2... | collective-permute-start | bytes 884744 | tf_op jit(solution)/shard_map/ppermute | solution.py:36
  211.5 42.7 %collective-permute-start = (bf16[64,2304]{1,0:T(8,128)(2,1)S(1)}, bf16[64,2304]{1,0:T(8,128)(2,1)}, u32[]{:S(2)}, u32[]{:S(2)}) collective-permute-start(bf16[64,2304]{1,0:T(8,128)(2,1)S(1)} %reshape.439), channel_id=1, source_target_pairs={{0,16},{4,20},{16,0},{20,4},{1,17},{5,21},{17,1},{21,5},{2,18},{6,... | collective-permute-start | bytes 884744 | tf_op jit(solution)/shard_map/ppermute | solution.py:36
  214.8 33.3 %collective-permute-start.31 = (bf16[64,2304]{1,0:T(8,128)(2,1)S(1)}, bf16[64,2304]{1,0:T(8,128)(2,1)S(1)}, u32[]{:S(2)}, u32[]{:S(2)}) collective-permute-start(bf16[64,2304]{1,0:T(8,128)(2,1)S(1)} %get-tuple-element.50), channel_id=1, source_target_pairs={{0,20},{4,16},{16,4},{20,0},{1,21},{5,17},{17,5},{21,1},{2,22},{6,... | collective-permute-start | bytes 884744 | tf_op jit(solution)/shard_map/ppermute | solution.py:36
  253.9 40.4 %collective-permute-start.35 = (bf16[184,2304]{1,0:T(8,128)(2,1)S(1)}, bf16[184,2304]{1,0:T(8,128)(2,1)S(1)}, u32[]{:S(2)}, u32[]{:S(2)}) collective-permute-start(bf16[184,2304]{1,0:T(8,128)(2,1)S(1)} %pad.20), channel_id=1, source_target_pairs={{0,8},{8,0},{1,9},{9,1},{2,10},{10,2},{3,11},{11,3},{4,12},{12,4},... | collective-permute-start | bytes 2543624 | tf_op jit(solution)/shard_map/ppermute | solution.py:82
  296.0 278.7 %reduce-scatter.5.cloned.1.call-start = ((), (), s32[]{:S(2)}) async-start(), calls=%async_computation.8 | async-start | bytes 8478720 | tf_op jit(solution)/shard_map/reduce_scatter | solution.py:88
  429.6 211.3 %reduce-scatter.11.cloned.1.call-start = ((), (), s32[]{:S(2)}) async-start(), calls=%async_computation.11 | async-start | bytes 3317760 | tf_op jit(solution)/shard_map/reduce_scatter | solution.py:88
  497.2 38.2 %collective-permute-start.40 = (bf16[64,2304]{1,0:T(8,128)(2,1)}, bf16[64,2304]{1,0:T(8,128)(2,1)}, u32[]{:S(2)}, u32[]{:S(2)}) collective-permute-start(bf16[64,2304]{1,0:T(8,128)(2,1)} %get-tuple-element.92), channel_id=1, source_target_pairs={{0,4},{4,0},{16,20},{20,16},{1,5},{5,1},{17,21},{21,17},{2,6},{6,2... | collective-permute-start | bytes 884744 | tf_op jit(solution)/shard_map/ppermute | solution.py:36
  499.5 35.9 %collective-permute-start.39 = (bf16[64,2304]{1,0:T(8,128)(2,1)}, bf16[64,2304]{1,0:T(8,128)(2,1)}, u32[]{:S(2)}, u32[]{:S(2)}) collective-permute-start(bf16[64,2304]{1,0:T(8,128)(2,1)} %get-tuple-element.90), channel_id=1, source_target_pairs={{0,16},{4,20},{16,0},{20,4},{1,17},{5,21},{17,1},{21,5},{2,18},{6,... | collective-permute-start | bytes 884744 | tf_op jit(solution)/shard_map/ppermute | solution.py:36
  505.2 30.3 %collective-permute-start.38 = (bf16[64,2304]{1,0:T(8,128)(2,1)}, bf16[64,2304]{1,0:T(8,128)(2,1)}, u32[]{:S(2)}, u32[]{:S(2)}) collective-permute-start(bf16[64,2304]{1,0:T(8,128)(2,1)} %get-tuple-element.88), channel_id=1, source_target_pairs={{0,20},{4,16},{16,4},{20,0},{1,21},{5,17},{17,5},{21,1},{2,22},{6,... | collective-permute-start | bytes 884744 | tf_op jit(solution)/shard_map/ppermute | solution.py:36
  510.2 25.2 %collective-permute-start.37 = (bf16[64,2304]{1,0:T(8,128)(2,1)}, bf16[64,2304]{1,0:T(8,128)(2,1)}, u32[]{:S(2)}, u32[]{:S(2)}) collective-permute-start(bf16[64,2304]{1,0:T(8,128)(2,1)} %get-tuple-element.89), channel_id=1, source_target_pairs={{0,4},{4,0},{16,20},{20,16},{1,5},{5,1},{17,21},{21,17},{2,6},{6,2... | collective-permute-start | bytes 884744 | tf_op jit(solution)/shard_map/ppermute | solution.py:36
  607.5 142.7 %reduce-scatter.7.cloned.1.call-start = ((), (), s32[]{:S(2)}) async-start(), calls=%async_computation.9 | async-start | bytes 16957440 | tf_op jit(solution)/shard_map/reduce_scatter | solution.py:88
  608.2 261.2 %reduce-scatter.9.cloned.1.call-start = ((), (), s32[]{:S(2)}) async-start(), calls=%async_computation.10 | async-start | bytes 10321920 | tf_op jit(solution)/shard_map/reduce_scatter | solution.py:88
  610.6 38.8 %collective-permute-start.70 = (bf16[184,2304]{1,0:T(8,128)(2,1)}, bf16[184,2304]{1,0:T(8,128)(2,1)}, u32[]{:S(2)}, u32[]{:S(2)}) collective-permute-start(bf16[184,2304]{1,0:T(8,128)(2,1)} %constant_dynamic-slice_fusion), channel_id=1, source_target_pairs={{0,8},{8,0},{1,9},{9,1},{2,10},{10,2},{3,11},{11,3},{4,12},{12,4},... | collective-permute-start | bytes 2543624 | tf_op jit(solution)/shard_map/ppermute | solution.py:97
  774.3 73.4 %collective-permute-start.66 = (bf16[288,2944]{1,0:T(8,128)(2,1)}, bf16[288,2944]{1,0:T(8,128)(2,1)}, u32[]{:S(2)}, u32[]{:S(2)}) collective-permute-start(bf16[288,2944]{1,0:T(8,128)(2,1)} %constant_dynamic-slice_fusion.1), channel_id=1, source_target_pairs={{0,8},{8,0},{1,9},{9,1},{2,10},{10,2},{3,11},{11,3},{4,12},{12,4},... | collective-permute-start | bytes 5087240 | tf_op jit(solution)/shard_map/ppermute | solution.py:97
  871.7 46.9 %collective-permute-start.60 = (bf16[288,1792]{1,0:T(8,128)(2,1)}, bf16[288,1792]{1,0:T(8,128)(2,1)}, u32[]{:S(2)}, u32[]{:S(2)}) collective-permute-start(bf16[288,1792]{1,0:T(8,128)(2,1)} %constant_dynamic-slice_fusion.4), channel_id=1, source_target_pairs={{0,8},{8,0},{1,9},{9,1},{2,10},{10,2},{3,11},{11,3},{4,12},{12,4},... | collective-permute-start | bytes 3096584 | tf_op jit(solution)/shard_map/ppermute | solution.py:97
  (153 other events, 1298.1 us)
Sparse Core Ops, SparseCore 0:
  81.8 57.7 all-gather.4
  141.8 29.5 all-gather.6
  205.9 85.5 all-gather.8
  296.1 47.0 all-gather.10
  429.8 61.2 reduce-scatter.4
  607.6 33.2 reduce-scatter.10
  643.6 106.5 reduce-scatter.6
  752.8 70.5 reduce-scatter.8

commit v2 on v1

--- a/solution.py
+++ b/solution.py
@@ -88,13 +88,15 @@
     return lax.psum_scatter(partial, LINE, scatter_dimension=0, tiled=True)
 
 
-def half_scatter(partial):
+def half_scatter(partial, *late):
     if lax.axis_size("h") == 2:
         rows = partial.shape[0] // 2
         h = lax.axis_index("h")
         other = lax.dynamic_slice_in_dim(partial, (1 - h) * rows, rows)
         own = lax.dynamic_slice_in_dim(partial, h * rows, rows)
         other = lax.ppermute(other, "h", [(0, 1), (1, 0)])
+        if late:
+            own = after(own, *late)
         return own.astype(F32) + other.astype(F32)
     return lax.psum_scatter(partial, "h", scatter_dimension=0, tiled=True).astype(F32)
 
@@ -105,8 +107,8 @@
     return half_gather(mine.reshape(four * rows, n))
 
 
-def column_grad(scattered, rows):
-    mine = half_scatter(scattered).astype(BF16)
+def column_grad(scattered, rows, *late):
+    mine = half_scatter(scattered, *late).astype(BF16)
     return plane_exchange(mine.reshape(4, rows, mine.shape[1]))
 
 
@@ -216,7 +218,6 @@
     else:
         out_block = half_gather(lax.ppermute(out_weight, HLXC, head_order(0)))
     other_lengths = lax.ppermute(lengths, "l", [(0, 1), (1, 0)])
-    gathered = [plane_gather(to_line(inputs[s], rows)) for s in range(count)]
     down_block = half_gather(jnp.pad(down_weight, ((0, padded - units), (0, 0))))
     qkv_block = column_block(
         jnp.concatenate(
@@ -226,6 +227,7 @@
     gu_block = column_block(
         jnp.concatenate([split_units(gate_weight), split_units(up_weight)], axis=2)
     )
+    gathered = [plane_gather(to_line(inputs[s], rows)) for s in range(count)]
     w_out = line_gather(out_block)
     w_qkv = line_gather(qkv_block)
     w_gu = line_gather(gu_block)
@@ -325,7 +327,8 @@
     input_grads = []
     for s in range(count):
         queries, keys, values, probs, attended = kept[s]
-        grad_att = dot(after(branch1[s], down_part), w_out, NT).astype(BF16).reshape(2, 2 * tokens, heads, HEAD_DIM)
+        grad_att = dot(after(branch1[s], down_part), w_out, NT).astype(BF16)
+        grad_att = grad_att.reshape(2, 2 * tokens, heads, HEAD_DIM)
         grad_probs = einsum("bqhe,bkhe->bhqk", grad_att, values)
         delta = jnp.sum(probs * grad_probs, axis=-1, keepdims=True)
         grad_scores = (probs * (grad_probs - delta)).astype(BF16)
@@ -345,7 +348,7 @@
         jnp.concatenate(normed, axis=0), jnp.concatenate(grad_qkv, axis=0), TN
     ).astype(BF16)
     qkv_part = line_scatter(qkv_terms)
-    all_attended = after(jnp.concatenate([k[4] for k in kept], axis=0), qkv_terms)
+    all_attended = after(jnp.concatenate([k[4] for k in kept], axis=0), qkv_terms, gu_part)
     out_terms = dot(all_attended, jnp.concatenate(branch1, axis=0), TN).astype(BF16)
     out_part = line_scatter(out_terms)
     own = out_part.shape[0] // halves
@@ -361,12 +364,12 @@
         )
     else:
         out_grad = lax.ppermute(half_scatter(out_part), HLXC, [(b, a) for a, b in head_order(0)])
-    gu_raw = column_grad(gu_part, rows)
+    all_in_terms = [dot(after(g, out_terms), w_qkv, NT).astype(BF16) for g in grad_qkv]
+    gu_raw = column_grad(gu_part, rows, *all_in_terms)
     qkv_raw = column_grad(qkv_part, rows)
     factor_one = [norm_factor(v) for v in x_float]
     for s in range(count):
-        in_terms = dot(after(grad_qkv[s], gu_part, out_terms), w_qkv, NT)
-        grad_norm = plane_scatter(in_terms)
+        grad_norm = plane_scatter(all_in_terms[s])
         grad_norm = from_line(grad_norm, rows) * gain_one
         input_grads.append(
             (grad_mids[s] + norm_back(x_float[s], factor_one[s], grad_norm)).astype(BF16)
@@ -394,7 +397,7 @@
         out_grad,
         gate_grad,
         up_grad,
-        half_scatter(down_part)[:units],
+        half_scatter(down_part, qkv_part)[:units],
         attn_gain_grad,
         ffn_gain_grad,
     )

time: 954 us -> 808 us (0.85)
  waiting for transfers between devices: 481 us -> 337 us
    reduce_scatter x4, waiting for transfers between devices: 121 us -> 0.03 us  [line_scatter(): return lax.psum_scatter(partial, LINE, scatter_dimension=0, tiled=True)]
    ppermute x3, waiting for transfers between devices: 75.5 us -> 39.1 us  [half_scatter(): other = lax.ppermute(other, 'h', [(0, 1), (1, 0)])]
    ppermute x3, waiting for transfers between devices: 120 us -> 130 us  [half_gather(): other = lax.ppermute(block, 'h', [(0, 1), (1, 0)])]
    ppermute x2, waiting for transfers between devices: 4.34 us -> 14.2 us  [body(): lax.ppermute(lax.dynamic_slice_in_dim(out_part, (h ^ flip) * own, own), H...]
    unnamed x220 -> x230, local copies, waits for them, and re-layouts: 34 us -> 33.2 us
  transfers between devices with their start and end apart: 79 -> 79, of which waited for: 38 -> 35; matrix products, arithmetic and copies ran while one was open for 31% -> 42% of each run, Pallas kernels for 0% -> 0%
where the time goes in v2:
time: 808 us; the launch traced here: 801 us
  waiting for transfers between devices  337 us (42%)
  local copies, waits for them, and re-layouts  161 us (20%)
  matrix products  134 us (17%)
  starting transfers between devices  86.1 us (11%)
  other arithmetic  66.6 us (8%)
  between operations  16.5 us (2%)
    ppermute x60, waiting for transfers between devices, flip_send(): return lax.ppermute(block, PLANE, [(p, p ^ flip) for p in range(4)])  150 us
    ppermute x3, waiting for transfers between devices, half_gather(): other = lax.ppermute(block, 'h', [(0, 1), (1, 0)])  130 us
    dot_general x21, matrix products, dot(): lax.dot_general(left, right, (contract, ((), ())), preferred_element_type...  124 us
    ppermute x60, starting transfers between devices, flip_send(): return lax.ppermute(block, PLANE, [(p, p ^ flip) for p in range(4)])  67.5 us
    ppermute x3, waiting for transfers between devices, half_scatter(): other = lax.ppermute(other, 'h', [(0, 1), (1, 0)])  39.1 us
    unnamed x230, local copies, waits for them, and re-layouts  33.2 us
    reshape x12, local copies, waits for them, and re-layouts, from_line(): blocks = tokens.reshape(count, 2, 2, -1, 2, 2, rows)  25.3 us
  transfers between devices with their start and end apart: 79, of which 35 were waited for; matrix products, arithmetic and copies ran while one was open for 42% of the time, Pallas kernels for 0%

profile of v2, /device:TPU:0, one launch (start us, length us, event | category | flops | bytes accessed | tf_op | source)
XLA Modules:
  0.0 801.2 jit_solution(865468033255949690)
XLA Ops:
  34.9 43.8 %collective-permute-done.6 = bf16[288,1792]{1,0:T(8,128)(2,1)S(1)} collective-permute-done((bf16[288,1792]{1,0:T(8,128)(2,1)S(1)}, bf16[288,1792]{1,0:T(8,128)(2,1)S(1)}, u32[]{:S(2)}, u32[]{:S(2)}) %collective-permute-start.6) | collective-permute-done | bytes 1032224 | tf_op jit(solution)/shard_map/ppermute | solution.py:82
  108.0 7.0 collective-permute-done.16
  115.0 8.8 %collective-permute-done.17 = bf16[72,2944]{1,0:T(8,128)(2,1)S(1)} collective-permute-done((bf16[72,2944]{1,0:T(8,128)(2,1)S(1)}, bf16[72,2944]{1,0:T(8,128)(2,1)S(1)}, u32[]{:S(2)}, u32[]{:S(2)}) %collective-permute-start.17) | collective-permute-done | bytes 423968 | tf_op jit(solution)/shard_map/ppermute | solution.py:36
  127.3 72.4 %collective-permute-done.19 = bf16[288,2944]{1,0:T(8,128)(2,1)S(1)} collective-permute-done((bf16[288,2944]{1,0:T(8,128)(2,1)S(1)}, bf16[288,2944]{1,0:T(8,128)(2,1)S(1)}, u32[]{:S(2)}, u32[]{:S(2)}) %collective-permute-start.19) | collective-permute-done | bytes 1695776 | tf_op jit(solution)/shard_map/ppermute | solution.py:82
  245.8 10.0 %collective-permute-done.1 = bf16[64,2304]{1,0:T(8,128)(2,1)S(1)} collective-permute-done((bf16[64,2304]{1,0:T(8,128)(2,1)S(1)}, bf16[64,2304]{1,0:T(8,128)(2,1)S(1)}, u32[]{:S(2)}, u32[]{:S(2)}) %collective-permute-start.1) | collective-permute-done | bytes 294944 | tf_op jit(solution)/shard_map/ppermute | solution.py:36
  255.8 6.5 collective-permute-done.2
  263.4 14.2 %collective-permute-done.35 = bf16[184,2304]{1,0:T(8,128)(2,1)S(1)} collective-permute-done((bf16[184,2304]{1,0:T(8,128)(2,1)S(1)}, bf16[184,2304]{1,0:T(8,128)(2,1)S(1)}, u32[]{:S(2)}, u32[]{:S(2)}) %collective-permute-start.35) | collective-permute-done | bytes 847904 | tf_op jit(solution)/shard_map/ppermute | solution.py:82
  286.0 6.7 fusion.2
  295.0 8.3 %fusion.4 = f32[256,1728]{0,1:T(8,128)} fusion(bf16[256,2304]{1,0:T(8,128)(2,1)S(1)} %copy-done.38, bf16[2304,1792]{1,0:T(8,128)(2,1)} %all-gather.5.cloned.1.call-done), kind=kOutput, calls=%fused_computation.7 | convolution fusion | flops 2038431744 | bytes 11206656 | tf_op jit(solution)/shard_map/dot_general | solution.py:28
  338.4 6.9 collective-permute-done.12
  373.7 7.9 fusion.38
  391.6 7.5 convolution_convert_fusion.2
  415.9 6.9 multiply_convert_fusion.1
  427.6 8.3 %convolution_convert_fusion.6 = bf16[256,2304]{1,0:T(8,128)(2,1)} fusion(bf16[256,2944]{1,0:T(8,128)(2,1)S(1)} %pad_maximum_fusion.4, bf16[2304,2944]{1,0:T(8,128)(2,1)} %all-gather.9.cloned.1.call-done), kind=kOutput, calls=%fused_computation.12 | convolution fusion | flops 3473473536 | bytes 16252928 | tf_op jit(solution)/shard_map/dot_general | solution.py:28
  435.9 8.3 %convolution_convert_fusion.7 = bf16[256,2304]{1,0:T(8,128)(2,1)} fusion(bf16[256,2944]{1,0:T(8,128)(2,1)S(1)} %pad_maximum_fusion.3, bf16[2304,2944]{1,0:T(8,128)(2,1)} %all-gather.9.cloned.1.call-done), kind=kOutput, calls=%fused_computation.13 | convolution fusion | flops 3473473536 | bytes 16252928 | tf_op jit(solution)/shard_map/dot_general | solution.py:28
  444.2 11.7 %convolution_convert_fusion = bf16[2304,2944]{1,0:T(8,128)(2,1)} fusion(bf16[512,2304]{1,0:T(8,128)(2,1)} %constant_dynamic-update-slice_fusion, bf16[256,2944]{1,0:T(8,128)(2,1)S(1)} %pad_maximum_fusion.4, bf16[256,2944]{1,0:T(8,128)(2,1)S(1)} %pad_maximum_fusion.3), kind=kOutput, calls=%fused_computation.2 | convolution fusion | flops 6958579712 | bytes 18939904 | tf_op jit(solution)/shard_map/dot_general | solution.py:28
  456.2 6.6 fusion.174
  468.4 6.4 fusion.173
  491.0 7.4 collective-permute-done.42
  581.7 6.7 convolution_convert_fusion.1
  636.1 24.7 %collective-permute-done.55 = bf16[64,2304]{1,0:T(8,128)(2,1)} collective-permute-done((bf16[64,2304]{1,0:T(8,128)(2,1)}, bf16[64,2304]{1,0:T(8,128)(2,1)}, u32[]{:S(2)}, u32[]{:S(2)}) %collective-permute-start.55) | collective-permute-done | bytes 294944 | tf_op jit(solution)/shard_map/ppermute | solution.py:36
  674.6 15.9 %collective-permute-done.66 = bf16[288,2944]{1,0:T(8,128)(2,1)} collective-permute-done((bf16[288,2944]{1,0:T(8,128)(2,1)}, bf16[288,2944]{1,0:T(8,128)(2,1)}, u32[]{:S(2)}, u32[]{:S(2)}) %collective-permute-start.66) | collective-permute-done | bytes 1695776 | tf_op jit(solution)/shard_map/ppermute | solution.py:97
  732.2 23.2 %collective-permute-done.60 = bf16[288,1792]{1,0:T(8,128)(2,1)} collective-permute-done((bf16[288,1792]{1,0:T(8,128)(2,1)}, bf16[288,1792]{1,0:T(8,128)(2,1)}, u32[]{:S(2)}, u32[]{:S(2)}) %collective-permute-start.60) | collective-permute-done | bytes 1032224 | tf_op jit(solution)/shard_map/ppermute | solution.py:97
  778.8 14.2 %collective-permute-done.65 = bf16[72,2304]{1,0:T(8,128)(2,1)S(1)} collective-permute-done((bf16[72,2304]{1,0:T(8,128)(2,1)S(1)}, bf16[72,2304]{1,0:T(8,128)(2,1)S(1)}, u32[]{:S(2)}, u32[]{:S(2)}) %collective-permute-start.65) | collective-permute-done | bytes 331808 | tf_op jit(solution)/shard_map/ppermute | solution.py:358
  (602 shorter events, 444.4 us)
Async XLA Ops:
  7.2 272.4 %all-gather.5.cloned.1.call-start = ((), (), s32[]{:S(2)}) async-start(), calls=%async_computation.4 | async-start | bytes 10321920 | tf_op jit(solution)/shard_map/all_gather | solution.py:69
  32.3 46.5 %collective-permute-start.6 = (bf16[288,1792]{1,0:T(8,128)(2,1)S(1)}, bf16[288,1792]{1,0:T(8,128)(2,1)S(1)}, u32[]{:S(2)}, u32[]{:S(2)}) collective-permute-start(bf16[288,1792]{1,0:T(8,128)(2,1)S(1)} %bitcast.295), channel_id=1, source_target_pairs={{0,8},{8,0},{1,9},{9,1},{2,10},{10,2},{3,11},{11,3},{4,12},{12,4},... | collective-permute-start | bytes 3096584 | tf_op jit(solution)/shard_map/ppermute | solution.py:82
  80.8 230.2 %all-gather.7.cloned.1.call-start = ((), (), s32[]{:S(2)}) async-start(), calls=%async_computation.5 | async-start | bytes 3317760 | tf_op jit(solution)/shard_map/all_gather | solution.py:69
  108.0 265.7 %all-gather.9.cloned.1.call-start = ((), (), s32[]{:S(2)}) async-start(), calls=%async_computation.6 | async-start | bytes 16957440 | tf_op jit(solution)/shard_map/all_gather | solution.py:69
  124.6 75.1 %collective-permute-start.19 = (bf16[288,2944]{1,0:T(8,128)(2,1)S(1)}, bf16[288,2944]{1,0:T(8,128)(2,1)S(1)}, u32[]{:S(2)}, u32[]{:S(2)}) collective-permute-start(bf16[288,2944]{1,0:T(8,128)(2,1)S(1)} %bitcast.286), channel_id=1, source_target_pairs={{0,8},{8,0},{1,9},{9,1},{2,10},{10,2},{3,11},{11,3},{4,12},{12,4},... | collective-permute-start | bytes 5087240 | tf_op jit(solution)/shard_map/ppermute | solution.py:82
  202.1 213.8 %all-gather.11.cloned.1.call-start = ((), (), s32[]{:S(2)}) async-start(), calls=%async_computation.7 | async-start | bytes 8478720 | tf_op jit(solution)/shard_map/all_gather | solution.py:69
  205.4 32.9 %collective-permute-start.20 = (bf16[64,2304]{1,0:T(8,128)(2,1)S(1)}, bf16[64,2304]{1,0:T(8,128)(2,1)S(1)}, u32[]{:S(2)}, u32[]{:S(2)}) collective-permute-start(bf16[64,2304]{1,0:T(8,128)(2,1)S(1)} %reshape.455), channel_id=1, source_target_pairs={{0,16},{4,20},{16,0},{20,4},{1,17},{5,21},{17,1},{21,5},{2,18},{6,... | collective-permute-start | bytes 884744 | tf_op jit(solution)/shard_map/ppermute | solution.py:36
  206.3 33.4 %collective-permute-start.21 = (bf16[64,2304]{1,0:T(8,128)(2,1)S(1)}, bf16[64,2304]{1,0:T(8,128)(2,1)S(1)}, u32[]{:S(2)}, u32[]{:S(2)}) collective-permute-start(bf16[64,2304]{1,0:T(8,128)(2,1)S(1)} %reshape.455), channel_id=1, source_target_pairs={{0,4},{4,0},{16,20},{20,16},{1,5},{5,1},{17,21},{21,17},{2,6},{6,2... | collective-permute-start | bytes 884744 | tf_op jit(solution)/shard_map/ppermute | solution.py:36
  206.9 35.5 %collective-permute-start.22 = (bf16[64,2304]{1,0:T(8,128)(2,1)S(1)}, bf16[64,2304]{1,0:T(8,128)(2,1)}, u32[]{:S(2)}, u32[]{:S(2)}) collective-permute-start(bf16[64,2304]{1,0:T(8,128)(2,1)S(1)} %reshape.455), channel_id=1, source_target_pairs={{0,20},{4,16},{16,4},{20,0},{1,21},{5,17},{17,5},{21,1},{2,22},{6,... | collective-permute-start | bytes 884744 | tf_op jit(solution)/shard_map/ppermute | solution.py:36
  239.7 37.9 %collective-permute-start.35 = (bf16[184,2304]{1,0:T(8,128)(2,1)S(1)}, bf16[184,2304]{1,0:T(8,128)(2,1)S(1)}, u32[]{:S(2)}, u32[]{:S(2)}) collective-permute-start(bf16[184,2304]{1,0:T(8,128)(2,1)S(1)} %pad.20), channel_id=1, source_target_pairs={{0,8},{8,0},{1,9},{9,1},{2,10},{10,2},{3,11},{11,3},{4,12},{12,4},... | collective-permute-start | bytes 2543624 | tf_op jit(solution)/shard_map/ppermute | solution.py:82
  244.3 83.8 %collective-permute-start.33 = (bf16[64,2304]{1,0:T(8,128)(2,1)}, bf16[64,2304]{1,0:T(8,128)(2,1)}, u32[]{:S(2)}, u32[]{:S(2)}) collective-permute-start(bf16[64,2304]{1,0:T(8,128)(2,1)} %get-tuple-element.52), channel_id=1, source_target_pairs={{0,4},{4,0},{16,20},{20,16},{1,5},{5,1},{17,21},{21,17},{2,6},{6,2... | collective-permute-start | bytes 884744 | tf_op jit(solution)/shard_map/ppermute | solution.py:36
  279.3 280.4 %reduce-scatter.5.cloned.1.call-start = ((), (), s32[]{:S(2)}) async-start(), calls=%async_computation.8 | async-start | bytes 8478720 | tf_op jit(solution)/shard_map/reduce_scatter | solution.py:88
  334.3 26.6 %collective-permute-start.34 = (bf16[64,2304]{1,0:T(8,128)(2,1)}, bf16[64,2304]{1,0:T(8,128)(2,1)}, u32[]{:S(2)}, u32[]{:S(2)}) collective-permute-start(bf16[64,2304]{1,0:T(8,128)(2,1)} %get-tuple-element.52), channel_id=1, source_target_pairs={{0,20},{4,16},{16,4},{20,0},{1,21},{5,17},{17,5},{21,1},{2,22},{6,... | collective-permute-start | bytes 884744 | tf_op jit(solution)/shard_map/ppermute | solution.py:36
  399.2 198.4 %reduce-scatter.7.cloned.1.call-start = ((), (), s32[]{:S(2)}) async-start(), calls=%async_computation.9 | async-start | bytes 16957440 | tf_op jit(solution)/shard_map/reduce_scatter | solution.py:88
  455.9 255.8 %reduce-scatter.9.cloned.1.call-start = ((), (), s32[]{:S(2)}) async-start(), calls=%async_computation.10 | async-start | bytes 10321920 | tf_op jit(solution)/shard_map/reduce_scatter | solution.py:88
  463.7 25.8 %collective-permute-start.36 = (bf16[64,2304]{1,0:T(8,128)(2,1)S(1)}, bf16[64,2304]{1,0:T(8,128)(2,1)}, u32[]{:S(2)}, u32[]{:S(2)}) collective-permute-start(bf16[64,2304]{1,0:T(8,128)(2,1)S(1)} %get-tuple-element.95), channel_id=1, source_target_pairs={{0,16},{4,20},{16,0},{20,4},{1,17},{5,21},{17,1},{21,5},{2,18},{6,... | collective-permute-start | bytes 884744 | tf_op jit(solution)/shard_map/ppermute | solution.py:36
  464.2 59.8 %collective-permute-start.37 = (bf16[64,2304]{1,0:T(8,128)(2,1)}, bf16[64,2304]{1,0:T(8,128)(2,1)}, u32[]{:S(2)}, u32[]{:S(2)}) collective-permute-start(bf16[64,2304]{1,0:T(8,128)(2,1)} %get-tuple-element.97), channel_id=1, source_target_pairs={{0,4},{4,0},{16,20},{20,16},{1,5},{5,1},{17,21},{21,17},{2,6},{6,2... | collective-permute-start | bytes 884744 | tf_op jit(solution)/shard_map/ppermute | solution.py:36
  489.5 34.5 %collective-permute-start.38 = (bf16[64,2304]{1,0:T(8,128)(2,1)}, bf16[64,2304]{1,0:T(8,128)(2,1)}, u32[]{:S(2)}, u32[]{:S(2)}) collective-permute-start(bf16[64,2304]{1,0:T(8,128)(2,1)} %get-tuple-element.96), channel_id=1, source_target_pairs={{0,20},{4,16},{16,4},{20,0},{1,21},{5,17},{17,5},{21,1},{2,22},{6,... | collective-permute-start | bytes 884744 | tf_op jit(solution)/shard_map/ppermute | solution.py:36
  588.4 186.0 %reduce-scatter.11.cloned.1.call-start = ((), (), s32[]{:S(2)}) async-start(), calls=%async_computation.11 | async-start | bytes 3317760 | tf_op jit(solution)/shard_map/reduce_scatter | solution.py:88
  594.9 166.0 %collective-permute-start.70 = (bf16[184,2304]{1,0:T(8,128)(2,1)}, bf16[184,2304]{1,0:T(8,128)(2,1)}, u32[]{:S(2)}, u32[]{:S(2)}) collective-permute-start(bf16[184,2304]{1,0:T(8,128)(2,1)} %get-tuple-element.72), channel_id=1, source_target_pairs={{0,8},{8,0},{1,9},{9,1},{2,10},{10,2},{3,11},{11,3},{4,12},{12,4},... | collective-permute-start | bytes 2543624 | tf_op jit(solution)/shard_map/ppermute | solution.py:97
  621.4 69.1 %collective-permute-start.66 = (bf16[288,2944]{1,0:T(8,128)(2,1)}, bf16[288,2944]{1,0:T(8,128)(2,1)}, u32[]{:S(2)}, u32[]{:S(2)}) collective-permute-start(bf16[288,2944]{1,0:T(8,128)(2,1)} %get-tuple-element.66), channel_id=1, source_target_pairs={{0,8},{8,0},{1,9},{9,1},{2,10},{10,2},{3,11},{11,3},{4,12},{12,4},... | collective-permute-start | bytes 5087240 | tf_op jit(solution)/shard_map/ppermute | solution.py:97
  623.3 37.5 %collective-permute-start.55 = (bf16[64,2304]{1,0:T(8,128)(2,1)}, bf16[64,2304]{1,0:T(8,128)(2,1)}, u32[]{:S(2)}, u32[]{:S(2)}) collective-permute-start(bf16[64,2304]{1,0:T(8,128)(2,1)} %get-tuple-element.85), channel_id=1, source_target_pairs={{0,4},{4,0},{16,20},{20,16},{1,5},{5,1},{17,21},{21,17},{2,6},{6,2... | collective-permute-start | bytes 884744 | tf_op jit(solution)/shard_map/ppermute | solution.py:36
  628.4 35.6 %collective-permute-start.56 = (bf16[64,2304]{1,0:T(8,128)(2,1)}, bf16[64,2304]{1,0:T(8,128)(2,1)}, u32[]{:S(2)}, u32[]{:S(2)}) collective-permute-start(bf16[64,2304]{1,0:T(8,128)(2,1)} %get-tuple-element.84), channel_id=1, source_target_pairs={{0,20},{4,16},{16,4},{20,0},{1,21},{5,17},{17,5},{21,1},{2,22},{6,... | collective-permute-start | bytes 884744 | tf_op jit(solution)/shard_map/ppermute | solution.py:36
  714.0 41.4 %collective-permute-start.60 = (bf16[288,1792]{1,0:T(8,128)(2,1)}, bf16[288,1792]{1,0:T(8,128)(2,1)}, u32[]{:S(2)}, u32[]{:S(2)}) collective-permute-start(bf16[288,1792]{1,0:T(8,128)(2,1)} %constant_dynamic-slice_fusion.6), channel_id=1, source_target_pairs={{0,8},{8,0},{1,9},{9,1},{2,10},{10,2},{3,11},{11,3},{4,12},{12,4},... | collective-permute-start | bytes 3096584 | tf_op jit(solution)/shard_map/ppermute | solution.py:97
  (158 other events, 1343.6 us)
Sparse Core Ops, SparseCore 0:
  81.0 57.8 all-gather.4
  140.9 30.3 all-gather.6
  202.2 87.0 all-gather.8
  291.3 49.1 all-gather.10
  399.3 60.7 reduce-scatter.4
  462.5 106.5 reduce-scatter.6
  588.5 68.8 reduce-scatter.8
  660.0 34.7 reduce-scatter.10

commit v3 on v2

--- a/solution.py
+++ b/solution.py
@@ -218,7 +218,6 @@
     else:
         out_block = half_gather(lax.ppermute(out_weight, HLXC, head_order(0)))
     other_lengths = lax.ppermute(lengths, "l", [(0, 1), (1, 0)])
-    down_block = half_gather(jnp.pad(down_weight, ((0, padded - units), (0, 0))))
     qkv_block = column_block(
         jnp.concatenate(
             [split_heads(w) for w in (query_weight, key_weight, value_weight)] + [extra], axis=2
@@ -227,12 +226,13 @@
     gu_block = column_block(
         jnp.concatenate([split_units(gate_weight), split_units(up_weight)], axis=2)
     )
+    down_own = jnp.pad(down_weight, ((0, padded - units), (0, 0)))
+    if halves == 2:
+        down_other = lax.ppermute(down_own, "h", [(0, 1), (1, 0)])
     gathered = [plane_gather(to_line(inputs[s], rows)) for s in range(count)]
     w_out = line_gather(out_block)
     w_qkv = line_gather(qkv_block)
     w_gu = line_gather(gu_block)
-    w_down = line_gather(down_block)
-
     step = jnp.arange(tokens, dtype=jnp.int32)
     place = jnp.concatenate([y * tokens + step, (1 - y) * tokens + step])
     local_place = place[:tokens]
@@ -260,7 +260,7 @@
     mids = []
     normed = []
     for s in range(count):
-        whole = gathered[s].astype(F32)
+        whole = after(gathered[s], gu_block).astype(F32)
         normed.append((whole * norm_factor(whole) * gain_one_line).astype(BF16))
         visible = (place[None, :] <= place[:, None])[None] & (
             place[None, None, :] < lengths_two[s][:, None, None]
@@ -276,6 +276,12 @@
         probs = expo / jnp.sum(expo, axis=-1, keepdims=True)
         attended = einsum("bhqk,bkhe->bqhe", probs.astype(BF16), values)
         attended = attended.astype(BF16).reshape(4 * tokens, part)
+        if s == 0:
+            if halves == 2:
+                down_block = in_order(down_own, after(down_other, attended))
+            else:
+                down_block = half_gather(down_own)
+            w_down = line_gather(down_block)
         mid = x_float[s] + BRANCH_SCALE * plane_scatter(dot(attended, w_out))
         kept.append((queries, keys, values, probs, attended))
         mids.append(mid)
@@ -312,16 +318,19 @@
 
     grad_mids = []
     branch1 = []
-    for s in range(count):
-        grad_norm = from_line(plane_scatter(norm_terms[s]), rows) * gain_two
+    own_branch1 = []
+    for s in range(count):
+        grad_norm = plane_scatter(norm_terms[s])
+        grad_norm = from_line(grad_norm, rows) * gain_two
         grad_mid = grad_y[s] + norm_back(mids[s], factor_two[s], grad_norm)
         grad_mids.append(grad_mid)
-        branch1.append(plane_gather((BRANCH_SCALE * grad_mid).astype(BF16)))
-
-    outputs = [
-        (mids[s] + BRANCH_SCALE * plane_scatter(dot(after(mixes[s], gu_terms), w_down))).astype(BF16)
-        for s in range(count)
-    ]
+        own_branch1.append((BRANCH_SCALE * grad_mid).astype(BF16))
+        branch1.append(plane_gather(own_branch1[s]))
+
+    outputs = []
+    for s in range(count):
+        terms = dot(after(mixes[s], gu_terms, *own_branch1), w_down)
+        outputs.append((mids[s] + BRANCH_SCALE * plane_scatter(terms)).astype(BF16))
 
     grad_qkv = []
     input_grads = []
@@ -375,8 +384,10 @@
             (grad_mids[s] + norm_back(x_float[s], factor_one[s], grad_norm)).astype(BF16)
         )
 
-    gate_grad = join_units(gu_raw[:, :, :hidden]).astype(F32)
-    up_grad = join_units(gu_raw[:, :, hidden:]).astype(F32)
+    gate_grad, up_grad = lax.optimization_barrier(
+        (join_units(gu_raw[:, :, :hidden]), join_units(gu_raw[:, :, hidden:]))
+    )
+    gate_grad, up_grad = gate_grad.astype(F32), up_grad.astype(F32)
     ffn_gain_grad = jnp.sum(
         gate_grad * gate_weight.astype(F32) + up_grad * up_weight.astype(F32), axis=1
     ) / ffn_gain.astype(F32)

time: 808 us -> 799 us (0.989)
    ppermute x3 -> x2, waiting for transfers between devices: 130 us -> 118 us  [half_gather(): other = lax.ppermute(block, 'h', [(0, 1), (1, 0)])]
    ppermute x60, waiting for transfers between devices: 150 us -> 162 us  [flip_send(): return lax.ppermute(block, PLANE, [(p, p ^ flip) for p in range(4)])]
    convert_element_type x4 -> x0, local copies, waits for them, and re-layouts: 10.5 us -> none  [the longest x2 5.24 us: body(): gate_grad = join_units(gu_raw[:, :, :hidden]).astype(F32)]
    unnamed x230 -> x224, local copies, waits for them, and re-layouts: 33.2 us -> 42 us
  transfers between devices with their start and end apart: 79 -> 79, of which waited for: 35 -> 36; matrix products, arithmetic and copies ran while one was open for 42% -> 40% of each run, Pallas kernels for 0% -> 0%
where the time goes in v3:
time: 799 us; the launch traced here: 793 us
  waiting for transfers between devices  335 us (42%)
  local copies, waits for them, and re-layouts  158 us (20%)
  matrix products  129 us (16%)
  starting transfers between devices  90.8 us (11%)
  other arithmetic  64 us (8%)
  between operations  16.2 us (2%)
    ppermute x60, waiting for transfers between devices, flip_send(): return lax.ppermute(block, PLANE, [(p, p ^ flip) for p in range(4)])  162 us
    dot_general x21, matrix products, dot(): lax.dot_general(left, right, (contract, ((), ())), preferred_element_type...  119 us
    ppermute x2, waiting for transfers between devices, half_gather(): other = lax.ppermute(block, 'h', [(0, 1), (1, 0)])  118 us
    ppermute x60, starting transfers between devices, flip_send(): return lax.ppermute(block, PLANE, [(p, p ^ flip) for p in range(4)])  70 us
    unnamed x224, local copies, waits for them, and re-layouts  42 us
    ppermute x3, waiting for transfers between devices, half_scatter(): other = lax.ppermute(other, 'h', [(0, 1), (1, 0)])  38.4 us
    reshape x12, local copies, waits for them, and re-layouts, from_line(): blocks = tokens.reshape(count, 2, 2, -1, 2, 2, rows)  23.2 us
  transfers between devices with their start and end apart: 79, of which 36 were waited for; matrix products, arithmetic and copies ran while one was open for 40% of the time, Pallas kernels for 0%

profile of v3, /device:TPU:0, one launch (start us, length us, event | category | flops | bytes accessed | tf_op | source)
XLA Modules:
  0.0 792.9 jit_solution(15648934569124351667)
XLA Ops:
  20.1 5.5 collective-permute-done.7
  25.6 6.1 collective-permute-done.8
  34.9 43.8 %collective-permute-done.10 = bf16[288,1792]{1,0:T(8,128)(2,1)S(1)} collective-permute-done((bf16[288,1792]{1,0:T(8,128)(2,1)S(1)}, bf16[288,1792]{1,0:T(8,128)(2,1)S(1)}, u32[]{:S(2)}, u32[]{:S(2)}) %collective-permute-start.10) | collective-permute-done | bytes 1032224 | tf_op jit(solution)/shard_map/ppermute | solution.py:82
  108.2 7.7 collective-permute-done.5
  115.9 7.8 collective-permute-done.3
  127.1 74.3 %collective-permute-done.6 = bf16[288,2944]{1,0:T(8,128)(2,1)S(1)} collective-permute-done((bf16[288,2944]{1,0:T(8,128)(2,1)S(1)}, bf16[288,2944]{1,0:T(8,128)(2,1)S(1)}, u32[]{:S(2)}, u32[]{:S(2)}) %collective-permute-start.6) | collective-permute-done | bytes 1695776 | tf_op jit(solution)/shard_map/ppermute | solution.py:82
  229.3 12.1 %collective-permute-done.29 = bf16[64,2304]{1,0:T(8,128)(2,1)S(1)} collective-permute-done((bf16[64,2304]{1,0:T(8,128)(2,1)}, bf16[64,2304]{1,0:T(8,128)(2,1)S(1)}, u32[]{:S(2)}, u32[]{:S(2)}) %collective-permute-start.29) | collective-permute-done | bytes 294944 | tf_op jit(solution)/shard_map/ppermute | solution.py:36
  251.1 7.8 fusion.2
  263.4 7.8 fusion.4
  363.0 7.7 fusion.30
  381.0 6.2 convolution_convert_fusion.2
  402.8 6.5 multiply_convert_fusion.3
  414.2 8.3 %convolution_convert_fusion.7 = bf16[256,2304]{1,0:T(8,128)(2,1)} fusion(bf16[256,2944]{1,0:T(8,128)(2,1)S(1)} %pad_maximum_fusion.3, bf16[2304,2944]{1,0:T(8,128)(2,1)} %all-gather.9.cloned.1.call-done), kind=kOutput, calls=%fused_computation.13 | convolution fusion | flops 3473473536 | bytes 16252928 | tf_op jit(solution)/shard_map/dot_general | solution.py:28
  422.5 7.3 convolution_convert_fusion.6
  429.8 12.2 %convolution_convert_fusion = bf16[2304,2944]{1,0:T(8,128)(2,1)} fusion(bf16[512,2304]{1,0:T(8,128)(2,1)} %constant_dynamic-update-slice_fusion, bf16[256,2944]{1,0:T(8,128)(2,1)S(1)} %pad_maximum_fusion.4, bf16[256,2944]{1,0:T(8,128)(2,1)S(1)} %pad_maximum_fusion.3), kind=kOutput, calls=%fused_computation.2 | convolution fusion | flops 6958579712 | bytes 18939904 | tf_op jit(solution)/shard_map/dot_general | solution.py:28
  531.9 6.7 convolution_convert_fusion.1
  564.4 6.0 collective-permute-done.47
  578.7 5.7 convolution_convert_fusion.4
  588.9 6.0 convolution_convert_fusion.5
  615.9 23.0 %collective-permute-done.55 = bf16[64,2304]{1,0:T(8,128)(2,1)} collective-permute-done((bf16[64,2304]{1,0:T(8,128)(2,1)}, bf16[64,2304]{1,0:T(8,128)(2,1)}, u32[]{:S(2)}, u32[]{:S(2)}) %collective-permute-start.55) | collective-permute-done | bytes 294944 | tf_op jit(solution)/shard_map/ppermute | solution.py:36
  660.6 38.4 %collective-permute-done.66 = bf16[288,2944]{1,0:T(8,128)(2,1)} collective-permute-done((bf16[288,2944]{1,0:T(8,128)(2,1)}, bf16[288,2944]{1,0:T(8,128)(2,1)}, u32[]{:S(2)}, u32[]{:S(2)}) %collective-permute-start.66) | collective-permute-done | bytes 1695776 | tf_op jit(solution)/shard_map/ppermute | solution.py:97
  707.7 15.1 %collective-permute-done.67 = bf16[72,2944]{1,0:T(8,128)(2,1)S(1)} collective-permute-done((bf16[72,2944]{1,0:T(8,128)(2,1)S(1)}, bf16[72,2944]{1,0:T(8,128)(2,1)S(1)}, u32[]{:S(2)}, u32[]{:S(2)}) %collective-permute-start.67) | collective-permute-done | bytes 423968 | tf_op jit(solution)/shard_map/ppermute | solution.py:36
  722.8 9.5 %collective-permute-done.69 = bf16[72,2944]{1,0:T(8,128)(2,1)S(1)} collective-permute-done((bf16[72,2944]{1,0:T(8,128)(2,1)S(1)}, bf16[72,2944]{1,0:T(8,128)(2,1)S(1)}, u32[]{:S(2)}, u32[]{:S(2)}) %collective-permute-start.69) | collective-permute-done | bytes 423968 | tf_op jit(solution)/shard_map/ppermute | solution.py:36
  771.7 13.2 %collective-permute-done.65 = bf16[72,2304]{1,0:T(8,128)(2,1)S(1)} collective-permute-done((bf16[72,2304]{1,0:T(8,128)(2,1)S(1)}, bf16[72,2304]{1,0:T(8,128)(2,1)S(1)}, u32[]{:S(2)}, u32[]{:S(2)}) %collective-permute-start.65) | collective-permute-done | bytes 331808 | tf_op jit(solution)/shard_map/ppermute | solution.py:367
  (597 shorter events, 432.0 us)
Async XLA Ops:
  7.2 239.4 %all-gather.5.cloned.1.call-start = ((), (), s32[]{:S(2)}) async-start(), calls=%async_computation.4 | async-start | bytes 10321920 | tf_op jit(solution)/shard_map/all_gather | solution.py:69
  32.3 46.5 %collective-permute-start.10 = (bf16[288,1792]{1,0:T(8,128)(2,1)S(1)}, bf16[288,1792]{1,0:T(8,128)(2,1)S(1)}, u32[]{:S(2)}, u32[]{:S(2)}) collective-permute-start(bf16[288,1792]{1,0:T(8,128)(2,1)S(1)} %bitcast.299), channel_id=1, source_target_pairs={{0,8},{8,0},{1,9},{9,1},{2,10},{10,2},{3,11},{11,3},{4,12},{12,4},... | collective-permute-start | bytes 3096584 | tf_op jit(solution)/shard_map/ppermute | solution.py:82
  80.8 223.3 %all-gather.7.cloned.1.call-start = ((), (), s32[]{:S(2)}) async-start(), calls=%async_computation.5 | async-start | bytes 3317760 | tf_op jit(solution)/shard_map/all_gather | solution.py:69
  80.9 24.9 %collective-permute-start.12 = (bf16[72,2304]{1,0:T(8,128)(2,1)}, bf16[72,2304]{1,0:T(8,128)(2,1)}, u32[]{:S(2)}, u32[]{:S(2)}) collective-permute-start(bf16[72,2304]{1,0:T(8,128)(2,1)} %param.17), channel_id=1, source_target_pairs={{0,0},{2,1},{4,2},{6,3},{8,4},{10,5},{12,6},{14,7},{1,8},{3,9},{5,... | collective-permute-start | bytes 995336 | tf_op jit(solution)/shard_map/ppermute | solution.py:216
  108.2 254.8 %all-gather.9.cloned.1.call-start = ((), (), s32[]{:S(2)}) async-start(), calls=%async_computation.6 | async-start | bytes 16957440 | tf_op jit(solution)/shard_map/all_gather | solution.py:69
  125.3 76.1 %collective-permute-start.6 = (bf16[288,2944]{1,0:T(8,128)(2,1)S(1)}, bf16[288,2944]{1,0:T(8,128)(2,1)S(1)}, u32[]{:S(2)}, u32[]{:S(2)}) collective-permute-start(bf16[288,2944]{1,0:T(8,128)(2,1)S(1)} %bitcast.290), channel_id=1, source_target_pairs={{0,8},{8,0},{1,9},{9,1},{2,10},{10,2},{3,11},{11,3},{4,12},{12,4},... | collective-permute-start | bytes 5087240 | tf_op jit(solution)/shard_map/ppermute | solution.py:82
  203.8 199.0 %all-gather.11.cloned.1.call-start = ((), (), s32[]{:S(2)}) async-start(), calls=%async_computation.7 | async-start | bytes 8478720 | tf_op jit(solution)/shard_map/all_gather | solution.py:69
  213.0 31.5 %collective-permute-start = (bf16[64,2304]{1,0:T(8,128)(2,1)S(1)}, bf16[64,2304]{1,0:T(8,128)(2,1)S(1)}, u32[]{:S(2)}, u32[]{:S(2)}) collective-permute-start(bf16[64,2304]{1,0:T(8,128)(2,1)S(1)} %reshape.439), channel_id=1, source_target_pairs={{0,16},{4,20},{16,0},{20,4},{1,17},{5,21},{17,1},{21,5},{2,18},{6,... | collective-permute-start | bytes 884744 | tf_op jit(solution)/shard_map/ppermute | solution.py:36
  222.8 21.6 %collective-permute-start.1 = (bf16[64,2304]{1,0:T(8,128)(2,1)S(1)}, bf16[64,2304]{1,0:T(8,128)(2,1)S(1)}, u32[]{:S(2)}, u32[]{:S(2)}) collective-permute-start(bf16[64,2304]{1,0:T(8,128)(2,1)S(1)} %reshape.439), channel_id=1, source_target_pairs={{0,4},{4,0},{16,20},{20,16},{1,5},{5,1},{17,21},{21,17},{2,6},{6,2... | collective-permute-start | bytes 884744 | tf_op jit(solution)/shard_map/ppermute | solution.py:36
  241.4 48.4 %collective-permute-start.31 = (bf16[64,2304]{1,0:T(8,128)(2,1)}, bf16[64,2304]{1,0:T(8,128)(2,1)}, u32[]{:S(2)}, u32[]{:S(2)}) collective-permute-start(bf16[64,2304]{1,0:T(8,128)(2,1)} %get-tuple-element.67), channel_id=1, source_target_pairs={{0,20},{4,16},{16,4},{20,0},{1,21},{5,17},{17,5},{21,1},{2,22},{6,... | collective-permute-start | bytes 884744 | tf_op jit(solution)/shard_map/ppermute | solution.py:36
  243.7 42.3 %collective-permute-start.35 = (bf16[184,2304]{1,0:T(8,128)(2,1)}, bf16[184,2304]{1,0:T(8,128)(2,1)}, u32[]{:S(2)}, u32[]{:S(2)}) collective-permute-start(bf16[184,2304]{1,0:T(8,128)(2,1)} %pad.20), channel_id=1, source_target_pairs={{0,8},{8,0},{1,9},{9,1},{2,10},{10,2},{3,11},{11,3},{4,12},{12,4},... | collective-permute-start | bytes 2543624 | tf_op jit(solution)/shard_map/ppermute | solution.py:231
  289.6 219.3 %reduce-scatter.5.cloned.1.call-start = ((), (), s32[]{:S(2)}) async-start(), calls=%async_computation.8 | async-start | bytes 8478720 | tf_op jit(solution)/shard_map/reduce_scatter | solution.py:88
  295.0 22.6 %collective-permute-start.33 = (bf16[64,2304]{1,0:T(8,128)(2,1)S(1)}, bf16[64,2304]{1,0:T(8,128)(2,1)}, u32[]{:S(2)}, u32[]{:S(2)}) collective-permute-start(bf16[64,2304]{1,0:T(8,128)(2,1)S(1)} %get-tuple-element.65), channel_id=1, source_target_pairs={{0,4},{4,0},{16,20},{20,16},{1,5},{5,1},{17,21},{21,17},{2,6},{6,2... | collective-permute-start | bytes 884744 | tf_op jit(solution)/shard_map/ppermute | solution.py:36
  387.2 186.7 %reduce-scatter.7.cloned.1.call-start = ((), (), s32[]{:S(2)}) async-start(), calls=%async_computation.9 | async-start | bytes 16957440 | tf_op jit(solution)/shard_map/reduce_scatter | solution.py:88
  442.1 213.0 %reduce-scatter.9.cloned.1.call-start = ((), (), s32[]{:S(2)}) async-start(), calls=%async_computation.10 | async-start | bytes 10321920 | tf_op jit(solution)/shard_map/reduce_scatter | solution.py:88
  538.6 226.0 %reduce-scatter.11.cloned.1.call-start = ((), (), s32[]{:S(2)}) async-start(), calls=%async_computation.11 | async-start | bytes 3317760 | tf_op jit(solution)/shard_map/reduce_scatter | solution.py:88
  573.8 131.3 %collective-permute-start.70 = (bf16[184,2304]{1,0:T(8,128)(2,1)}, bf16[184,2304]{1,0:T(8,128)(2,1)}, u32[]{:S(2)}, u32[]{:S(2)}) collective-permute-start(bf16[184,2304]{1,0:T(8,128)(2,1)} %get-tuple-element.85), channel_id=1, source_target_pairs={{0,8},{8,0},{1,9},{9,1},{2,10},{10,2},{3,11},{11,3},{4,12},{12,4},... | collective-permute-start | bytes 2543624 | tf_op jit(solution)/shard_map/ppermute | solution.py:97
  597.3 101.7 %collective-permute-start.66 = (bf16[288,2944]{1,0:T(8,128)(2,1)}, bf16[288,2944]{1,0:T(8,128)(2,1)}, u32[]{:S(2)}, u32[]{:S(2)}) collective-permute-start(bf16[288,2944]{1,0:T(8,128)(2,1)} %get-tuple-element.79), channel_id=1, source_target_pairs={{0,8},{8,0},{1,9},{9,1},{2,10},{10,2},{3,11},{11,3},{4,12},{12,4},... | collective-permute-start | bytes 5087240 | tf_op jit(solution)/shard_map/ppermute | solution.py:97
  601.3 37.5 %collective-permute-start.55 = (bf16[64,2304]{1,0:T(8,128)(2,1)}, bf16[64,2304]{1,0:T(8,128)(2,1)}, u32[]{:S(2)}, u32[]{:S(2)}) collective-permute-start(bf16[64,2304]{1,0:T(8,128)(2,1)} %get-tuple-element.98), channel_id=1, source_target_pairs={{0,4},{4,0},{16,20},{20,16},{1,5},{5,1},{17,21},{21,17},{2,6},{6,2... | collective-permute-start | bytes 884744 | tf_op jit(solution)/shard_map/ppermute | solution.py:36
  606.0 36.0 %collective-permute-start.56 = (bf16[64,2304]{1,0:T(8,128)(2,1)}, bf16[64,2304]{1,0:T(8,128)(2,1)}, u32[]{:S(2)}, u32[]{:S(2)}) collective-permute-start(bf16[64,2304]{1,0:T(8,128)(2,1)} %get-tuple-element.97), channel_id=1, source_target_pairs={{0,20},{4,16},{16,4},{20,0},{1,21},{5,17},{17,5},{21,1},{2,22},{6,... | collective-permute-start | bytes 884744 | tf_op jit(solution)/shard_map/ppermute | solution.py:36
  657.3 87.4 %collective-permute-start.60 = (bf16[288,1792]{1,0:T(8,128)(2,1)}, bf16[288,1792]{1,0:T(8,128)(2,1)}, u32[]{:S(2)}, u32[]{:S(2)}) collective-permute-start(bf16[288,1792]{1,0:T(8,128)(2,1)} %constant_dynamic-slice_fusion.6), channel_id=1, source_target_pairs={{0,8},{8,0},{1,9},{9,1},{2,10},{10,2},{3,11},{11,3},{4,12},{12,4},... | collective-permute-start | bytes 3096584 | tf_op jit(solution)/shard_map/ppermute | solution.py:97
  701.6 21.2 %collective-permute-start.67 = (bf16[72,2944]{1,0:T(8,128)(2,1)S(1)}, bf16[72,2944]{1,0:T(8,128)(2,1)S(1)}, u32[]{:S(2)}, u32[]{:S(2)}) collective-permute-start(bf16[72,2944]{1,0:T(8,128)(2,1)S(1)} %get-tuple-element.91), channel_id=1, source_target_pairs={{0,4},{4,0},{16,20},{20,16},{1,5},{5,1},{17,21},{21,17},{2,6},{6,2... | collective-permute-start | bytes 1271816 | tf_op jit(solution)/shard_map/ppermute | solution.py:36
  701.7 21.1 %collective-permute-start.68 = (bf16[72,2944]{1,0:T(8,128)(2,1)S(1)}, bf16[72,2944]{1,0:T(8,128)(2,1)S(1)}, u32[]{:S(2)}, u32[]{:S(2)}) collective-permute-start(bf16[72,2944]{1,0:T(8,128)(2,1)S(1)} %get-tuple-element.90), channel_id=1, source_target_pairs={{0,16},{4,20},{16,0},{20,4},{1,17},{5,21},{17,1},{21,5},{2,18},{6,... | collective-permute-start | bytes 1271816 | tf_op jit(solution)/shard_map/ppermute | solution.py:36
  703.2 29.0 %collective-permute-start.69 = (bf16[72,2944]{1,0:T(8,128)(2,1)S(1)}, bf16[72,2944]{1,0:T(8,128)(2,1)S(1)}, u32[]{:S(2)}, u32[]{:S(2)}) collective-permute-start(bf16[72,2944]{1,0:T(8,128)(2,1)S(1)} %get-tuple-element.89), channel_id=1, source_target_pairs={{0,20},{4,16},{16,4},{20,0},{1,21},{5,17},{17,5},{21,1},{2,22},{6,... | collective-permute-start | bytes 1271816 | tf_op jit(solution)/shard_map/ppermute | solution.py:36
  (153 other events, 1132.9 us)
Sparse Core Ops, SparseCore 0:
  81.0 57.7 all-gather.4
  140.9 30.4 all-gather.6
  203.9 87.3 all-gather.8
  293.3 49.1 all-gather.10
  387.3 60.7 reduce-scatter.4
  450.5 106.5 reduce-scatter.6
  559.8 70.6 reduce-scatter.8
  633.0 34.7 reduce-scatter.10

commit v4 on v3

--- a/solution.py
+++ b/solution.py
@@ -36,8 +36,11 @@
     return lax.ppermute(block, PLANE, [(p, p ^ flip) for p in range(4)])
 
 
-def plane_gather(block):
-    return jnp.concatenate([block] + [flip_send(block, f) for f in FLIPS[1:]], axis=0)
+def plane_gather(block, *late):
+    got = [flip_send(block, f) for f in FLIPS[1:]]
+    if late:
+        got = [after(g, *late) for g in got]
+    return jnp.concatenate([block] + got, axis=0)
 
 
 def plane_scatter(partial):
@@ -245,7 +248,6 @@
     for s in range(count):
         live = (local_place < lengths[s]).astype(F32)
         grad_y.append(cotangent[s].astype(F32) * live[:, None])
-        branch2.append(plane_gather((BRANCH_SCALE * grad_y[s]).astype(BF16)))
 
     pick = (
         lax.broadcasted_iota(jnp.int32, (8, spare), 0)
@@ -287,10 +289,12 @@
         mids.append(mid)
 
     factor_two = [norm_factor(v) for v in mids]
-    normed_ffn = [
-        plane_gather(to_line((v * f * gain_two).astype(BF16), rows))
-        for v, f in zip(mids, factor_two)
+    own_ffn = [
+        to_line((v * f * gain_two).astype(BF16), rows) for v, f in zip(mids, factor_two)
     ]
+    normed_ffn = [plane_gather(v) for v in own_ffn]
+    for s in range(count):
+        branch2.append(plane_gather((BRANCH_SCALE * grad_y[s]).astype(BF16), *own_ffn))
     mixes = []
     acts = []
     for s in range(count):
@@ -313,8 +317,12 @@
         grad_boths.append(jnp.concatenate([grad_gate.astype(BF16), grad_up.astype(BF16)], axis=1))
     norm_terms = [dot(g, w_gu, NT).astype(BF16) for g in grad_boths]
     all_ffn = after(jnp.concatenate(normed_ffn, axis=0), *norm_terms)
-    gu_terms = dot(all_ffn, jnp.concatenate(grad_boths, axis=0), TN).astype(BF16)
-    gu_part = line_scatter(gu_terms)
+    all_boths = jnp.concatenate(grad_boths, axis=0)
+    cut = -(-hidden // 128) * 128
+    one_terms = dot(all_ffn, all_boths[:, :cut], TN).astype(BF16)
+    one_part = line_scatter(one_terms)
+    two_terms = dot(after(all_ffn, one_terms), all_boths[:, cut:], TN).astype(BF16)
+    two_part = line_scatter(two_terms)
 
     grad_mids = []
     branch1 = []
@@ -329,7 +337,7 @@
 
     outputs = []
     for s in range(count):
-        terms = dot(after(mixes[s], gu_terms, *own_branch1), w_down)
+        terms = dot(after(mixes[s], two_terms, *own_branch1), w_down)
         outputs.append((mids[s] + BRANCH_SCALE * plane_scatter(terms)).astype(BF16))
 
     grad_qkv = []
@@ -357,7 +365,7 @@
         jnp.concatenate(normed, axis=0), jnp.concatenate(grad_qkv, axis=0), TN
     ).astype(BF16)
     qkv_part = line_scatter(qkv_terms)
-    all_attended = after(jnp.concatenate([k[4] for k in kept], axis=0), qkv_terms, gu_part)
+    all_attended = after(jnp.concatenate([k[4] for k in kept], axis=0), qkv_terms, two_part)
     out_terms = dot(all_attended, jnp.concatenate(branch1, axis=0), TN).astype(BF16)
     out_part = line_scatter(out_terms)
     own = out_part.shape[0] // halves
@@ -374,7 +382,6 @@
     else:
         out_grad = lax.ppermute(half_scatter(out_part), HLXC, [(b, a) for a, b in head_order(0)])
     all_in_terms = [dot(after(g, out_terms), w_qkv, NT).astype(BF16) for g in grad_qkv]
-    gu_raw = column_grad(gu_part, rows, *all_in_terms)
     qkv_raw = column_grad(qkv_part, rows)
     factor_one = [norm_factor(v) for v in x_float]
     for s in range(count):
@@ -383,6 +390,11 @@
         input_grads.append(
             (grad_mids[s] + norm_back(x_float[s], factor_one[s], grad_norm)).astype(BF16)
         )
+
+    gu_raw = jnp.concatenate(
+        [column_grad(one_part, rows, qkv_terms), column_grad(two_part, rows, *input_grads)],
+        axis=2,
+    )
 
     gate_grad, up_grad = lax.optimization_barrier(
         (join_units(gu_raw[:, :, :hidden]), join_units(gu_raw[:, :, hidden:]))

time: 799 us -> 817 us (1.023)
  waiting for transfers between devices: 335 us -> 354 us
  matrix products: 129 us -> 140 us
    ppermute x3 -> x4, waiting for transfers between devices: 38.4 us -> 72.4 us  [half_scatter(): other = lax.ppermute(other, 'h', [(0, 1), (1, 0)])]
    dot_general x21 -> x22, matrix products: 119 us -> 128 us  [dot(): lax.dot_general(left, right, (contract, ((), ())), preferred_element_type...]
    ppermute x60 -> x63, waiting for transfers between devices: 162 us -> 154 us  [flip_send(): return lax.ppermute(block, PLANE, [(p, p ^ flip) for p in range(4)])]
    unnamed x224 -> x214, local copies, waits for them, and re-layouts: 42 us -> 44 us
    ppermute x60 -> x63, starting transfers between devices: 70 us -> 70.6 us  [flip_send(): return lax.ppermute(block, PLANE, [(p, p ^ flip) for p in range(4)])]
  transfers between devices with their start and end apart: 79 -> 84, of which waited for: 36 -> 41; matrix products, arithmetic and copies ran while one was open for 40% -> 38% of each run, Pallas kernels for 0% -> 0%
where the time goes in v4:
time: 817 us; the launch traced here: 811 us
  waiting for transfers between devices  354 us (43%)
  local copies, waits for them, and re-layouts  150 us (18%)
  matrix products  140 us (17%)
  starting transfers between devices  88.6 us (11%)
  other arithmetic  62.5 us (8%)
  between operations  16.1 us (2%)
    ppermute x63, waiting for transfers between devices, flip_send(): return lax.ppermute(block, PLANE, [(p, p ^ flip) for p in range(4)])  154 us
    dot_general x22, matrix products, dot(): lax.dot_general(left, right, (contract, ((), ())), preferred_element_type...  128 us
    ppermute x2, waiting for transfers between devices, half_gather(): other = lax.ppermute(block, 'h', [(0, 1), (1, 0)])  118 us
    ppermute x4, waiting for transfers between devices, half_scatter(): other = lax.ppermute(other, 'h', [(0, 1), (1, 0)])  72.4 us
    ppermute x63, starting transfers between devices, flip_send(): return lax.ppermute(block, PLANE, [(p, p ^ flip) for p in range(4)])  70.6 us
    unnamed x214, local copies, waits for them, and re-layouts  44 us
  transfers between devices with their start and end apart: 84, of which 41 were waited for; matrix products, arithmetic and copies ran while one was open for 38% of the time, Pallas kernels for 0%

profile of v4, /device:TPU:0, one launch (start us, length us, event | category | flops | bytes accessed | tf_op | source)
XLA Modules:
  0.0 810.9 jit_solution(16681435964432400739)
XLA Ops:
  25.6 6.1 collective-permute-done.8
  34.9 43.8 %collective-permute-done.10 = bf16[288,1792]{1,0:T(8,128)(2,1)S(1)} collective-permute-done((bf16[288,1792]{1,0:T(8,128)(2,1)S(1)}, bf16[288,1792]{1,0:T(8,128)(2,1)S(1)}, u32[]{:S(2)}, u32[]{:S(2)}) %collective-permute-start.10) | collective-permute-done | bytes 1032224 | tf_op jit(solution)/shard_map/ppermute | solution.py:85
  107.9 7.8 collective-permute-done.5
  115.7 7.8 collective-permute-done.3
  126.9 74.3 %collective-permute-done.6 = bf16[288,2944]{1,0:T(8,128)(2,1)S(1)} collective-permute-done((bf16[288,2944]{1,0:T(8,128)(2,1)S(1)}, bf16[288,2944]{1,0:T(8,128)(2,1)S(1)}, u32[]{:S(2)}, u32[]{:S(2)}) %collective-permute-start.6) | collective-permute-done | bytes 1695776 | tf_op jit(solution)/shard_map/ppermute | solution.py:85
  228.7 12.4 %collective-permute-done.1 = bf16[64,2304]{1,0:T(8,128)(2,1)S(1)} collective-permute-done((bf16[64,2304]{1,0:T(8,128)(2,1)S(1)}, bf16[64,2304]{1,0:T(8,128)(2,1)S(1)}, u32[]{:S(2)}, u32[]{:S(2)}) %collective-permute-start.1) | collective-permute-done | bytes 294944 | tf_op jit(solution)/shard_map/ppermute | solution.py:36
  241.0 6.2 collective-permute-done.2
  252.0 8.0 fusion.2
  265.0 7.9 fusion.4
  309.9 9.6 %collective-permute-done.14 = bf16[64,2304]{1,0:T(8,128)(2,1)S(1)} collective-permute-done((bf16[64,2304]{1,0:T(8,128)(2,1)}, bf16[64,2304]{1,0:T(8,128)(2,1)S(1)}, u32[]{:S(2)}, u32[]{:S(2)}) %collective-permute-start.14) | collective-permute-done | bytes 294944 | tf_op jit(solution)/shard_map/ppermute | solution.py:36
  349.2 6.7 collective-permute-done.34
  372.8 7.7 fusion.30
  391.3 6.1 convolution_convert_fusion.3
  413.2 6.5 multiply_convert_fusion.3
  424.6 8.9 %convolution_convert_fusion.8 = bf16[256,2304]{1,0:T(8,128)(2,1)} fusion(bf16[256,2944]{1,0:T(8,128)(2,1)S(1)} %pad_maximum_fusion.2, bf16[2304,2944]{1,0:T(8,128)(2,1)} %all-gather.9.cloned.1.call-done), kind=kOutput, calls=%fused_computation.14 | convolution fusion | flops 3473473536 | bytes 16252928 | tf_op jit(solution)/shard_map/dot_general | solution.py:28
  433.5 7.3 convolution_convert_fusion.7
  440.9 8.1 convolution_convert_fusion.2
  449.0 8.6 %convolution_convert_fusion.1 = bf16[2304,1408]{1,0:T(8,128)(2,1)} fusion(bf16[512,2304]{1,0:T(8,128)(2,1)} %constant_dynamic-update-slice_fusion, bf16[256,2944]{1,0:T(8,128)(2,1)} %copy-done.27, bf16[256,2944]{1,0:T(8,128)(2,1)} %copy-done.26), kind=kOutput, calls=%fused_computation.3 | convolution fusion | flops 3328016384 | bytes 11862016 | tf_op jit(solution)/shard_map/dot_general | solution.py:28
  547.2 6.7 convolution_convert_fusion
  568.6 6.4 fusion.172
  586.6 13.6 %collective-permute-done.47 = bf16[64,2304]{1,0:T(8,128)(2,1)} collective-permute-done((bf16[64,2304]{1,0:T(8,128)(2,1)}, bf16[64,2304]{1,0:T(8,128)(2,1)}, u32[]{:S(2)}, u32[]{:S(2)}) %collective-permute-start.47) | collective-permute-done | bytes 294944 | tf_op jit(solution)/shard_map/ppermute | solution.py:36
  650.5 7.9 collective-permute-done.70
  673.0 23.4 %collective-permute-done.66 = bf16[288,1536]{1,0:T(8,128)(2,1)S(1)} collective-permute-done((bf16[288,1536]{1,0:T(8,128)(2,1)S(1)}, bf16[288,1536]{1,0:T(8,128)(2,1)S(1)}, u32[]{:S(2)}, u32[]{:S(2)}) %collective-permute-start.66) | collective-permute-done | bytes 884768 | tf_op jit(solution)/shard_map/ppermute | solution.py:100
  738.2 41.1 %collective-permute-done.60 = bf16[288,1792]{1,0:T(8,128)(2,1)S(1)} collective-permute-done((bf16[288,1792]{1,0:T(8,128)(2,1)S(1)}, bf16[288,1792]{1,0:T(8,128)(2,1)S(1)}, u32[]{:S(2)}, u32[]{:S(2)}) %collective-permute-start.60) | collective-permute-done | bytes 1032224 | tf_op jit(solution)/shard_map/ppermute | solution.py:100
  (606 shorter events, 451.9 us)
Async XLA Ops:
  7.2 240.8 %all-gather.5.cloned.1.call-start = ((), (), s32[]{:S(2)}) async-start(), calls=%async_computation.5 | async-start | bytes 10321920 | tf_op jit(solution)/shard_map/all_gather | solution.py:72
  32.3 46.5 %collective-permute-start.10 = (bf16[288,1792]{1,0:T(8,128)(2,1)S(1)}, bf16[288,1792]{1,0:T(8,128)(2,1)S(1)}, u32[]{:S(2)}, u32[]{:S(2)}) collective-permute-start(bf16[288,1792]{1,0:T(8,128)(2,1)S(1)} %bitcast.308), channel_id=1, source_target_pairs={{0,8},{8,0},{1,9},{9,1},{2,10},{10,2},{3,11},{11,3},{4,12},{12,4},... | collective-permute-start | bytes 3096584 | tf_op jit(solution)/shard_map/ppermute | solution.py:85
  80.9 203.0 %all-gather.7.cloned.1.call-start = ((), (), s32[]{:S(2)}) async-start(), calls=%async_computation.6 | async-start | bytes 3317760 | tf_op jit(solution)/shard_map/all_gather | solution.py:72
  80.9 24.6 %collective-permute-start.12 = (bf16[72,2304]{1,0:T(8,128)(2,1)}, bf16[72,2304]{1,0:T(8,128)(2,1)}, u32[]{:S(2)}, u32[]{:S(2)}) collective-permute-start(bf16[72,2304]{1,0:T(8,128)(2,1)} %param.17), channel_id=1, source_target_pairs={{0,0},{2,1},{4,2},{6,3},{8,4},{10,5},{12,6},{14,7},{1,8},{3,9},{5,... | collective-permute-start | bytes 995336 | tf_op jit(solution)/shard_map/ppermute | solution.py:219
  85.4 20.2 %collective-permute-start.13 = (bf16[72,2304]{1,0:T(8,128)(2,1)}, bf16[72,2304]{1,0:T(8,128)(2,1)}, u32[]{:S(2)}, u32[]{:S(2)}) collective-permute-start(bf16[72,2304]{1,0:T(8,128)(2,1)} %param.17), channel_id=1, source_target_pairs={{0,8},{2,9},{4,10},{6,11},{8,12},{10,13},{12,14},{14,15},{1,0},{3,... | collective-permute-start | bytes 995336 | tf_op jit(solution)/shard_map/ppermute | solution.py:219
  102.9 20.5 %collective-permute-start.3 = (bf16[72,2944]{1,0:T(8,128)(2,1)S(1)}, bf16[72,2944]{1,0:T(8,128)(2,1)S(1)}, u32[]{:S(2)}, u32[]{:S(2)}) collective-permute-start(bf16[72,2944]{1,0:T(8,128)(2,1)S(1)} %get-tuple-element.105), channel_id=1, source_target_pairs={{0,4},{4,0},{16,20},{20,16},{1,5},{5,1},{17,21},{21,17},{2,6},{6,2... | collective-permute-start | bytes 1271816 | tf_op jit(solution)/shard_map/ppermute | solution.py:36
  107.9 264.9 %all-gather.9.cloned.1.call-start = ((), (), s32[]{:S(2)}) async-start(), calls=%async_computation.7 | async-start | bytes 16957440 | tf_op jit(solution)/shard_map/all_gather | solution.py:72
  125.1 76.1 %collective-permute-start.6 = (bf16[288,2944]{1,0:T(8,128)(2,1)S(1)}, bf16[288,2944]{1,0:T(8,128)(2,1)S(1)}, u32[]{:S(2)}, u32[]{:S(2)}) collective-permute-start(bf16[288,2944]{1,0:T(8,128)(2,1)S(1)} %bitcast.300), channel_id=1, source_target_pairs={{0,8},{8,0},{1,9},{9,1},{2,10},{10,2},{3,11},{11,3},{4,12},{12,4},... | collective-permute-start | bytes 5087240 | tf_op jit(solution)/shard_map/ppermute | solution.py:85
  203.5 209.7 %all-gather.11.cloned.1.call-start = ((), (), s32[]{:S(2)}) async-start(), calls=%async_computation.8 | async-start | bytes 8478720 | tf_op jit(solution)/shard_map/all_gather | solution.py:72
  223.9 23.3 %collective-permute-start.2 = (bf16[64,2304]{1,0:T(8,128)(2,1)S(1)}, bf16[64,2304]{1,0:T(8,128)(2,1)S(1)}, u32[]{:S(2)}, u32[]{:S(2)}) collective-permute-start(bf16[64,2304]{1,0:T(8,128)(2,1)S(1)} %reshape.448), channel_id=1, source_target_pairs={{0,20},{4,16},{16,4},{20,0},{1,21},{5,17},{17,5},{21,1},{2,22},{6,... | collective-permute-start | bytes 884744 | tf_op jit(solution)/shard_map/ppermute | solution.py:36
  226.5 70.0 %collective-permute-start.35 = (bf16[184,2304]{1,0:T(8,128)(2,1)}, bf16[184,2304]{1,0:T(8,128)(2,1)}, u32[]{:S(2)}, u32[]{:S(2)}) collective-permute-start(bf16[184,2304]{1,0:T(8,128)(2,1)} %pad.20), channel_id=1, source_target_pairs={{0,8},{8,0},{1,9},{9,1},{2,10},{10,2},{3,11},{11,3},{4,12},{12,4},... | collective-permute-start | bytes 2543624 | tf_op jit(solution)/shard_map/ppermute | solution.py:234
  300.2 224.7 %reduce-scatter.6.cloned.1.call-start = ((), (), s32[]{:S(2)}) async-start(), calls=%async_computation.9 | async-start | bytes 8478720 | tf_op jit(solution)/shard_map/reduce_scatter | solution.py:91
  309.3 29.7 %collective-permute-start.29 = (bf16[64,2304]{1,0:T(8,128)(2,1)S(1)}, bf16[64,2304]{1,0:T(8,128)(2,1)}, u32[]{:S(2)}, u32[]{:S(2)}) collective-permute-start(bf16[64,2304]{1,0:T(8,128)(2,1)S(1)} %get-tuple-element.83), channel_id=1, source_target_pairs={{0,16},{4,20},{16,0},{20,4},{1,17},{5,21},{17,1},{21,5},{2,18},{6,... | collective-permute-start | bytes 884744 | tf_op jit(solution)/shard_map/ppermute | solution.py:36
  309.4 29.6 %collective-permute-start.30 = (bf16[64,2304]{1,0:T(8,128)(2,1)S(1)}, bf16[64,2304]{1,0:T(8,128)(2,1)}, u32[]{:S(2)}, u32[]{:S(2)}) collective-permute-start(bf16[64,2304]{1,0:T(8,128)(2,1)S(1)} %get-tuple-element.83), channel_id=1, source_target_pairs={{0,4},{4,0},{16,20},{20,16},{1,5},{5,1},{17,21},{21,17},{2,6},{6,2... | collective-permute-start | bytes 884744 | tf_op jit(solution)/shard_map/ppermute | solution.py:36
  360.8 21.4 %collective-permute-start.26 = (bf16[64,2304]{1,0:T(8,128)(2,1)}, bf16[64,2304]{1,0:T(8,128)(2,1)}, u32[]{:S(2)}, u32[]{:S(2)}) collective-permute-start(bf16[64,2304]{1,0:T(8,128)(2,1)} %reshape.468), channel_id=1, source_target_pairs={{0,16},{4,20},{16,0},{20,4},{1,17},{5,21},{17,1},{21,5},{2,18},{6,... | collective-permute-start | bytes 884744 | tf_op jit(solution)/shard_map/ppermute | solution.py:36
  397.5 156.4 %reduce-scatter.8.cloned.1.call-start = ((), (), s32[]{:S(2)}) async-start(), calls=%async_computation.10 | async-start | bytes 8110080 | tf_op jit(solution)/shard_map/reduce_scatter | solution.py:91
  457.6 206.0 %reduce-scatter.14.cloned.1.call-start = ((), (), s32[]{:S(2)}) async-start(), calls=%async_computation.13 | async-start | bytes 8847360 | tf_op jit(solution)/shard_map/reduce_scatter | solution.py:91
  458.4 261.3 %reduce-scatter.12.cloned.1.call-start = ((), (), s32[]{:S(2)}) async-start(), calls=%async_computation.12 | async-start | bytes 3317760 | tf_op jit(solution)/shard_map/reduce_scatter | solution.py:91
  558.9 164.3 %reduce-scatter.10.cloned.1.call-start = ((), (), s32[]{:S(2)}) async-start(), calls=%async_computation.11 | async-start | bytes 10321920 | tf_op jit(solution)/shard_map/reduce_scatter | solution.py:91
  578.0 22.2 %collective-permute-start.47 = (bf16[64,2304]{1,0:T(8,128)(2,1)}, bf16[64,2304]{1,0:T(8,128)(2,1)}, u32[]{:S(2)}, u32[]{:S(2)}) collective-permute-start(bf16[64,2304]{1,0:T(8,128)(2,1)} %get-tuple-element.118), channel_id=1, source_target_pairs={{0,20},{4,16},{16,4},{20,0},{1,21},{5,17},{17,5},{21,1},{2,22},{6,... | collective-permute-start | bytes 884744 | tf_op jit(solution)/shard_map/ppermute | solution.py:36
  603.9 182.4 %collective-permute-start.74 = (bf16[184,2304]{1,0:T(8,128)(2,1)}, bf16[184,2304]{1,0:T(8,128)(2,1)}, u32[]{:S(2)}, u32[]{:S(2)}) collective-permute-start(bf16[184,2304]{1,0:T(8,128)(2,1)} %get-tuple-element.101), channel_id=1, source_target_pairs={{0,8},{8,0},{1,9},{9,1},{2,10},{10,2},{3,11},{11,3},{4,12},{12,4},... | collective-permute-start | bytes 2543624 | tf_op jit(solution)/shard_map/ppermute | solution.py:100
  629.0 29.3 %collective-permute-start.70 = (bf16[288,1408]{1,0:T(8,128)(2,1)}, bf16[288,1408]{1,0:T(8,128)(2,1)}, u32[]{:S(2)}, u32[]{:S(2)}) collective-permute-start(bf16[288,1408]{1,0:T(8,128)(2,1)} %get-tuple-element.107), channel_id=1, source_target_pairs={{0,8},{8,0},{1,9},{9,1},{2,10},{10,2},{3,11},{11,3},{4,12},{12,4},... | collective-permute-start | bytes 2433032 | tf_op jit(solution)/shard_map/ppermute | solution.py:100
  665.2 31.3 %collective-permute-start.66 = (bf16[288,1536]{1,0:T(8,128)(2,1)S(1)}, bf16[288,1536]{1,0:T(8,128)(2,1)S(1)}, u32[]{:S(2)}, u32[]{:S(2)}) collective-permute-start(bf16[288,1536]{1,0:T(8,128)(2,1)S(1)} %get-tuple-element.95), channel_id=1, source_target_pairs={{0,8},{8,0},{1,9},{9,1},{2,10},{10,2},{3,11},{11,3},{4,12},{12,4},... | collective-permute-start | bytes 2654216 | tf_op jit(solution)/shard_map/ppermute | solution.py:100
  724.6 54.6 %collective-permute-start.60 = (bf16[288,1792]{1,0:T(8,128)(2,1)S(1)}, bf16[288,1792]{1,0:T(8,128)(2,1)S(1)}, u32[]{:S(2)}, u32[]{:S(2)}) collective-permute-start(bf16[288,1792]{1,0:T(8,128)(2,1)S(1)} %constant_dynamic-slice_fusion.8), channel_id=1, source_target_pairs={{0,8},{8,0},{1,9},{9,1},{2,10},{10,2},{3,11},{11,3},{4,12},{12,4},... | collective-permute-start | bytes 3096584 | tf_op jit(solution)/shard_map/ppermute | solution.py:100
  (153 other events, 1232.1 us)
Sparse Core Ops, SparseCore 0:
  81.0 57.8 all-gather.4
  141.0 30.3 all-gather.6
  203.6 87.3 all-gather.8
  300.3 47.2 all-gather.10
  397.6 60.2 reduce-scatter.5
  460.4 60.1 reduce-scatter.7
  523.1 64.2 reduce-scatter.13
  589.9 34.7 reduce-scatter.11
  627.3 70.5 reduce-scatter.9

commit v5 on v4

--- a/solution.py
+++ b/solution.py
@@ -40,7 +40,7 @@
     got = [flip_send(block, f) for f in FLIPS[1:]]
     if late:
         got = [after(g, *late) for g in got]
-    return jnp.concatenate([block] + got, axis=0)
+    return lax.optimization_barrier(jnp.concatenate([block] + got, axis=0))
 
 
 def plane_scatter(partial):
@@ -262,13 +262,14 @@
     mids = []
     normed = []
     for s in range(count):
-        whole = after(gathered[s], gu_block).astype(F32)
+        whole = gathered[s].astype(F32)
         normed.append((whole * norm_factor(whole) * gain_one_line).astype(BF16))
         visible = (place[None, :] <= place[:, None])[None] & (
             place[None, None, :] < lengths_two[s][:, None, None]
         )
         visible = visible[:, None, :, :]
-        lin = dot(normed[s], w_qkv)[:, : 3 * part].reshape(2, 2 * tokens, 3, heads, HEAD_DIM)
+        lin = after(dot(normed[s], w_qkv), gu_block)
+        lin = lin[:, : 3 * part].reshape(2, 2 * tokens, 3, heads, HEAD_DIM)
         queries = rotate(lin[:, :, 0], cosine, sine).astype(BF16)
         keys = rotate(lin[:, :, 1], cosine, sine).astype(BF16)
         values = lin[:, :, 2].astype(BF16)
@@ -284,7 +285,9 @@
             else:
                 down_block = half_gather(down_own)
             w_down = line_gather(down_block)
-        mid = x_float[s] + BRANCH_SCALE * plane_scatter(dot(attended, w_out))
+        out_sum = dot(attended, w_out)
+        out_sum = plane_scatter(out_sum)
+        mid = x_float[s] + BRANCH_SCALE * out_sum
         kept.append((queries, keys, values, probs, attended))
         mids.append(mid)
 
@@ -318,11 +321,8 @@
     norm_terms = [dot(g, w_gu, NT).astype(BF16) for g in grad_boths]
     all_ffn = after(jnp.concatenate(normed_ffn, axis=0), *norm_terms)
     all_boths = jnp.concatenate(grad_boths, axis=0)
-    cut = -(-hidden // 128) * 128
-    one_terms = dot(all_ffn, all_boths[:, :cut], TN).astype(BF16)
-    one_part = line_scatter(one_terms)
-    two_terms = dot(after(all_ffn, one_terms), all_boths[:, cut:], TN).astype(BF16)
-    two_part = line_scatter(two_terms)
+    gu_terms = dot(all_ffn, all_boths, TN).astype(BF16)
+    gu_part = line_scatter(gu_terms)
 
     grad_mids = []
     branch1 = []
@@ -337,7 +337,7 @@
 
     outputs = []
     for s in range(count):
-        terms = dot(after(mixes[s], two_terms, *own_branch1), w_down)
+        terms = dot(after(mixes[s], gu_terms, *own_branch1), w_down)
         outputs.append((mids[s] + BRANCH_SCALE * plane_scatter(terms)).astype(BF16))
 
     grad_qkv = []
@@ -361,13 +361,30 @@
             axis=2,
         ).reshape(4 * tokens, 3 * part)
         grad_qkv.append(jnp.pad(grads, ((0, 0), (0, spare))))
-    qkv_terms = dot(
-        jnp.concatenate(normed, axis=0), jnp.concatenate(grad_qkv, axis=0), TN
-    ).astype(BF16)
-    qkv_part = line_scatter(qkv_terms)
-    all_attended = after(jnp.concatenate([k[4] for k in kept], axis=0), qkv_terms, two_part)
+    all_normed = jnp.concatenate(normed, axis=0)
+    all_grads = jnp.concatenate(grad_qkv, axis=0)
+    v_terms = dot(all_normed, all_grads[:, 2 * part :], TN).astype(BF16)
+    v_part = line_scatter(v_terms)
+    qk_terms = dot(after(all_normed, v_terms), all_grads[:, : 2 * part], TN).astype(BF16)
+    qk_part = line_scatter(qk_terms)
+    all_attended = after(jnp.concatenate([k[4] for k in kept], axis=0), qk_terms)
     out_terms = dot(all_attended, jnp.concatenate(branch1, axis=0), TN).astype(BF16)
     out_part = line_scatter(out_terms)
+    all_in_terms = [dot(after(g, out_terms), w_qkv, NT).astype(BF16) for g in grad_qkv]
+    factor_one = [norm_factor(v) for v in x_float]
+    for s in range(count):
+        grad_norm = plane_scatter(all_in_terms[s])
+        grad_norm = from_line(grad_norm, rows) * gain_one
+        input_grads.append(
+            (grad_mids[s] + norm_back(x_float[s], factor_one[s], grad_norm)).astype(BF16)
+        )
+
+    qk_part = after(qk_part, *input_grads)
+    gu_raw = after(column_grad(gu_part, rows, *input_grads), qk_part)
+    gate_grad, up_grad = lax.optimization_barrier(
+        (join_units(gu_raw[:, :, :hidden]), join_units(gu_raw[:, :, hidden:]))
+    )
+    out_part = after(out_part, gate_grad, up_grad)
     own = out_part.shape[0] // halves
     if halves == 2:
         h = lax.axis_index("h")
@@ -381,24 +398,10 @@
         )
     else:
         out_grad = lax.ppermute(half_scatter(out_part), HLXC, [(b, a) for a, b in head_order(0)])
-    all_in_terms = [dot(after(g, out_terms), w_qkv, NT).astype(BF16) for g in grad_qkv]
-    qkv_raw = column_grad(qkv_part, rows)
-    factor_one = [norm_factor(v) for v in x_float]
-    for s in range(count):
-        grad_norm = plane_scatter(all_in_terms[s])
-        grad_norm = from_line(grad_norm, rows) * gain_one
-        input_grads.append(
-            (grad_mids[s] + norm_back(x_float[s], factor_one[s], grad_norm)).astype(BF16)
-        )
-
-    gu_raw = jnp.concatenate(
-        [column_grad(one_part, rows, qkv_terms), column_grad(two_part, rows, *input_grads)],
-        axis=2,
-    )
-
-    gate_grad, up_grad = lax.optimization_barrier(
-        (join_units(gu_raw[:, :, :hidden]), join_units(gu_raw[:, :, hidden:]))
-    )
+    v_raw = column_grad(v_part, rows, qk_part)
+    qk_raw = column_grad(qk_part, rows, gate_grad, up_grad)
+    qkv_raw = jnp.concatenate([qk_raw, v_raw], axis=2)
+
     gate_grad, up_grad = gate_grad.astype(F32), up_grad.astype(F32)
     ffn_gain_grad = jnp.sum(
         gate_grad * gate_weight.astype(F32) + up_grad * up_weight.astype(F32), axis=1
@@ -420,7 +423,7 @@
         out_grad,
         gate_grad,
         up_grad,
-        half_scatter(down_part, qkv_part)[:units],
+        half_scatter(down_part, v_part)[:units],
         attn_gain_grad,
         ffn_gain_grad,
     )

time: 817 us -> 832 us (1.018)
  waiting for transfers between devices: 354 us -> 409 us
  local copies, waits for them, and re-layouts: 150 us -> 121 us
  matrix products: 140 us -> 127 us
    reduce_scatter x5, waiting for transfers between devices: 0.01 us -> 79.8 us  [line_scatter(): return lax.psum_scatter(partial, LINE, scatter_dimension=0, tiled=True)]
    ppermute x4, waiting for transfers between devices: 72.4 us -> 25.6 us  [half_scatter(): other = lax.ppermute(other, 'h', [(0, 1), (1, 0)])]
    unnamed x214 -> x201, local copies, waits for them, and re-layouts: 44 us -> 22.6 us
    ppermute x63, waiting for transfers between devices: 154 us -> 174 us  [flip_send(): return lax.ppermute(block, PLANE, [(p, p ^ flip) for p in range(4)])]
    dot_general x22, matrix products: 128 us -> 117 us  [dot(): lax.dot_general(left, right, (contract, ((), ())), preferred_element_type...]
    ppermute x63, starting transfers between devices: 70.6 us -> 61.7 us  [flip_send(): return lax.ppermute(block, PLANE, [(p, p ^ flip) for p in range(4)])]
  transfers between devices with their start and end apart: 84 -> 84, of which waited for: 41 -> 43; matrix products, arithmetic and copies ran while one was open for 38% -> 32% of each run, Pallas kernels for 0% -> 0%
where the time goes in v5:
time: 832 us; the launch traced here: 827 us
  waiting for transfers between devices  409 us (49%)
  matrix products  127 us (15%)
  local copies, waits for them, and re-layouts  121 us (15%)
  starting transfers between devices  84.5 us (10%)
  other arithmetic  69 us (8%)
  between operations  16.1 us (2%)
    ppermute x63, waiting for transfers between devices, flip_send(): return lax.ppermute(block, PLANE, [(p, p ^ flip) for p in range(4)])  174 us
    dot_general x22, matrix products, dot(): lax.dot_general(left, right, (contract, ((), ())), preferred_element_type...  117 us
    ppermute x2, waiting for transfers between devices, half_gather(): other = lax.ppermute(block, 'h', [(0, 1), (1, 0)])  116 us
    reduce_scatter x5, waiting for transfers between devices, line_scatter(): return lax.psum_scatter(partial, LINE, scatter_dimension=0, tiled=True)  79.8 us
    ppermute x63, starting transfers between devices, flip_send(): return lax.ppermute(block, PLANE, [(p, p ^ flip) for p in range(4)])  61.7 us
    ppermute x4, waiting for transfers between devices, half_scatter(): other = lax.ppermute(other, 'h', [(0, 1), (1, 0)])  25.6 us
    unnamed x201, local copies, waits for them, and re-layouts  22.6 us
  transfers between devices with their start and end apart: 84, of which 43 were waited for; matrix products, arithmetic and copies ran while one was open for 32% of the time, Pallas kernels for 0%

profile of v5, /device:TPU:0, one launch (start us, length us, event | category | flops | bytes accessed | tf_op | source)
XLA Modules:
  0.0 826.6 jit_solution(11836206143802451752)
XLA Ops:
  23.3 6.1 collective-permute-done.4
  32.6 43.8 %collective-permute-done.6 = bf16[288,1792]{1,0:T(8,128)(2,1)S(1)} collective-permute-done((bf16[288,1792]{1,0:T(8,128)(2,1)S(1)}, bf16[288,1792]{1,0:T(8,128)(2,1)S(1)}, u32[]{:S(2)}, u32[]{:S(2)}) %collective-permute-start.6) | collective-permute-done | bytes 1032224 | tf_op jit(solution)/shard_map/ppermute | solution.py:85
  105.5 7.0 collective-permute-done.7
  112.5 8.8 %collective-permute-done.8 = bf16[72,2944]{1,0:T(8,128)(2,1)S(1)} collective-permute-done((bf16[72,2944]{1,0:T(8,128)(2,1)S(1)}, bf16[72,2944]{1,0:T(8,128)(2,1)S(1)}, u32[]{:S(2)}, u32[]{:S(2)}) %collective-permute-start.8) | collective-permute-done | bytes 423968 | tf_op jit(solution)/shard_map/ppermute | solution.py:36
  124.8 72.4 %collective-permute-done.10 = bf16[288,2944]{1,0:T(8,128)(2,1)S(1)} collective-permute-done((bf16[288,2944]{1,0:T(8,128)(2,1)S(1)}, bf16[288,2944]{1,0:T(8,128)(2,1)S(1)}, u32[]{:S(2)}, u32[]{:S(2)}) %collective-permute-start.10) | collective-permute-done | bytes 1695776 | tf_op jit(solution)/shard_map/ppermute | solution.py:85
  225.0 13.4 %collective-permute-done.1 = bf16[64,2304]{1,0:T(8,128)(2,1)S(1)} collective-permute-done((bf16[64,2304]{1,0:T(8,128)(2,1)S(1)}, bf16[64,2304]{1,0:T(8,128)(2,1)S(1)}, u32[]{:S(2)}, u32[]{:S(2)}) %collective-permute-start.1) | collective-permute-done | bytes 294944 | tf_op jit(solution)/shard_map/ppermute | solution.py:36
  249.0 7.5 fusion.188
  259.5 7.3 fusion.186
  310.5 5.8 collective-permute-done.14
  354.2 6.8 collective-permute-done.19
  371.8 7.6 fusion.187
  389.7 6.2 convolution_convert_fusion.2
  396.0 7.5 multiply_convert_fusion.3
  403.9 8.3 %convolution_convert_fusion.8 = bf16[256,2304]{1,0:T(8,128)(2,1)S(1)} fusion(bf16[256,2944]{1,0:T(8,128)(2,1)S(1)} %pad_maximum_fusion.5, bf16[2304,2944]{1,0:T(8,128)(2,1)} %all-gather.9.cloned.1.call-done), kind=kOutput, calls=%fused_computation.10 | convolution fusion | flops 3473473536 | bytes 16252928 | tf_op jit(solution)/shard_map/dot_general | solution.py:28
  421.7 8.0 convolution_convert_fusion.7
  460.8 6.0 collective-permute-done.51
  466.8 7.2 collective-permute-done.53
  509.9 10.1 %convolution_convert_fusion = bf16[2304,2944]{1,0:T(8,128)(2,1)} fusion(bf16[512,2304]{1,0:T(8,128)(2,1)S(1)} %pad_maximum_fusion, bf16[256,2944]{1,0:T(8,128)(2,1)S(1)} %copy-done.30, bf16[256,2944]{1,0:T(8,128)(2,1)S(1)} %copy-done.28), kind=kOutput, calls=%fused_computation.2 | convolution fusion | flops 6958579712 | bytes 18939904 | tf_op jit(solution)/shard_map/dot_general | solution.py:28
  615.0 33.7 %reduce-scatter.10.cloned.1.call-done = bf16[576,2944]{1,0:T(8,128)(2,1)} async-done(((bf16[2304,2944]{1,0:T(8,128)(2,1)}), bf16[576,2944]{1,0:T(8,128)(2,1)}) %reduce-scatter.10.cloned.1.call-update) | async-done | bytes 3391504 | tf_op jit(solution)/shard_map/reduce_scatter | solution.py:91
  657.0 46.1 %reduce-scatter.8.cloned.1.call-done = bf16[576,1152]{1,0:T(8,128)(2,1)} async-done(((bf16[2304,1152]{1,0:T(8,128)(2,1)}), bf16[576,1152]{1,0:T(8,128)(2,1)}) %reduce-scatter.8.cloned.1.call-update) | async-done | bytes 1327120 | tf_op jit(solution)/shard_map/reduce_scatter | solution.py:91
  717.9 25.6 %collective-permute-done.60 = bf16[288,2944]{1,0:T(8,128)(2,1)} collective-permute-done((bf16[288,2944]{1,0:T(8,128)(2,1)}, bf16[288,2944]{1,0:T(8,128)(2,1)}, u32[]{:S(2)}, u32[]{:S(2)}) %collective-permute-start.60) | collective-permute-done | bytes 1695776 | tf_op jit(solution)/shard_map/ppermute | solution.py:100
  751.3 14.5 %collective-permute-done.61 = bf16[72,2944]{1,0:T(8,128)(2,1)S(1)} collective-permute-done((bf16[72,2944]{1,0:T(8,128)(2,1)S(1)}, bf16[72,2944]{1,0:T(8,128)(2,1)S(1)}, u32[]{:S(2)}, u32[]{:S(2)}) %collective-permute-start.61) | collective-permute-done | bytes 423968 | tf_op jit(solution)/shard_map/ppermute | solution.py:36
  765.8 10.0 %collective-permute-done.63 = bf16[72,2944]{1,0:T(8,128)(2,1)} collective-permute-done((bf16[72,2944]{1,0:T(8,128)(2,1)S(1)}, bf16[72,2944]{1,0:T(8,128)(2,1)}, u32[]{:S(2)}, u32[]{:S(2)}) %collective-permute-start.63) | collective-permute-done | bytes 423968 | tf_op jit(solution)/shard_map/ppermute | solution.py:36
  808.5 9.3 %collective-permute-done.73 = bf16[72,2304]{1,0:T(8,128)(2,1)} collective-permute-done((bf16[72,2304]{1,0:T(8,128)(2,1)}, bf16[72,2304]{1,0:T(8,128)(2,1)}, u32[]{:S(2)}, u32[]{:S(2)}) %collective-permute-start.73) | collective-permute-done | bytes 331808 | tf_op jit(solution)/shard_map/ppermute | solution.py:392
  (597 shorter events, 431.3 us)
Async XLA Ops:
  7.2 238.2 %all-gather.5.cloned.1.call-start = ((), (), s32[]{:S(2)}) async-start(), calls=%async_computation.5 | async-start | bytes 10321920 | tf_op jit(solution)/shard_map/all_gather | solution.py:72
  29.9 46.5 %collective-permute-start.6 = (bf16[288,1792]{1,0:T(8,128)(2,1)S(1)}, bf16[288,1792]{1,0:T(8,128)(2,1)S(1)}, u32[]{:S(2)}, u32[]{:S(2)}) collective-permute-start(bf16[288,1792]{1,0:T(8,128)(2,1)S(1)} %bitcast.303), channel_id=1, source_target_pairs={{0,8},{8,0},{1,9},{9,1},{2,10},{10,2},{3,11},{11,3},{4,12},{12,4},... | collective-permute-start | bytes 3096584 | tf_op jit(solution)/shard_map/ppermute | solution.py:85
  78.6 209.6 %all-gather.7.cloned.1.call-start = ((), (), s32[]{:S(2)}) async-start(), calls=%async_computation.6 | async-start | bytes 3317760 | tf_op jit(solution)/shard_map/all_gather | solution.py:72
  78.6 24.7 %collective-permute-start.12 = (bf16[72,2304]{1,0:T(8,128)(2,1)}, bf16[72,2304]{1,0:T(8,128)(2,1)S(1)}, u32[]{:S(2)}, u32[]{:S(2)}) collective-permute-start(bf16[72,2304]{1,0:T(8,128)(2,1)} %param.17), channel_id=1, source_target_pairs={{0,0},{2,1},{4,2},{6,3},{8,4},{10,5},{12,6},{14,7},{1,8},{3,9},{5,... | collective-permute-start | bytes 995336 | tf_op jit(solution)/shard_map/ppermute | solution.py:219
  80.4 23.0 %collective-permute-start.13 = (bf16[72,2304]{1,0:T(8,128)(2,1)}, bf16[72,2304]{1,0:T(8,128)(2,1)}, u32[]{:S(2)}, u32[]{:S(2)}) collective-permute-start(bf16[72,2304]{1,0:T(8,128)(2,1)} %param.17), channel_id=1, source_target_pairs={{0,8},{2,9},{4,10},{6,11},{8,12},{10,13},{12,14},{14,15},{1,0},{3,... | collective-permute-start | bytes 995336 | tf_op jit(solution)/shard_map/ppermute | solution.py:219
  105.4 266.3 %all-gather.9.cloned.1.call-start = ((), (), s32[]{:S(2)}) async-start(), calls=%async_computation.7 | async-start | bytes 16957440 | tf_op jit(solution)/shard_map/all_gather | solution.py:72
  122.1 75.1 %collective-permute-start.10 = (bf16[288,2944]{1,0:T(8,128)(2,1)S(1)}, bf16[288,2944]{1,0:T(8,128)(2,1)S(1)}, u32[]{:S(2)}, u32[]{:S(2)}) collective-permute-start(bf16[288,2944]{1,0:T(8,128)(2,1)S(1)} %bitcast.296), channel_id=1, source_target_pairs={{0,8},{8,0},{1,9},{9,1},{2,10},{10,2},{3,11},{11,3},{4,12},{12,4},... | collective-permute-start | bytes 5087240 | tf_op jit(solution)/shard_map/ppermute | solution.py:85
  199.6 196.4 %all-gather.11.cloned.1.call-start = ((), (), s32[]{:S(2)}) async-start(), calls=%async_computation.8 | async-start | bytes 8478720 | tf_op jit(solution)/shard_map/all_gather | solution.py:72
  220.3 23.5 %collective-permute-start.2 = (bf16[64,2304]{1,0:T(8,128)(2,1)S(1)}, bf16[64,2304]{1,0:T(8,128)(2,1)S(1)}, u32[]{:S(2)}, u32[]{:S(2)}) collective-permute-start(bf16[64,2304]{1,0:T(8,128)(2,1)S(1)} %reshape.448), channel_id=1, source_target_pairs={{0,20},{4,16},{16,4},{20,0},{1,21},{5,17},{17,5},{21,1},{2,22},{6,... | collective-permute-start | bytes 884744 | tf_op jit(solution)/shard_map/ppermute | solution.py:36
  222.4 59.1 %collective-permute-start.35 = (bf16[184,2304]{1,0:T(8,128)(2,1)}, bf16[184,2304]{1,0:T(8,128)(2,1)}, u32[]{:S(2)}, u32[]{:S(2)}) collective-permute-start(bf16[184,2304]{1,0:T(8,128)(2,1)} %pad.20), channel_id=1, source_target_pairs={{0,8},{8,0},{1,9},{9,1},{2,10},{10,2},{3,11},{11,3},{4,12},{12,4},... | collective-permute-start | bytes 2543624 | tf_op jit(solution)/shard_map/ppermute | solution.py:234
  285.2 196.6 %reduce-scatter.6.cloned.1.call-start = ((), (), s32[]{:S(2)}) async-start(), calls=%async_computation.9 | async-start | bytes 8478720 | tf_op jit(solution)/shard_map/reduce_scatter | solution.py:91
  306.9 24.0 %collective-permute-start.32 = (bf16[64,2304]{1,0:T(8,128)(2,1)}, bf16[64,2304]{1,0:T(8,128)(2,1)}, u32[]{:S(2)}, u32[]{:S(2)}) collective-permute-start(bf16[64,2304]{1,0:T(8,128)(2,1)} %get-tuple-element.170), channel_id=1, source_target_pairs={{0,16},{4,20},{16,0},{20,4},{1,17},{5,21},{17,1},{21,5},{2,18},{6,... | collective-permute-start | bytes 884744 | tf_op jit(solution)/shard_map/ppermute | solution.py:36
  310.4 22.1 %collective-permute-start.33 = (bf16[64,2304]{1,0:T(8,128)(2,1)}, bf16[64,2304]{1,0:T(8,128)(2,1)}, u32[]{:S(2)}, u32[]{:S(2)}) collective-permute-start(bf16[64,2304]{1,0:T(8,128)(2,1)} %get-tuple-element.170), channel_id=1, source_target_pairs={{0,4},{4,0},{16,20},{20,16},{1,5},{5,1},{17,21},{21,17},{2,6},{6,2... | collective-permute-start | bytes 884744 | tf_op jit(solution)/shard_map/ppermute | solution.py:36
  316.3 25.4 %collective-permute-start.29 = (bf16[64,2304]{1,0:T(8,128)(2,1)}, bf16[64,2304]{1,0:T(8,128)(2,1)}, u32[]{:S(2)}, u32[]{:S(2)}) collective-permute-start(bf16[64,2304]{1,0:T(8,128)(2,1)} %get-tuple-element.171), channel_id=1, source_target_pairs={{0,16},{4,20},{16,0},{20,4},{1,17},{5,21},{17,1},{21,5},{2,18},{6,... | collective-permute-start | bytes 884744 | tf_op jit(solution)/shard_map/ppermute | solution.py:36
  341.7 23.2 %collective-permute-start.26 = (bf16[64,2304]{1,0:T(8,128)(2,1)S(1)}, bf16[64,2304]{1,0:T(8,128)(2,1)S(1)}, u32[]{:S(2)}, u32[]{:S(2)}) collective-permute-start(bf16[64,2304]{1,0:T(8,128)(2,1)S(1)} %reshape.468), channel_id=1, source_target_pairs={{0,16},{4,20},{16,0},{20,4},{1,17},{5,21},{17,1},{21,5},{2,18},{6,... | collective-permute-start | bytes 884744 | tf_op jit(solution)/shard_map/ppermute | solution.py:36
  395.9 217.6 %reduce-scatter.12.cloned.1.call-start = ((), (), s32[]{:S(2)}) async-start(), calls=%async_computation.12 | async-start | bytes 3686400 | tf_op jit(solution)/shard_map/reduce_scatter | solution.py:91
  506.9 141.8 %reduce-scatter.10.cloned.1.call-start = ((), (), s32[]{:S(2)}) async-start(), calls=%async_computation.11 | async-start | bytes 16957440 | tf_op jit(solution)/shard_map/reduce_scatter | solution.py:91
  520.1 183.0 %reduce-scatter.8.cloned.1.call-start = ((), (), s32[]{:S(2)}) async-start(), calls=%async_computation.10 | async-start | bytes 6635520 | tf_op jit(solution)/shard_map/reduce_scatter | solution.py:91
  527.2 269.6 %reduce-scatter.14.cloned.1.call-start = ((), (), s32[]{:S(2)}) async-start(), calls=%async_computation.13 | async-start | bytes 3317760 | tf_op jit(solution)/shard_map/reduce_scatter | solution.py:91
  586.2 68.3 %collective-permute-start.74 = (bf16[184,2304]{1,0:T(8,128)(2,1)}, bf16[184,2304]{1,0:T(8,128)(2,1)}, u32[]{:S(2)}, u32[]{:S(2)}) collective-permute-start(bf16[184,2304]{1,0:T(8,128)(2,1)} %get-tuple-element.107), channel_id=1, source_target_pairs={{0,8},{8,0},{1,9},{9,1},{2,10},{10,2},{3,11},{11,3},{4,12},{12,4},... | collective-permute-start | bytes 2543624 | tf_op jit(solution)/shard_map/ppermute | solution.py:100
  614.7 88.4 %collective-permute-start.68 = (bf16[288,640]{1,0:T(8,128)(2,1)S(1)}, bf16[288,640]{1,0:T(8,128)(2,1)}, u32[]{:S(2)}, u32[]{:S(2)}) collective-permute-start(bf16[288,640]{1,0:T(8,128)(2,1)S(1)} %get-tuple-element.149), channel_id=1, source_target_pairs={{0,8},{8,0},{1,9},{9,1},{2,10},{10,2},{3,11},{11,3},{4,12},{12,4},... | collective-permute-start | bytes 1105928 | tf_op jit(solution)/shard_map/ppermute | solution.py:100
  652.1 91.4 %collective-permute-start.60 = (bf16[288,2944]{1,0:T(8,128)(2,1)}, bf16[288,2944]{1,0:T(8,128)(2,1)}, u32[]{:S(2)}, u32[]{:S(2)}) collective-permute-start(bf16[288,2944]{1,0:T(8,128)(2,1)} %get-tuple-element.97), channel_id=1, source_target_pairs={{0,8},{8,0},{1,9},{9,1},{2,10},{10,2},{3,11},{11,3},{4,12},{12,4},... | collective-permute-start | bytes 5087240 | tf_op jit(solution)/shard_map/ppermute | solution.py:100
  709.2 80.0 %collective-permute-start.64 = (bf16[288,1152]{1,0:T(8,128)(2,1)}, bf16[288,1152]{1,0:T(8,128)(2,1)}, u32[]{:S(2)}, u32[]{:S(2)}) collective-permute-start(bf16[288,1152]{1,0:T(8,128)(2,1)} %get-tuple-element.119), channel_id=1, source_target_pairs={{0,8},{8,0},{1,9},{9,1},{2,10},{10,2},{3,11},{11,3},{4,12},{12,4},... | collective-permute-start | bytes 1990664 | tf_op jit(solution)/shard_map/ppermute | solution.py:100
  747.7 28.1 %collective-permute-start.63 = (bf16[72,2944]{1,0:T(8,128)(2,1)S(1)}, bf16[72,2944]{1,0:T(8,128)(2,1)}, u32[]{:S(2)}, u32[]{:S(2)}) collective-permute-start(bf16[72,2944]{1,0:T(8,128)(2,1)S(1)} %get-tuple-element.111), channel_id=1, source_target_pairs={{0,20},{4,16},{16,4},{20,0},{1,21},{5,17},{17,5},{21,1},{2,22},{6,... | collective-permute-start | bytes 1271816 | tf_op jit(solution)/shard_map/ppermute | solution.py:36
  (157 other events, 1466.6 us)
Sparse Core Ops, SparseCore 0:
  78.7 57.7 all-gather.4
  138.6 30.4 all-gather.6
  199.7 87.0 all-gather.8
  288.8 49.1 all-gather.10
  396.1 58.8 reduce-scatter.5
  507.0 32.6 reduce-scatter.11
  542.3 106.3 reduce-scatter.9
  651.2 51.7 reduce-scatter.7
  705.6 34.7 reduce-scatter.13

commit v6 on v5

--- a/solution.py
+++ b/solution.py
@@ -58,9 +58,11 @@
     return pairs.reshape(blocks.shape)
 
 
-def plane_exchange(blocks):
+def plane_exchange(blocks, *late):
     mine = reorder(blocks)
     got = [mine[0]] + [flip_send(mine[f], f) for f in (1, 2, 3)]
+    if late:
+        got = [after(g, *late) for g in got]
     return reorder(jnp.stack(got))
 
 
@@ -104,9 +106,9 @@
     return lax.psum_scatter(partial, "h", scatter_dimension=0, tiled=True).astype(F32)
 
 
-def column_block(blocks):
+def column_block(blocks, *late):
     four, rows, n = blocks.shape
-    mine = plane_exchange(blocks)
+    mine = plane_exchange(blocks, *late)
     return half_gather(mine.reshape(four * rows, n))
 
 
@@ -221,21 +223,25 @@
     else:
         out_block = half_gather(lax.ppermute(out_weight, HLXC, head_order(0)))
     other_lengths = lax.ppermute(lengths, "l", [(0, 1), (1, 0)])
+    down_block = half_gather(jnp.pad(down_weight, ((0, padded - units), (0, 0))))
+    gu_columns = jnp.concatenate(
+        [split_units(after(gate_weight, out_block)), split_units(after(up_weight, out_block))],
+        axis=2,
+    )
     qkv_block = column_block(
         jnp.concatenate(
             [split_heads(w) for w in (query_weight, key_weight, value_weight)] + [extra], axis=2
         ),
-    )
-    gu_block = column_block(
-        jnp.concatenate([split_units(gate_weight), split_units(up_weight)], axis=2)
-    )
-    down_own = jnp.pad(down_weight, ((0, padded - units), (0, 0)))
-    if halves == 2:
-        down_other = lax.ppermute(down_own, "h", [(0, 1), (1, 0)])
+        gu_columns,
+    )
+    gu_block = column_block(gu_columns)
     gathered = [plane_gather(to_line(inputs[s], rows)) for s in range(count)]
     w_out = line_gather(out_block)
+    first = width // 3
+    w_down_a = line_gather(down_block[:, :first])
     w_qkv = line_gather(qkv_block)
     w_gu = line_gather(gu_block)
+    w_down_b = line_gather(down_block[:, first:])
     step = jnp.arange(tokens, dtype=jnp.int32)
     place = jnp.concatenate([y * tokens + step, (1 - y) * tokens + step])
     local_place = place[:tokens]
@@ -279,12 +285,6 @@
         probs = expo / jnp.sum(expo, axis=-1, keepdims=True)
         attended = einsum("bhqk,bkhe->bqhe", probs.astype(BF16), values)
         attended = attended.astype(BF16).reshape(4 * tokens, part)
-        if s == 0:
-            if halves == 2:
-                down_block = in_order(down_own, after(down_other, attended))
-            else:
-                down_block = half_gather(down_own)
-            w_down = line_gather(down_block)
         out_sum = dot(attended, w_out)
         out_sum = plane_scatter(out_sum)
         mid = x_float[s] + BRANCH_SCALE * out_sum
@@ -314,7 +314,8 @@
     grad_boths = []
     for s in range(count):
         gate_pre, up_pre, sigmoid = acts[s]
-        grad_mixed = dot(after(branch2[s], down_terms), w_down, NT)
+        late = after(branch2[s], down_terms)
+        grad_mixed = dot(late[:, :first], w_down_a, NT) + dot(late[:, first:], w_down_b, NT)
         grad_gate = grad_mixed * up_pre * (sigmoid + gate_pre * sigmoid * (1.0 - sigmoid))
         grad_up = grad_mixed * gate_pre * sigmoid
         grad_boths.append(jnp.concatenate([grad_gate.astype(BF16), grad_up.astype(BF16)], axis=1))
@@ -334,11 +335,6 @@
         grad_mids.append(grad_mid)
         own_branch1.append((BRANCH_SCALE * grad_mid).astype(BF16))
         branch1.append(plane_gather(own_branch1[s]))
-
-    outputs = []
-    for s in range(count):
-        terms = dot(after(mixes[s], gu_terms, *own_branch1), w_down)
-        outputs.append((mids[s] + BRANCH_SCALE * plane_scatter(terms)).astype(BF16))
 
     grad_qkv = []
     input_grads = []
@@ -367,9 +363,17 @@
     v_part = line_scatter(v_terms)
     qk_terms = dot(after(all_normed, v_terms), all_grads[:, : 2 * part], TN).astype(BF16)
     qk_part = line_scatter(qk_terms)
-    all_attended = after(jnp.concatenate([k[4] for k in kept], axis=0), qk_terms)
+    all_attended = after(jnp.concatenate([k[4] for k in kept], axis=0), qk_terms, gu_part)
     out_terms = dot(all_attended, jnp.concatenate(branch1, axis=0), TN).astype(BF16)
     out_part = line_scatter(out_terms)
+    outputs = []
+    for s in range(count):
+        late = after(mixes[s], out_terms)
+        terms = jnp.concatenate(
+            [dot(late, w_down_a).astype(BF16), dot(late, w_down_b).astype(BF16)], axis=1
+        )
+        outputs.append((mids[s] + BRANCH_SCALE * plane_scatter(terms)).astype(BF16))
+
     all_in_terms = [dot(after(g, out_terms), w_qkv, NT).astype(BF16) for g in grad_qkv]
     factor_one = [norm_factor(v) for v in x_float]
     for s in range(count):

time: 832 us -> 906 us (1.089)
  starting transfers between devices: 84.5 us -> 112 us
  waiting for transfers between devices: 409 us -> 425 us
  local copies, waits for them, and re-layouts: 121 us -> 133 us
    ppermute x2 -> x3, waiting for transfers between devices: 116 us -> 133 us  [half_gather(): other = lax.ppermute(block, 'h', [(0, 1), (1, 0)])]
    ppermute x63, waiting for transfers between devices: 174 us -> 160 us  [flip_send(): return lax.ppermute(block, PLANE, [(p, p ^ flip) for p in range(4)])]
    ppermute x63, starting transfers between devices: 61.7 us -> 72.9 us  [flip_send(): return lax.ppermute(block, PLANE, [(p, p ^ flip) for p in range(4)])]
    all_gather x4 -> x5, starting transfers between devices: 0.16 us -> 11.1 us  [line_gather(): return lax.all_gather(block, LINE, axis=0, tiled=True)]
    dot_general x22 -> x26, matrix products: 117 us -> 122 us  [dot(): lax.dot_general(left, right, (contract, ((), ())), preferred_element_type...]
    unnamed x201 -> x231, local copies, waits for them, and re-layouts: 22.6 us -> 22.1 us
  transfers between devices with their start and end apart: 84 -> 85, of which waited for: 43 -> 41; matrix products, arithmetic and copies ran while one was open for 32% -> 33% of each run, Pallas kernels for 0% -> 0%
where the time goes in v6:
time: 906 us; the launch traced here: 893 us
  waiting for transfers between devices  425 us (47%)
  local copies, waits for them, and re-layouts  133 us (15%)
  matrix products  132 us (15%)
  starting transfers between devices  112 us (12%)
  other arithmetic  73.8 us (8%)
  between operations  16.6 us (2%)
    ppermute x63, waiting for transfers between devices, flip_send(): return lax.ppermute(block, PLANE, [(p, p ^ flip) for p in range(4)])  160 us
    ppermute x3, waiting for transfers between devices, half_gather(): other = lax.ppermute(block, 'h', [(0, 1), (1, 0)])  133 us
    dot_general x26, matrix products, dot(): lax.dot_general(left, right, (contract, ((), ())), preferred_element_type...  122 us
    reduce_scatter x5, waiting for transfers between devices, line_scatter(): return lax.psum_scatter(partial, LINE, scatter_dimension=0, tiled=True)  84.4 us
    ppermute x63, starting transfers between devices, flip_send(): return lax.ppermute(block, PLANE, [(p, p ^ flip) for p in range(4)])  72.9 us
    ppermute x4, waiting for transfers between devices, half_scatter(): other = lax.ppermute(other, 'h', [(0, 1), (1, 0)])  27 us
    reshape x12, local copies, waits for them, and re-layouts, from_line(): blocks = tokens.reshape(count, 2, 2, -1, 2, 2, rows)  22.9 us
    unnamed x231, local copies, waits for them, and re-layouts  22.1 us
  transfers between devices with their start and end apart: 85, of which 41 were waited for; matrix products, arithmetic and copies ran while one was open for 33% of the time, Pallas kernels for 0%

profile of v6, /device:TPU:0, one launch (start us, length us, event | category | flops | bytes accessed | tf_op | source)
XLA Modules:
  0.0 892.8 jit_solution(11827689780129708074)
XLA Ops:
  42.8 45.5 %collective-permute-done.8 = bf16[288,1792]{1,0:T(8,128)(2,1)S(1)} collective-permute-done((bf16[288,1792]{1,0:T(8,128)(2,1)S(1)}, bf16[288,1792]{1,0:T(8,128)(2,1)S(1)}, u32[]{:S(2)}, u32[]{:S(2)}) %collective-permute-start.8) | collective-permute-done | bytes 1032224 | tf_op jit(solution)/shard_map/ppermute | solution.py:87
  90.5 10.9 %all-gather.8.cloned.1.call-start = ((), (), s32[]{:S(2)}) async-start(), calls=%async_computation.6 | async-start | bytes 3317760 | tf_op jit(solution)/shard_map/all_gather | solution.py:74
  109.4 9.1 %collective-permute-done.9 = bf16[72,2944]{1,0:T(8,128)(2,1)S(1)} collective-permute-done((bf16[72,2944]{1,0:T(8,128)(2,1)S(1)}, bf16[72,2944]{1,0:T(8,128)(2,1)S(1)}, u32[]{:S(2)}, u32[]{:S(2)}) %collective-permute-start.9) | collective-permute-done | bytes 423968 | tf_op jit(solution)/shard_map/ppermute | solution.py:36
  118.5 8.1 collective-permute-done.10
  131.9 72.5 %collective-permute-done.12 = bf16[288,2944]{1,0:T(8,128)(2,1)S(1)} collective-permute-done((bf16[288,2944]{1,0:T(8,128)(2,1)S(1)}, bf16[288,2944]{1,0:T(8,128)(2,1)S(1)}, u32[]{:S(2)}, u32[]{:S(2)}) %collective-permute-start.12) | collective-permute-done | bytes 1695776 | tf_op jit(solution)/shard_map/ppermute | solution.py:87
  233.1 13.5 %collective-permute-done.1 = bf16[64,2304]{1,0:T(8,128)(2,1)S(1)} collective-permute-done((bf16[64,2304]{1,0:T(8,128)(2,1)S(1)}, bf16[64,2304]{1,0:T(8,128)(2,1)S(1)}, u32[]{:S(2)}, u32[]{:S(2)}) %collective-permute-start.1) | collective-permute-done | bytes 294944 | tf_op jit(solution)/shard_map/ppermute | solution.py:36
  252.5 15.5 %collective-permute-done.35 = bf16[184,2304]{1,0:T(8,128)(2,1)S(1)} collective-permute-done((bf16[184,2304]{1,0:T(8,128)(2,1)S(1)}, bf16[184,2304]{1,0:T(8,128)(2,1)S(1)}, u32[]{:S(2)}, u32[]{:S(2)}) %collective-permute-start.35) | collective-permute-done | bytes 847904 | tf_op jit(solution)/shard_map/ppermute | solution.py:87
  273.8 7.6 fusion.185
  284.3 7.4 fusion.183
  329.9 6.9 collective-permute-done.14
  390.3 7.4 fusion.184
  408.1 6.1 convolution_convert_fusion.2
  424.7 8.3 convolution_convert_fusion.7
  442.8 7.9 convolution_convert_fusion.8
  482.3 7.6 collective-permute-done.39
  533.7 10.1 %convolution_convert_fusion = bf16[2304,2944]{1,0:T(8,128)(2,1)} fusion(bf16[512,2304]{1,0:T(8,128)(2,1)S(1)} %pad_maximum_fusion.1, bf16[256,2944]{1,0:T(8,128)(2,1)S(1)} %copy-done.39, bf16[256,2944]{1,0:T(8,128)(2,1)S(1)} %copy-done.41), kind=kOutput, calls=%fused_computation.2 | convolution fusion | flops 6958579712 | bytes 18939904 | tf_op jit(solution)/shard_map/dot_general | solution.py:28
  556.1 9.2 %reduce-scatter.12.cloned.1.call-done = bf16[576,640]{1,0:T(8,128)(2,1)} async-done(((bf16[2304,640]{1,0:T(8,128)(2,1)}), bf16[576,640]{1,0:T(8,128)(2,1)}) %reduce-scatter.12.cloned.1.call-update) | async-done | bytes 737296 | tf_op jit(solution)/shard_map/reduce_scatter | solution.py:93
  569.8 27.0 %collective-permute-done.74 = bf16[184,2304]{1,0:T(8,128)(2,1)} collective-permute-done((bf16[184,2304]{1,0:T(8,128)(2,1)}, bf16[184,2304]{1,0:T(8,128)(2,1)}, u32[]{:S(2)}, u32[]{:S(2)}) %collective-permute-start.74) | collective-permute-done | bytes 847904 | tf_op jit(solution)/shard_map/ppermute | solution.py:102
  599.4 75.1 %reduce-scatter.8.cloned.1.call-done = bf16[576,2944]{1,0:T(8,128)(2,1)} async-done(((bf16[2304,2944]{1,0:T(8,128)(2,1)}), bf16[576,2944]{1,0:T(8,128)(2,1)}) %reduce-scatter.8.cloned.1.call-update) | async-done | bytes 3391504 | tf_op jit(solution)/shard_map/reduce_scatter | solution.py:93
  734.8 8.0 collective-permute-done.56
  764.9 6.6 collective-permute-done.49
  786.0 10.0 %collective-permute-done.52 = bf16[64,2304]{1,0:T(8,128)(2,1)S(1)} collective-permute-done((bf16[64,2304]{1,0:T(8,128)(2,1)S(1)}, bf16[64,2304]{1,0:T(8,128)(2,1)S(1)}, u32[]{:S(2)}, u32[]{:S(2)}) %collective-permute-start.52) | collective-permute-done | bytes 294944 | tf_op jit(solution)/shard_map/ppermute | solution.py:36
  813.7 20.8 %collective-permute-done.61 = bf16[72,2944]{1,0:T(8,128)(2,1)S(1)} collective-permute-done((bf16[72,2944]{1,0:T(8,128)(2,1)}, bf16[72,2944]{1,0:T(8,128)(2,1)S(1)}, u32[]{:S(2)}, u32[]{:S(2)}) %collective-permute-start.61) | collective-permute-done | bytes 423968 | tf_op jit(solution)/shard_map/ppermute | solution.py:36
  871.3 13.6 %collective-permute-done.73 = bf16[72,2304]{1,0:T(8,128)(2,1)S(1)} collective-permute-done((bf16[72,2304]{1,0:T(8,128)(2,1)S(1)}, bf16[72,2304]{1,0:T(8,128)(2,1)S(1)}, u32[]{:S(2)}, u32[]{:S(2)}) %collective-permute-start.73) | collective-permute-done | bytes 331808 | tf_op jit(solution)/shard_map/ppermute | solution.py:396
  (637 shorter events, 461.4 us)
Async XLA Ops:
  7.2 263.6 %all-gather.6.cloned.1.call-start = ((), (), s32[]{:S(2)}) async-start(), calls=%async_computation.5 | async-start | bytes 10321920 | tf_op jit(solution)/shard_map/all_gather | solution.py:74
  38.3 50.0 %collective-permute-start.8 = (bf16[288,1792]{1,0:T(8,128)(2,1)S(1)}, bf16[288,1792]{1,0:T(8,128)(2,1)S(1)}, u32[]{:S(2)}, u32[]{:S(2)}) collective-permute-start(bf16[288,1792]{1,0:T(8,128)(2,1)S(1)} %bitcast.310), channel_id=1, source_target_pairs={{0,8},{8,0},{1,9},{9,1},{2,10},{10,2},{3,11},{11,3},{4,12},{12,4},... | collective-permute-start | bytes 3096584 | tf_op jit(solution)/shard_map/ppermute | solution.py:87
  90.5 215.1 %all-gather.8.cloned.1.call-start = ((), (), s32[]{:S(2)}) async-start(), calls=%async_computation.6 | async-start | bytes 3317760 | tf_op jit(solution)/shard_map/all_gather | solution.py:74
  109.3 281.0 %all-gather.10.cloned.1.call-start = ((), (), s32[]{:S(2)}) async-start(), calls=%async_computation.7 | async-start | bytes 16957440 | tf_op jit(solution)/shard_map/all_gather | solution.py:74
  128.5 75.8 %collective-permute-start.12 = (bf16[288,2944]{1,0:T(8,128)(2,1)S(1)}, bf16[288,2944]{1,0:T(8,128)(2,1)S(1)}, u32[]{:S(2)}, u32[]{:S(2)}) collective-permute-start(bf16[288,2944]{1,0:T(8,128)(2,1)S(1)} %bitcast.303), channel_id=1, source_target_pairs={{0,8},{8,0},{1,9},{9,1},{2,10},{10,2},{3,11},{11,3},{4,12},{12,4},... | collective-permute-start | bytes 5087240 | tf_op jit(solution)/shard_map/ppermute | solution.py:87
  206.8 207.6 %all-gather.14.cloned.1.call-start = ((), (), s32[]{:S(2)}) async-start(), calls=%async_computation.9 | async-start | bytes 5652480 | tf_op jit(solution)/shard_map/all_gather | solution.py:74
  229.5 38.4 %collective-permute-start.35 = (bf16[184,2304]{1,0:T(8,128)(2,1)S(1)}, bf16[184,2304]{1,0:T(8,128)(2,1)S(1)}, u32[]{:S(2)}, u32[]{:S(2)}) collective-permute-start(bf16[184,2304]{1,0:T(8,128)(2,1)S(1)} %pad.20), channel_id=1, source_target_pairs={{0,8},{8,0},{1,9},{9,1},{2,10},{10,2},{3,11},{11,3},{4,12},{12,4},... | collective-permute-start | bytes 2543624 | tf_op jit(solution)/shard_map/ppermute | solution.py:87
  270.8 148.7 %all-gather.12.cloned.1.call-start = ((), (), s32[]{:S(2)}) async-start(), calls=%async_computation.8 | async-start | bytes 2826240 | tf_op jit(solution)/shard_map/all_gather | solution.py:74
  327.1 176.8 %reduce-scatter.6.cloned.1.call-start = ((), (), s32[]{:S(2)}) async-start(), calls=%async_computation.10 | async-start | bytes 8478720 | tf_op jit(solution)/shard_map/reduce_scatter | solution.py:93
  414.3 151.0 %reduce-scatter.12.cloned.1.call-start = ((), (), s32[]{:S(2)}) async-start(), calls=%async_computation.13 | async-start | bytes 3686400 | tf_op jit(solution)/shard_map/reduce_scatter | solution.py:93
  531.1 143.5 %reduce-scatter.8.cloned.1.call-start = ((), (), s32[]{:S(2)}) async-start(), calls=%async_computation.11 | async-start | bytes 16957440 | tf_op jit(solution)/shard_map/reduce_scatter | solution.py:93
  543.8 216.0 %reduce-scatter.10.cloned.1.call-start = ((), (), s32[]{:S(2)}) async-start(), calls=%async_computation.12 | async-start | bytes 6635520 | tf_op jit(solution)/shard_map/reduce_scatter | solution.py:93
  550.8 314.9 %reduce-scatter.14.cloned.1.call-start = ((), (), s32[]{:S(2)}) async-start(), calls=%async_computation.14 | async-start | bytes 3317760 | tf_op jit(solution)/shard_map/reduce_scatter | solution.py:93
  553.6 43.2 %collective-permute-start.74 = (bf16[184,2304]{1,0:T(8,128)(2,1)}, bf16[184,2304]{1,0:T(8,128)(2,1)}, u32[]{:S(2)}, u32[]{:S(2)}) collective-permute-start(bf16[184,2304]{1,0:T(8,128)(2,1)} %get-tuple-element.117), channel_id=1, source_target_pairs={{0,8},{8,0},{1,9},{9,1},{2,10},{10,2},{3,11},{11,3},{4,12},{12,4},... | collective-permute-start | bytes 2543624 | tf_op jit(solution)/shard_map/ppermute | solution.py:102
  567.3 192.5 %collective-permute-start.68 = (bf16[288,640]{1,0:T(8,128)(2,1)}, bf16[288,640]{1,0:T(8,128)(2,1)}, u32[]{:S(2)}, u32[]{:S(2)}) collective-permute-start(bf16[288,640]{1,0:T(8,128)(2,1)} %get-tuple-element.159), channel_id=1, source_target_pairs={{0,8},{8,0},{1,9},{9,1},{2,10},{10,2},{3,11},{11,3},{4,12},{12,4},... | collective-permute-start | bytes 1105928 | tf_op jit(solution)/shard_map/ppermute | solution.py:102
  697.1 34.6 %collective-permute-start.54 = (bf16[64,2304]{1,0:T(8,128)(2,1)}, bf16[64,2304]{1,0:T(8,128)(2,1)}, u32[]{:S(2)}, u32[]{:S(2)}) collective-permute-start(bf16[64,2304]{1,0:T(8,128)(2,1)} %get-tuple-element.130), channel_id=1, source_target_pairs={{0,16},{4,20},{16,0},{20,4},{1,17},{5,21},{17,1},{21,5},{2,18},{6,... | collective-permute-start | bytes 884744 | tf_op jit(solution)/shard_map/ppermute | solution.py:36
  714.9 28.0 %collective-permute-start.56 = (bf16[64,2304]{1,0:T(8,128)(2,1)}, bf16[64,2304]{1,0:T(8,128)(2,1)}, u32[]{:S(2)}, u32[]{:S(2)}) collective-permute-start(bf16[64,2304]{1,0:T(8,128)(2,1)} %get-tuple-element.131), channel_id=1, source_target_pairs={{0,20},{4,16},{16,4},{20,0},{1,21},{5,17},{17,5},{21,1},{2,22},{6,... | collective-permute-start | bytes 884744 | tf_op jit(solution)/shard_map/ppermute | solution.py:36
  716.1 88.8 %collective-permute-start.60 = (bf16[288,2944]{1,0:T(8,128)(2,1)}, bf16[288,2944]{1,0:T(8,128)(2,1)}, u32[]{:S(2)}, u32[]{:S(2)}) collective-permute-start(bf16[288,2944]{1,0:T(8,128)(2,1)} %get-tuple-element.107), channel_id=1, source_target_pairs={{0,8},{8,0},{1,9},{9,1},{2,10},{10,2},{3,11},{11,3},{4,12},{12,4},... | collective-permute-start | bytes 5087240 | tf_op jit(solution)/shard_map/ppermute | solution.py:102
  731.7 29.7 %collective-permute-start.48 = (bf16[64,2304]{1,0:T(8,128)(2,1)}, bf16[64,2304]{1,0:T(8,128)(2,1)}, u32[]{:S(2)}, u32[]{:S(2)}) collective-permute-start(bf16[64,2304]{1,0:T(8,128)(2,1)} %get-tuple-element.136), channel_id=1, source_target_pairs={{0,16},{4,20},{16,0},{20,4},{1,17},{5,21},{17,1},{21,5},{2,18},{6,... | collective-permute-start | bytes 884744 | tf_op jit(solution)/shard_map/ppermute | solution.py:36
  734.8 36.8 %collective-permute-start.49 = (bf16[64,2304]{1,0:T(8,128)(2,1)}, bf16[64,2304]{1,0:T(8,128)(2,1)}, u32[]{:S(2)}, u32[]{:S(2)}) collective-permute-start(bf16[64,2304]{1,0:T(8,128)(2,1)} %get-tuple-element.138), channel_id=1, source_target_pairs={{0,4},{4,0},{16,20},{20,16},{1,5},{5,1},{17,21},{21,17},{2,6},{6,2... | collective-permute-start | bytes 884744 | tf_op jit(solution)/shard_map/ppermute | solution.py:36
  742.9 35.0 %collective-permute-start.50 = (bf16[64,2304]{1,0:T(8,128)(2,1)}, bf16[64,2304]{1,0:T(8,128)(2,1)}, u32[]{:S(2)}, u32[]{:S(2)}) collective-permute-start(bf16[64,2304]{1,0:T(8,128)(2,1)} %get-tuple-element.137), channel_id=1, source_target_pairs={{0,20},{4,16},{16,4},{20,0},{1,21},{5,17},{17,5},{21,1},{2,22},{6,... | collective-permute-start | bytes 884744 | tf_op jit(solution)/shard_map/ppermute | solution.py:36
  761.5 34.5 %collective-permute-start.52 = (bf16[64,2304]{1,0:T(8,128)(2,1)S(1)}, bf16[64,2304]{1,0:T(8,128)(2,1)S(1)}, u32[]{:S(2)}, u32[]{:S(2)}) collective-permute-start(bf16[64,2304]{1,0:T(8,128)(2,1)S(1)} %copy-done.83), channel_id=1, source_target_pairs={{0,4},{4,0},{16,20},{20,16},{1,5},{5,1},{17,21},{21,17},{2,6},{6,2... | collective-permute-start | bytes 884744 | tf_op jit(solution)/shard_map/ppermute | solution.py:36
  771.6 29.9 %collective-permute-start.53 = (bf16[64,2304]{1,0:T(8,128)(2,1)S(1)}, bf16[64,2304]{1,0:T(8,128)(2,1)S(1)}, u32[]{:S(2)}, u32[]{:S(2)}) collective-permute-start(bf16[64,2304]{1,0:T(8,128)(2,1)S(1)} %copy-done.82), channel_id=1, source_target_pairs={{0,20},{4,16},{16,4},{20,0},{1,21},{5,17},{17,5},{21,1},{2,22},{6,... | collective-permute-start | bytes 884744 | tf_op jit(solution)/shard_map/ppermute | solution.py:36
  801.5 51.5 %collective-permute-start.64 = (bf16[288,1152]{1,0:T(8,128)(2,1)}, bf16[288,1152]{1,0:T(8,128)(2,1)}, u32[]{:S(2)}, u32[]{:S(2)}) collective-permute-start(bf16[288,1152]{1,0:T(8,128)(2,1)} %get-tuple-element.129), channel_id=1, source_target_pairs={{0,8},{8,0},{1,9},{9,1},{2,10},{10,2},{3,11},{11,3},{4,12},{12,4},... | collective-permute-start | bytes 1990664 | tf_op jit(solution)/shard_map/ppermute | solution.py:102
  (173 other events, 1756.5 us)
Sparse Core Ops, SparseCore 0:
  90.7 58.3 all-gather.5
  151.2 25.7 all-gather.7
  206.9 86.9 all-gather.9
  295.3 36.3 all-gather.13
  333.6 23.4 all-gather.11
  414.4 61.1 reduce-scatter.5
  531.2 34.0 reduce-scatter.11
  567.9 106.5 reduce-scatter.7
  677.1 51.7 reduce-scatter.9
  731.3 34.7 reduce-scatter.13

commit v7 on v5

--- a/solution.py
+++ b/solution.py
@@ -363,11 +363,9 @@
         grad_qkv.append(jnp.pad(grads, ((0, 0), (0, spare))))
     all_normed = jnp.concatenate(normed, axis=0)
     all_grads = jnp.concatenate(grad_qkv, axis=0)
-    v_terms = dot(all_normed, all_grads[:, 2 * part :], TN).astype(BF16)
-    v_part = line_scatter(v_terms)
-    qk_terms = dot(after(all_normed, v_terms), all_grads[:, : 2 * part], TN).astype(BF16)
-    qk_part = line_scatter(qk_terms)
-    all_attended = after(jnp.concatenate([k[4] for k in kept], axis=0), qk_terms)
+    qkv_terms = dot(all_normed, all_grads, TN).astype(BF16)
+    qkv_part = line_scatter(qkv_terms)
+    all_attended = after(jnp.concatenate([k[4] for k in kept], axis=0), qkv_terms, gu_part)
     out_terms = dot(all_attended, jnp.concatenate(branch1, axis=0), TN).astype(BF16)
     out_part = line_scatter(out_terms)
     all_in_terms = [dot(after(g, out_terms), w_qkv, NT).astype(BF16) for g in grad_qkv]
@@ -379,8 +377,8 @@
             (grad_mids[s] + norm_back(x_float[s], factor_one[s], grad_norm)).astype(BF16)
         )
 
-    qk_part = after(qk_part, *input_grads)
-    gu_raw = after(column_grad(gu_part, rows, *input_grads), qk_part)
+    qkv_part = after(qkv_part, *input_grads)
+    gu_raw = after(column_grad(gu_part, rows, *input_grads), qkv_part)
     gate_grad, up_grad = lax.optimization_barrier(
         (join_units(gu_raw[:, :, :hidden]), join_units(gu_raw[:, :, hidden:]))
     )
@@ -398,9 +396,7 @@
         )
     else:
         out_grad = lax.ppermute(half_scatter(out_part), HLXC, [(b, a) for a, b in head_order(0)])
-    v_raw = column_grad(v_part, rows, qk_part)
-    qk_raw = column_grad(qk_part, rows, gate_grad, up_grad)
-    qkv_raw = jnp.concatenate([qk_raw, v_raw], axis=2)
+    qkv_raw = column_grad(qkv_part, rows, gate_grad, up_grad)
 
     gate_grad, up_grad = gate_grad.astype(F32), up_grad.astype(F32)
     ffn_gain_grad = jnp.sum(
@@ -423,7 +419,7 @@
         out_grad,
         gate_grad,
         up_grad,
-        half_scatter(down_part, v_part)[:units],
+        half_scatter(down_part, qkv_part)[:units],
         attn_gain_grad,
         ffn_gain_grad,
     )

time: 832 us -> 834 us (level)
  local copies, waits for them, and re-layouts: 121 us -> 136 us
  waiting for transfers between devices: 409 us -> 400 us
    reduce_scatter x5 -> x4, waiting for transfers between devices: 79.8 us -> 0.01 us  [line_scatter(): return lax.psum_scatter(partial, LINE, scatter_dimension=0, tiled=True)]
    ppermute x4 -> x3, waiting for transfers between devices: 25.6 us -> 66.5 us  [half_scatter(): other = lax.ppermute(other, 'h', [(0, 1), (1, 0)])]
    ppermute x63 -> x60, waiting for transfers between devices: 174 us -> 194 us  [flip_send(): return lax.ppermute(block, PLANE, [(p, p ^ flip) for p in range(4)])]
    ppermute x63 -> x60, starting transfers between devices: 61.7 us -> 67.4 us  [flip_send(): return lax.ppermute(block, PLANE, [(p, p ^ flip) for p in range(4)])]
    dot_general x22 -> x21, matrix products: 117 us -> 117 us  [dot(): lax.dot_general(left, right, (contract, ((), ())), preferred_element_type...]
    unnamed x201 -> x181, local copies, waits for them, and re-layouts: 22.6 us -> 22.6 us
  transfers between devices with their start and end apart: 84 -> 79, of which waited for: 43 -> 45; matrix products, arithmetic and copies ran while one was open for 32% -> 35% of each run, Pallas kernels for 0% -> 0%
where the time goes in v7:
time: 834 us; the launch traced here: 828 us
  waiting for transfers between devices  400 us (48%)
  local copies, waits for them, and re-layouts  136 us (16%)
  matrix products  125 us (15%)
  starting transfers between devices  83.6 us (10%)
  other arithmetic  66.7 us (8%)
  between operations  16.1 us (2%)
    ppermute x60, waiting for transfers between devices, flip_send(): return lax.ppermute(block, PLANE, [(p, p ^ flip) for p in range(4)])  194 us
    ppermute x2, waiting for transfers between devices, half_gather(): other = lax.ppermute(block, 'h', [(0, 1), (1, 0)])  120 us
    dot_general x21, matrix products, dot(): lax.dot_general(left, right, (contract, ((), ())), preferred_element_type...  117 us
    ppermute x60, starting transfers between devices, flip_send(): return lax.ppermute(block, PLANE, [(p, p ^ flip) for p in range(4)])  67.4 us
    ppermute x3, waiting for transfers between devices, half_scatter(): other = lax.ppermute(other, 'h', [(0, 1), (1, 0)])  66.5 us
    unnamed x181, local copies, waits for them, and re-layouts  22.6 us
    reshape x12, local copies, waits for them, and re-layouts, from_line(): blocks = tokens.reshape(count, 2, 2, -1, 2, 2, rows)  22.1 us
  transfers between devices with their start and end apart: 79, of which 45 were waited for; matrix products, arithmetic and copies ran while one was open for 35% of the time, Pallas kernels for 0%

profile of v7, /device:TPU:0, one launch (start us, length us, event | category | flops | bytes accessed | tf_op | source)
XLA Modules:
  0.0 827.9 jit_solution(11994693708928906533)
XLA Ops:
  21.4 6.5 collective-permute-done.5
  35.9 45.0 %collective-permute-done.6 = bf16[288,1792]{1,0:T(8,128)(2,1)S(1)} collective-permute-done((bf16[288,1792]{1,0:T(8,128)(2,1)S(1)}, bf16[288,1792]{1,0:T(8,128)(2,1)S(1)}, u32[]{:S(2)}, u32[]{:S(2)}) %collective-permute-start.6) | collective-permute-done | bytes 1032224 | tf_op jit(solution)/shard_map/ppermute | solution.py:85
  110.2 7.3 collective-permute-done.9
  117.5 9.7 %collective-permute-done.8 = bf16[72,2944]{1,0:T(8,128)(2,1)S(1)} collective-permute-done((bf16[72,2944]{1,0:T(8,128)(2,1)S(1)}, bf16[72,2944]{1,0:T(8,128)(2,1)S(1)}, u32[]{:S(2)}, u32[]{:S(2)}) %collective-permute-start.8) | collective-permute-done | bytes 423968 | tf_op jit(solution)/shard_map/ppermute | solution.py:36
  129.5 75.0 %collective-permute-done.10 = bf16[288,2944]{1,0:T(8,128)(2,1)S(1)} collective-permute-done((bf16[288,2944]{1,0:T(8,128)(2,1)S(1)}, bf16[288,2944]{1,0:T(8,128)(2,1)S(1)}, u32[]{:S(2)}, u32[]{:S(2)}) %collective-permute-start.10) | collective-permute-done | bytes 1695776 | tf_op jit(solution)/shard_map/ppermute | solution.py:85
  232.5 8.6 %collective-permute-done.22 = bf16[64,2304]{1,0:T(8,128)(2,1)S(1)} collective-permute-done((bf16[64,2304]{1,0:T(8,128)(2,1)S(1)}, bf16[64,2304]{1,0:T(8,128)(2,1)S(1)}, u32[]{:S(2)}, u32[]{:S(2)}) %collective-permute-start.22) | collective-permute-done | bytes 294944 | tf_op jit(solution)/shard_map/ppermute | solution.py:36
  250.8 7.4 fusion.186
  262.2 7.4 fusion.188
  302.8 9.5 %collective-permute-done.23 = bf16[64,2304]{1,0:T(8,128)(2,1)S(1)} collective-permute-done((bf16[64,2304]{1,0:T(8,128)(2,1)S(1)}, bf16[64,2304]{1,0:T(8,128)(2,1)S(1)}, u32[]{:S(2)}, u32[]{:S(2)}) %collective-permute-start.23) | collective-permute-done | bytes 294944 | tf_op jit(solution)/shard_map/ppermute | solution.py:36
  363.6 6.5 collective-permute-done.28
  374.5 7.6 fusion.187
  401.2 7.9 multiply_convert_fusion.1
  414.7 7.3 convolution_convert_fusion.7
  422.0 8.8 %convolution_convert_fusion.6 = bf16[256,2304]{1,0:T(8,128)(2,1)} fusion(bf16[256,2944]{1,0:T(8,128)(2,1)S(1)} %pad_maximum_fusion.5, bf16[2304,2944]{1,0:T(8,128)(2,1)} %all-gather.9.cloned.1.call-done), kind=kOutput, calls=%fused_computation.8 | convolution fusion | flops 3473473536 | bytes 16252928 | tf_op jit(solution)/shard_map/dot_general | solution.py:28
  430.8 10.1 %convolution_convert_fusion = bf16[2304,2944]{1,0:T(8,128)(2,1)} fusion(bf16[512,2304]{1,0:T(8,128)(2,1)S(1)} %copy-done.23, bf16[256,2944]{1,0:T(8,128)(2,1)S(1)} %pad_maximum_fusion.5, bf16[256,2944]{1,0:T(8,128)(2,1)S(1)} %pad_maximum_fusion.4), kind=kOutput, calls=%fused_computation.2 | convolution fusion | flops 6958579712 | bytes 18939904 | tf_op jit(solution)/shard_map/dot_general | solution.py:28
  448.4 12.8 %collective-permute-done.39 = bf16[64,2304]{1,0:T(8,128)(2,1)S(1)} collective-permute-done((bf16[64,2304]{1,0:T(8,128)(2,1)S(1)}, bf16[64,2304]{1,0:T(8,128)(2,1)S(1)}, u32[]{:S(2)}, u32[]{:S(2)}) %collective-permute-start.39) | collective-permute-done | bytes 294944 | tf_op jit(solution)/shard_map/ppermute | solution.py:36
  531.5 6.8 convolution_convert_fusion.1
  558.5 6.5 collective-permute-done.42
  566.3 9.5 %collective-permute-done.45 = bf16[64,2304]{1,0:T(8,128)(2,1)S(1)} collective-permute-done((bf16[64,2304]{1,0:T(8,128)(2,1)S(1)}, bf16[64,2304]{1,0:T(8,128)(2,1)S(1)}, u32[]{:S(2)}, u32[]{:S(2)}) %collective-permute-start.45) | collective-permute-done | bytes 294944 | tf_op jit(solution)/shard_map/ppermute | solution.py:36
  607.4 15.5 %collective-permute-done.59 = bf16[64,2304]{1,0:T(8,128)(2,1)S(1)} collective-permute-done((bf16[64,2304]{1,0:T(8,128)(2,1)S(1)}, bf16[64,2304]{1,0:T(8,128)(2,1)S(1)}, u32[]{:S(2)}, u32[]{:S(2)}) %collective-permute-start.59) | collective-permute-done | bytes 294944 | tf_op jit(solution)/shard_map/ppermute | solution.py:36
  656.9 66.5 %collective-permute-done.60 = bf16[288,2944]{1,0:T(8,128)(2,1)} collective-permute-done((bf16[288,2944]{1,0:T(8,128)(2,1)}, bf16[288,2944]{1,0:T(8,128)(2,1)}, u32[]{:S(2)}, u32[]{:S(2)}) %collective-permute-start.60) | collective-permute-done | bytes 1695776 | tf_op jit(solution)/shard_map/ppermute | solution.py:100
  732.1 23.0 %collective-permute-done.63 = bf16[72,2944]{1,0:T(8,128)(2,1)S(1)} collective-permute-done((bf16[72,2944]{1,0:T(8,128)(2,1)S(1)}, bf16[72,2944]{1,0:T(8,128)(2,1)S(1)}, u32[]{:S(2)}, u32[]{:S(2)}) %collective-permute-start.63) | collective-permute-done | bytes 423968 | tf_op jit(solution)/shard_map/ppermute | solution.py:36
  755.1 7.8 collective-permute-done.61
  805.6 14.3 %collective-permute-done.69 = bf16[72,2304]{1,0:T(8,128)(2,1)S(1)} collective-permute-done((bf16[72,2304]{1,0:T(8,128)(2,1)S(1)}, bf16[72,2304]{1,0:T(8,128)(2,1)S(1)}, u32[]{:S(2)}, u32[]{:S(2)}) %collective-permute-start.69) | collective-permute-done | bytes 331808 | tf_op jit(solution)/shard_map/ppermute | solution.py:390
  (552 shorter events, 424.4 us)
Async XLA Ops:
  7.2 240.1 %all-gather.5.cloned.1.call-start = ((), (), s32[]{:S(2)}) async-start(), calls=%async_computation.4 | async-start | bytes 10321920 | tf_op jit(solution)/shard_map/all_gather | solution.py:72
  33.2 47.7 %collective-permute-start.6 = (bf16[288,1792]{1,0:T(8,128)(2,1)S(1)}, bf16[288,1792]{1,0:T(8,128)(2,1)S(1)}, u32[]{:S(2)}, u32[]{:S(2)}) collective-permute-start(bf16[288,1792]{1,0:T(8,128)(2,1)S(1)} %bitcast.287), channel_id=1, source_target_pairs={{0,8},{8,0},{1,9},{9,1},{2,10},{10,2},{3,11},{11,3},{4,12},{12,4},... | collective-permute-start | bytes 3096584 | tf_op jit(solution)/shard_map/ppermute | solution.py:85
  83.1 206.9 %all-gather.7.cloned.1.call-start = ((), (), s32[]{:S(2)}) async-start(), calls=%async_computation.5 | async-start | bytes 3317760 | tf_op jit(solution)/shard_map/all_gather | solution.py:72
  83.1 25.0 %collective-permute-start.13 = (bf16[72,2304]{1,0:T(8,128)(2,1)}, bf16[72,2304]{1,0:T(8,128)(2,1)S(1)}, u32[]{:S(2)}, u32[]{:S(2)}) collective-permute-start(bf16[72,2304]{1,0:T(8,128)(2,1)} %param.17), channel_id=1, source_target_pairs={{0,8},{2,9},{4,10},{6,11},{8,12},{10,13},{12,14},{14,15},{1,0},{3,... | collective-permute-start | bytes 995336 | tf_op jit(solution)/shard_map/ppermute | solution.py:219
  110.2 264.3 %all-gather.9.cloned.1.call-start = ((), (), s32[]{:S(2)}) async-start(), calls=%async_computation.6 | async-start | bytes 16957440 | tf_op jit(solution)/shard_map/all_gather | solution.py:72
  128.1 76.5 %collective-permute-start.10 = (bf16[288,2944]{1,0:T(8,128)(2,1)S(1)}, bf16[288,2944]{1,0:T(8,128)(2,1)S(1)}, u32[]{:S(2)}, u32[]{:S(2)}) collective-permute-start(bf16[288,2944]{1,0:T(8,128)(2,1)S(1)} %bitcast.278), channel_id=1, source_target_pairs={{0,8},{8,0},{1,9},{9,1},{2,10},{10,2},{3,11},{11,3},{4,12},{12,4},... | collective-permute-start | bytes 5087240 | tf_op jit(solution)/shard_map/ppermute | solution.py:85
  207.0 194.2 %all-gather.11.cloned.1.call-start = ((), (), s32[]{:S(2)}) async-start(), calls=%async_computation.7 | async-start | bytes 8478720 | tf_op jit(solution)/shard_map/all_gather | solution.py:72
  216.1 24.9 %collective-permute-start.22 = (bf16[64,2304]{1,0:T(8,128)(2,1)S(1)}, bf16[64,2304]{1,0:T(8,128)(2,1)S(1)}, u32[]{:S(2)}, u32[]{:S(2)}) collective-permute-start(bf16[64,2304]{1,0:T(8,128)(2,1)S(1)} %reshape.455), channel_id=1, source_target_pairs={{0,20},{4,16},{16,4},{20,0},{1,21},{5,17},{17,5},{21,1},{2,22},{6,... | collective-permute-start | bytes 884744 | tf_op jit(solution)/shard_map/ppermute | solution.py:36
  229.2 54.2 %collective-permute-start.35 = (bf16[184,2304]{1,0:T(8,128)(2,1)}, bf16[184,2304]{1,0:T(8,128)(2,1)}, u32[]{:S(2)}, u32[]{:S(2)}) collective-permute-start(bf16[184,2304]{1,0:T(8,128)(2,1)} %pad.20), channel_id=1, source_target_pairs={{0,8},{8,0},{1,9},{9,1},{2,10},{10,2},{3,11},{11,3},{4,12},{12,4},... | collective-permute-start | bytes 2543624 | tf_op jit(solution)/shard_map/ppermute | solution.py:234
  287.0 223.1 %reduce-scatter.5.cloned.1.call-start = ((), (), s32[]{:S(2)}) async-start(), calls=%async_computation.8 | async-start | bytes 8478720 | tf_op jit(solution)/shard_map/reduce_scatter | solution.py:91
  324.8 25.5 %collective-permute-start.30 = (bf16[64,2304]{1,0:T(8,128)(2,1)}, bf16[64,2304]{1,0:T(8,128)(2,1)}, u32[]{:S(2)}, u32[]{:S(2)}) collective-permute-start(bf16[64,2304]{1,0:T(8,128)(2,1)} %get-tuple-element.166), channel_id=1, source_target_pairs={{0,4},{4,0},{16,20},{20,16},{1,5},{5,1},{17,21},{21,17},{2,6},{6,2... | collective-permute-start | bytes 884744 | tf_op jit(solution)/shard_map/ppermute | solution.py:36
  398.3 181.8 %reduce-scatter.7.cloned.1.call-start = ((), (), s32[]{:S(2)}) async-start(), calls=%async_computation.9 | async-start | bytes 16957440 | tf_op jit(solution)/shard_map/reduce_scatter | solution.py:91
  440.9 211.4 %reduce-scatter.9.cloned.1.call-start = ((), (), s32[]{:S(2)}) async-start(), calls=%async_computation.10 | async-start | bytes 10321920 | tf_op jit(solution)/shard_map/reduce_scatter | solution.py:91
  538.3 261.9 %reduce-scatter.11.cloned.1.call-start = ((), (), s32[]{:S(2)}) async-start(), calls=%async_computation.11 | async-start | bytes 3317760 | tf_op jit(solution)/shard_map/reduce_scatter | solution.py:91
  580.2 149.4 %collective-permute-start.70 = (bf16[184,2304]{1,0:T(8,128)(2,1)}, bf16[184,2304]{1,0:T(8,128)(2,1)}, u32[]{:S(2)}, u32[]{:S(2)}) collective-permute-start(bf16[184,2304]{1,0:T(8,128)(2,1)} %get-tuple-element.105), channel_id=1, source_target_pairs={{0,8},{8,0},{1,9},{9,1},{2,10},{10,2},{3,11},{11,3},{4,12},{12,4},... | collective-permute-start | bytes 2543624 | tf_op jit(solution)/shard_map/ppermute | solution.py:100
  594.1 28.9 %collective-permute-start.59 = (bf16[64,2304]{1,0:T(8,128)(2,1)S(1)}, bf16[64,2304]{1,0:T(8,128)(2,1)S(1)}, u32[]{:S(2)}, u32[]{:S(2)}) collective-permute-start(bf16[64,2304]{1,0:T(8,128)(2,1)S(1)} %get-tuple-element.120), channel_id=1, source_target_pairs={{0,20},{4,16},{16,4},{20,0},{1,21},{5,17},{17,5},{21,1},{2,22},{6,... | collective-permute-start | bytes 884744 | tf_op jit(solution)/shard_map/ppermute | solution.py:36
  595.0 32.7 %collective-permute-start.58 = (bf16[64,2304]{1,0:T(8,128)(2,1)S(1)}, bf16[64,2304]{1,0:T(8,128)(2,1)S(1)}, u32[]{:S(2)}, u32[]{:S(2)}) collective-permute-start(bf16[64,2304]{1,0:T(8,128)(2,1)S(1)} %get-tuple-element.121), channel_id=1, source_target_pairs={{0,4},{4,0},{16,20},{20,16},{1,5},{5,1},{17,21},{21,17},{2,6},{6,2... | collective-permute-start | bytes 884744 | tf_op jit(solution)/shard_map/ppermute | solution.py:36
  602.7 34.3 %collective-permute-start.54 = (bf16[64,2304]{1,0:T(8,128)(2,1)}, bf16[64,2304]{1,0:T(8,128)(2,1)}, u32[]{:S(2)}, u32[]{:S(2)}) collective-permute-start(bf16[64,2304]{1,0:T(8,128)(2,1)} %get-tuple-element.116), channel_id=1, source_target_pairs={{0,16},{4,20},{16,0},{20,4},{1,17},{5,21},{17,1},{21,5},{2,18},{6,... | collective-permute-start | bytes 884744 | tf_op jit(solution)/shard_map/ppermute | solution.py:36
  606.0 31.0 %collective-permute-start.56 = (bf16[64,2304]{1,0:T(8,128)(2,1)}, bf16[64,2304]{1,0:T(8,128)(2,1)}, u32[]{:S(2)}, u32[]{:S(2)}) collective-permute-start(bf16[64,2304]{1,0:T(8,128)(2,1)} %get-tuple-element.117), channel_id=1, source_target_pairs={{0,20},{4,16},{16,4},{20,0},{1,21},{5,17},{17,5},{21,1},{2,22},{6,... | collective-permute-start | bytes 884744 | tf_op jit(solution)/shard_map/ppermute | solution.py:36
  627.7 95.7 %collective-permute-start.60 = (bf16[288,2944]{1,0:T(8,128)(2,1)}, bf16[288,2944]{1,0:T(8,128)(2,1)}, u32[]{:S(2)}, u32[]{:S(2)}) collective-permute-start(bf16[288,2944]{1,0:T(8,128)(2,1)} %get-tuple-element.93), channel_id=1, source_target_pairs={{0,8},{8,0},{1,9},{9,1},{2,10},{10,2},{3,11},{11,3},{4,12},{12,4},... | collective-permute-start | bytes 5087240 | tf_op jit(solution)/shard_map/ppermute | solution.py:100
  655.1 125.4 %collective-permute-start.64 = (bf16[288,1792]{1,0:T(8,128)(2,1)}, bf16[288,1792]{1,0:T(8,128)(2,1)}, u32[]{:S(2)}, u32[]{:S(2)}) collective-permute-start(bf16[288,1792]{1,0:T(8,128)(2,1)} %get-tuple-element.95), channel_id=1, source_target_pairs={{0,8},{8,0},{1,9},{9,1},{2,10},{10,2},{3,11},{11,3},{4,12},{12,4},... | collective-permute-start | bytes 3096584 | tf_op jit(solution)/shard_map/ppermute | solution.py:100
  726.0 29.1 %collective-permute-start.63 = (bf16[72,2944]{1,0:T(8,128)(2,1)S(1)}, bf16[72,2944]{1,0:T(8,128)(2,1)S(1)}, u32[]{:S(2)}, u32[]{:S(2)}) collective-permute-start(bf16[72,2944]{1,0:T(8,128)(2,1)S(1)} %get-tuple-element.109), channel_id=1, source_target_pairs={{0,20},{4,16},{16,4},{20,0},{1,21},{5,17},{17,5},{21,1},{2,22},{6,... | collective-permute-start | bytes 1271816 | tf_op jit(solution)/shard_map/ppermute | solution.py:36
  726.1 29.0 %collective-permute-start.62 = (bf16[72,2944]{1,0:T(8,128)(2,1)S(1)}, bf16[72,2944]{1,0:T(8,128)(2,1)S(1)}, u32[]{:S(2)}, u32[]{:S(2)}) collective-permute-start(bf16[72,2944]{1,0:T(8,128)(2,1)S(1)} %get-tuple-element.110), channel_id=1, source_target_pairs={{0,16},{4,20},{16,0},{20,4},{1,17},{5,21},{17,1},{21,5},{2,18},{6,... | collective-permute-start | bytes 1271816 | tf_op jit(solution)/shard_map/ppermute | solution.py:36
  728.0 34.8 %collective-permute-start.61 = (bf16[72,2944]{1,0:T(8,128)(2,1)S(1)}, bf16[72,2944]{1,0:T(8,128)(2,1)S(1)}, u32[]{:S(2)}, u32[]{:S(2)}) collective-permute-start(bf16[72,2944]{1,0:T(8,128)(2,1)S(1)} %get-tuple-element.111), channel_id=1, source_target_pairs={{0,4},{4,0},{16,20},{20,16},{1,5},{5,1},{17,21},{21,17},{2,6},{6,2... | collective-permute-start | bytes 1271816 | tf_op jit(solution)/shard_map/ppermute | solution.py:36
  (142 other events, 1417.7 us)
Sparse Core Ops, SparseCore 0:
  83.2 57.7 all-gather.4
  143.1 29.5 all-gather.6
  207.1 85.5 all-gather.8
  294.7 49.1 all-gather.10
  398.5 61.1 reduce-scatter.4
  462.2 106.5 reduce-scatter.6
  571.4 70.6 reduce-scatter.8
  644.6 34.7 reduce-scatter.10

commit v8 on v7

--- a/solution.py
+++ b/solution.py
@@ -43,11 +43,14 @@
     return lax.optimization_barrier(jnp.concatenate([block] + got, axis=0))
 
 
-def plane_scatter(partial):
+def plane_scatter(partial, *late):
     rows = partial.shape[0] // 4
     total = partial[:rows].astype(F32)
     for k, f in enumerate(FLIPS[1:], 1):
-        total = total + flip_send(partial[k * rows : (k + 1) * rows].astype(BF16), f).astype(F32)
+        got = flip_send(partial[k * rows : (k + 1) * rows].astype(BF16), f)
+        if late:
+            got = after(got, *late)
+        total = total + got.astype(F32)
     return total
 
 
@@ -91,7 +94,7 @@
     return lax.psum_scatter(partial, LINE, scatter_dimension=0, tiled=True)
 
 
-def half_scatter(partial, *late):
+def half_scatter(partial, kind, *late):
     if lax.axis_size("h") == 2:
         rows = partial.shape[0] // 2
         h = lax.axis_index("h")
@@ -100,19 +103,14 @@
         other = lax.ppermute(other, "h", [(0, 1), (1, 0)])
         if late:
             own = after(own, *late)
-        return own.astype(F32) + other.astype(F32)
-    return lax.psum_scatter(partial, "h", scatter_dimension=0, tiled=True).astype(F32)
+        return (own.astype(F32) + other.astype(F32)).astype(kind)
+    return lax.psum_scatter(partial, "h", scatter_dimension=0, tiled=True).astype(kind)
 
 
 def column_block(blocks):
     four, rows, n = blocks.shape
     mine = plane_exchange(blocks)
     return half_gather(mine.reshape(four * rows, n))
-
-
-def column_grad(scattered, rows, *late):
-    mine = half_scatter(scattered, *late).astype(BF16)
-    return plane_exchange(mine.reshape(4, rows, mine.shape[1]))
 
 
 def to_line(tokens, rows):
@@ -335,10 +333,7 @@
         own_branch1.append((BRANCH_SCALE * grad_mid).astype(BF16))
         branch1.append(plane_gather(own_branch1[s]))
 
-    outputs = []
-    for s in range(count):
-        terms = dot(after(mixes[s], gu_terms, *own_branch1), w_down)
-        outputs.append((mids[s] + BRANCH_SCALE * plane_scatter(terms)).astype(BF16))
+    y_terms = [dot(after(mixes[s], gu_terms, *own_branch1), w_down).astype(BF16) for s in range(count)]
 
     grad_qkv = []
     input_grads = []
@@ -368,21 +363,26 @@
     all_attended = after(jnp.concatenate([k[4] for k in kept], axis=0), qkv_terms, gu_part)
     out_terms = dot(all_attended, jnp.concatenate(branch1, axis=0), TN).astype(BF16)
     out_part = line_scatter(out_terms)
+    outputs = []
+    for s in range(count):
+        y_sum = plane_scatter(y_terms[s], out_terms)
+        outputs.append((mids[s] + BRANCH_SCALE * y_sum).astype(BF16))
+
     all_in_terms = [dot(after(g, out_terms), w_qkv, NT).astype(BF16) for g in grad_qkv]
     factor_one = [norm_factor(v) for v in x_float]
-    for s in range(count):
-        grad_norm = plane_scatter(all_in_terms[s])
+
+    def input_grad_of(s, *late):
+        grad_norm = plane_scatter(all_in_terms[s], *late)
         grad_norm = from_line(grad_norm, rows) * gain_one
-        input_grads.append(
-            (grad_mids[s] + norm_back(x_float[s], factor_one[s], grad_norm)).astype(BF16)
-        )
-
-    qkv_part = after(qkv_part, *input_grads)
-    gu_raw = after(column_grad(gu_part, rows, *input_grads), qkv_part)
-    gate_grad, up_grad = lax.optimization_barrier(
-        (join_units(gu_raw[:, :, :hidden]), join_units(gu_raw[:, :, hidden:]))
-    )
-    out_part = after(out_part, gate_grad, up_grad)
+        return (grad_mids[s] + norm_back(x_float[s], factor_one[s], grad_norm)).astype(BF16)
+
+    input_grads = [input_grad_of(s) for s in range(count - 1)]
+    gu_mine = half_scatter(gu_part, BF16, qkv_part, *input_grads)
+    gu_raw = plane_exchange(gu_mine.reshape(4, rows, 2 * hidden))
+    input_grads.append(input_grad_of(count - 1, gu_mine))
+    qkv_mine = half_scatter(qkv_part, BF16, input_grads[-1])
+    qkv_raw = plane_exchange(qkv_mine.reshape(4, rows, 3 * part + spare))
+    out_part = after(out_part, input_grads[-1])
     own = out_part.shape[0] // halves
     if halves == 2:
         h = lax.axis_index("h")
@@ -395,8 +395,13 @@
             for flip in (0, 1)
         )
     else:
-        out_grad = lax.ppermute(half_scatter(out_part), HLXC, [(b, a) for a, b in head_order(0)])
-    qkv_raw = column_grad(qkv_part, rows, gate_grad, up_grad)
+        out_grad = lax.ppermute(
+            half_scatter(out_part, F32), HLXC, [(b, a) for a, b in head_order(0)]
+        )
+    gu_raw = after(gu_raw, qkv_mine)
+    gate_grad, up_grad = lax.optimization_barrier(
+        (join_units(gu_raw[:, :, :hidden]), join_units(gu_raw[:, :, hidden:]))
+    )
 
     gate_grad, up_grad = gate_grad.astype(F32), up_grad.astype(F32)
     ffn_gain_grad = jnp.sum(
@@ -419,7 +424,7 @@
         out_grad,
         gate_grad,
         up_grad,
-        half_scatter(down_part, qkv_part)[:units],
+        half_scatter(down_part, F32, qkv_part)[:units],
         attn_gain_grad,
         ffn_gain_grad,
     )

time: 834 us -> 828 us (level)
  waiting for transfers between devices: 400 us -> 378 us
  starting transfers between devices: 83.6 us -> 92.3 us
    ppermute x60, waiting for transfers between devices: 194 us -> 155 us  [flip_send(): return lax.ppermute(block, PLANE, [(p, p ^ flip) for p in range(4)])]
    reduce_scatter x4, waiting for transfers between devices: 0.01 us -> 12 us  [line_scatter(): return lax.psum_scatter(partial, LINE, scatter_dimension=0, tiled=True)]
    unnamed x181 -> x189, local copies, waits for them, and re-layouts: 22.6 us -> 20.3 us
  transfers between devices with their start and end apart: 79 -> 79, of which waited for: 45 -> 41; matrix products, arithmetic and copies ran while one was open for 35% -> 37% of each run, Pallas kernels for 0% -> 0%
where the time goes in v8:
time: 828 us; the launch traced here: 822 us
  waiting for transfers between devices  378 us (46%)
  local copies, waits for them, and re-layouts  137 us (17%)
  matrix products  124 us (15%)
  starting transfers between devices  92.3 us (11%)
  other arithmetic  73.1 us (9%)
  between operations  16.2 us (2%)
    ppermute x60, waiting for transfers between devices, flip_send(): return lax.ppermute(block, PLANE, [(p, p ^ flip) for p in range(4)])  155 us
    ppermute x2, waiting for transfers between devices, half_gather(): other = lax.ppermute(block, 'h', [(0, 1), (1, 0)])  120 us
    dot_general x21, matrix products, dot(): lax.dot_general(left, right, (contract, ((), ())), preferred_element_type...  117 us
    ppermute x3, waiting for transfers between devices, half_scatter(): other = lax.ppermute(other, 'h', [(0, 1), (1, 0)])  74.7 us
    ppermute x60, starting transfers between devices, flip_send(): return lax.ppermute(block, PLANE, [(p, p ^ flip) for p in range(4)])  71.3 us
    unnamed x189, local copies, waits for them, and re-layouts  20.3 us
    reshape x12, local copies, waits for them, and re-layouts, from_line(): blocks = tokens.reshape(count, 2, 2, -1, 2, 2, rows)  19.9 us
  transfers between devices with their start and end apart: 79, of which 41 were waited for; matrix products, arithmetic and copies ran while one was open for 37% of the time, Pallas kernels for 0%

profile of v8, /device:TPU:0, one launch (start us, length us, event | category | flops | bytes accessed | tf_op | source)
XLA Modules:
  0.0 821.6 jit_solution(5607981666569509505)
XLA Ops:
  21.4 6.5 collective-permute-done.5
  35.9 45.0 %collective-permute-done.6 = bf16[288,1792]{1,0:T(8,128)(2,1)S(1)} collective-permute-done((bf16[288,1792]{1,0:T(8,128)(2,1)S(1)}, bf16[288,1792]{1,0:T(8,128)(2,1)S(1)}, u32[]{:S(2)}, u32[]{:S(2)}) %collective-permute-start.6) | collective-permute-done | bytes 1032224 | tf_op jit(solution)/shard_map/ppermute | solution.py:88
  110.5 7.1 collective-permute-done.9
  117.6 9.7 %collective-permute-done.8 = bf16[72,2944]{1,0:T(8,128)(2,1)S(1)} collective-permute-done((bf16[72,2944]{1,0:T(8,128)(2,1)S(1)}, bf16[72,2944]{1,0:T(8,128)(2,1)S(1)}, u32[]{:S(2)}, u32[]{:S(2)}) %collective-permute-start.8) | collective-permute-done | bytes 423968 | tf_op jit(solution)/shard_map/ppermute | solution.py:36
  129.5 75.0 %collective-permute-done.10 = bf16[288,2944]{1,0:T(8,128)(2,1)S(1)} collective-permute-done((bf16[288,2944]{1,0:T(8,128)(2,1)S(1)}, bf16[288,2944]{1,0:T(8,128)(2,1)S(1)}, u32[]{:S(2)}, u32[]{:S(2)}) %collective-permute-start.10) | collective-permute-done | bytes 1695776 | tf_op jit(solution)/shard_map/ppermute | solution.py:88
  231.6 9.5 %collective-permute-done.22 = bf16[64,2304]{1,0:T(8,128)(2,1)S(1)} collective-permute-done((bf16[64,2304]{1,0:T(8,128)(2,1)S(1)}, bf16[64,2304]{1,0:T(8,128)(2,1)S(1)}, u32[]{:S(2)}, u32[]{:S(2)}) %collective-permute-start.22) | collective-permute-done | bytes 294944 | tf_op jit(solution)/shard_map/ppermute | solution.py:36
  262.2 7.0 fusion.176
  303.4 9.7 %collective-permute-done.23 = bf16[64,2304]{1,0:T(8,128)(2,1)S(1)} collective-permute-done((bf16[64,2304]{1,0:T(8,128)(2,1)S(1)}, bf16[64,2304]{1,0:T(8,128)(2,1)S(1)}, u32[]{:S(2)}, u32[]{:S(2)}) %collective-permute-start.23) | collective-permute-done | bytes 294944 | tf_op jit(solution)/shard_map/ppermute | solution.py:36
  364.0 6.5 collective-permute-done.28
  374.8 7.6 fusion.175
  401.6 7.9 multiply_convert_fusion.1
  415.2 7.3 convolution_convert_fusion.9
  422.6 8.8 %convolution_convert_fusion.8 = bf16[256,2304]{1,0:T(8,128)(2,1)} fusion(bf16[256,2944]{1,0:T(8,128)(2,1)S(1)} %pad_maximum_fusion.5, bf16[2304,2944]{1,0:T(8,128)(2,1)} %all-gather.9.cloned.1.call-done), kind=kOutput, calls=%fused_computation.10 | convolution fusion | flops 3473473536 | bytes 16252928 | tf_op jit(solution)/shard_map/dot_general | solution.py:28
  431.4 10.1 %convolution_convert_fusion = bf16[2304,2944]{1,0:T(8,128)(2,1)} fusion(bf16[512,2304]{1,0:T(8,128)(2,1)S(1)} %copy-done.24, bf16[256,2944]{1,0:T(8,128)(2,1)S(1)} %pad_maximum_fusion.5, bf16[256,2944]{1,0:T(8,128)(2,1)S(1)} %pad_maximum_fusion.4), kind=kOutput, calls=%fused_computation.2 | convolution fusion | flops 6958579712 | bytes 18939904 | tf_op jit(solution)/shard_map/dot_general | solution.py:28
  449.0 12.9 %collective-permute-done.39 = bf16[64,2304]{1,0:T(8,128)(2,1)S(1)} collective-permute-done((bf16[64,2304]{1,0:T(8,128)(2,1)S(1)}, bf16[64,2304]{1,0:T(8,128)(2,1)S(1)}, u32[]{:S(2)}, u32[]{:S(2)}) %collective-permute-start.39) | collective-permute-done | bytes 294944 | tf_op jit(solution)/shard_map/ppermute | solution.py:36
  531.6 6.8 convolution_convert_fusion.1
  561.8 7.4 reduce-scatter.7.cloned.1.call-done
  578.1 7.3 convolution_convert_fusion.4
  603.3 6.3 collective-permute-start.60
  609.6 12.1 %collective-permute-done.56 = bf16[64,2304]{1,0:T(8,128)(2,1)S(1)} collective-permute-done((bf16[64,2304]{1,0:T(8,128)(2,1)S(1)}, bf16[64,2304]{1,0:T(8,128)(2,1)S(1)}, u32[]{:S(2)}, u32[]{:S(2)}) %collective-permute-start.56) | collective-permute-done | bytes 294944 | tf_op jit(solution)/shard_map/ppermute | solution.py:36
  650.4 74.7 %collective-permute-done.58 = bf16[288,2944]{1,0:T(8,128)(2,1)} collective-permute-done((bf16[288,2944]{1,0:T(8,128)(2,1)}, bf16[288,2944]{1,0:T(8,128)(2,1)}, u32[]{:S(2)}, u32[]{:S(2)}) %collective-permute-start.58) | collective-permute-done | bytes 1695776 | tf_op jit(solution)/shard_map/ppermute | solution.py:103
  741.8 12.6 %collective-permute-done.69 = bf16[72,2944]{1,0:T(8,128)(2,1)S(1)} collective-permute-done((bf16[72,2944]{1,0:T(8,128)(2,1)S(1)}, bf16[72,2944]{1,0:T(8,128)(2,1)S(1)}, u32[]{:S(2)}, u32[]{:S(2)}) %collective-permute-start.69) | collective-permute-done | bytes 423968 | tf_op jit(solution)/shard_map/ppermute | solution.py:36
  756.2 6.4 collective-permute-done.67
  800.0 13.6 %collective-permute-done.66 = bf16[72,2304]{1,0:T(8,128)(2,1)S(1)} collective-permute-done((bf16[72,2304]{1,0:T(8,128)(2,1)S(1)}, bf16[72,2304]{1,0:T(8,128)(2,1)S(1)}, u32[]{:S(2)}, u32[]{:S(2)}) %collective-permute-start.66) | collective-permute-done | bytes 331808 | tf_op jit(solution)/shard_map/ppermute | solution.py:390
  (562 shorter events, 427.7 us)
Async XLA Ops:
  7.2 240.1 %all-gather.5.cloned.1.call-start = ((), (), s32[]{:S(2)}) async-start(), calls=%async_computation.4 | async-start | bytes 10321920 | tf_op jit(solution)/shard_map/all_gather | solution.py:75
  33.2 47.7 %collective-permute-start.6 = (bf16[288,1792]{1,0:T(8,128)(2,1)S(1)}, bf16[288,1792]{1,0:T(8,128)(2,1)S(1)}, u32[]{:S(2)}, u32[]{:S(2)}) collective-permute-start(bf16[288,1792]{1,0:T(8,128)(2,1)S(1)} %bitcast.287), channel_id=1, source_target_pairs={{0,8},{8,0},{1,9},{9,1},{2,10},{10,2},{3,11},{11,3},{4,12},{12,4},... | collective-permute-start | bytes 3096584 | tf_op jit(solution)/shard_map/ppermute | solution.py:88
  83.1 207.3 %all-gather.7.cloned.1.call-start = ((), (), s32[]{:S(2)}) async-start(), calls=%async_computation.5 | async-start | bytes 3317760 | tf_op jit(solution)/shard_map/all_gather | solution.py:75
  83.1 25.0 %collective-permute-start.13 = (bf16[72,2304]{1,0:T(8,128)(2,1)}, bf16[72,2304]{1,0:T(8,128)(2,1)}, u32[]{:S(2)}, u32[]{:S(2)}) collective-permute-start(bf16[72,2304]{1,0:T(8,128)(2,1)} %param.17), channel_id=1, source_target_pairs={{0,8},{2,9},{4,10},{6,11},{8,12},{10,13},{12,14},{14,15},{1,0},{3,... | collective-permute-start | bytes 995336 | tf_op jit(solution)/shard_map/ppermute | solution.py:217
  83.2 24.9 %collective-permute-start.12 = (bf16[72,2304]{1,0:T(8,128)(2,1)}, bf16[72,2304]{1,0:T(8,128)(2,1)}, u32[]{:S(2)}, u32[]{:S(2)}) collective-permute-start(bf16[72,2304]{1,0:T(8,128)(2,1)} %param.17), channel_id=1, source_target_pairs={{0,0},{2,1},{4,2},{6,3},{8,4},{10,5},{12,6},{14,7},{1,8},{3,9},{5,... | collective-permute-start | bytes 995336 | tf_op jit(solution)/shard_map/ppermute | solution.py:217
  110.4 264.4 %all-gather.9.cloned.1.call-start = ((), (), s32[]{:S(2)}) async-start(), calls=%async_computation.6 | async-start | bytes 16957440 | tf_op jit(solution)/shard_map/all_gather | solution.py:75
  128.1 76.5 %collective-permute-start.10 = (bf16[288,2944]{1,0:T(8,128)(2,1)S(1)}, bf16[288,2944]{1,0:T(8,128)(2,1)S(1)}, u32[]{:S(2)}, u32[]{:S(2)}) collective-permute-start(bf16[288,2944]{1,0:T(8,128)(2,1)S(1)} %bitcast.279), channel_id=1, source_target_pairs={{0,8},{8,0},{1,9},{9,1},{2,10},{10,2},{3,11},{11,3},{4,12},{12,4},... | collective-permute-start | bytes 5087240 | tf_op jit(solution)/shard_map/ppermute | solution.py:88
  207.0 194.6 %all-gather.11.cloned.1.call-start = ((), (), s32[]{:S(2)}) async-start(), calls=%async_computation.7 | async-start | bytes 8478720 | tf_op jit(solution)/shard_map/all_gather | solution.py:75
  216.2 24.9 %collective-permute-start.22 = (bf16[64,2304]{1,0:T(8,128)(2,1)S(1)}, bf16[64,2304]{1,0:T(8,128)(2,1)S(1)}, u32[]{:S(2)}, u32[]{:S(2)}) collective-permute-start(bf16[64,2304]{1,0:T(8,128)(2,1)S(1)} %reshape.455), channel_id=1, source_target_pairs={{0,20},{4,16},{16,4},{20,0},{1,21},{5,17},{17,5},{21,1},{2,22},{6,... | collective-permute-start | bytes 884744 | tf_op jit(solution)/shard_map/ppermute | solution.py:36
  229.3 54.9 %collective-permute-start.35 = (bf16[184,2304]{1,0:T(8,128)(2,1)}, bf16[184,2304]{1,0:T(8,128)(2,1)}, u32[]{:S(2)}, u32[]{:S(2)}) collective-permute-start(bf16[184,2304]{1,0:T(8,128)(2,1)} %pad.20), channel_id=1, source_target_pairs={{0,8},{8,0},{1,9},{9,1},{2,10},{10,2},{3,11},{11,3},{4,12},{12,4},... | collective-permute-start | bytes 2543624 | tf_op jit(solution)/shard_map/ppermute | solution.py:232
  287.7 222.5 %reduce-scatter.5.cloned.1.call-start = ((), (), s32[]{:S(2)}) async-start(), calls=%async_computation.8 | async-start | bytes 8478720 | tf_op jit(solution)/shard_map/reduce_scatter | solution.py:94
  325.3 25.5 %collective-permute-start.30 = (bf16[64,2304]{1,0:T(8,128)(2,1)}, bf16[64,2304]{1,0:T(8,128)(2,1)}, u32[]{:S(2)}, u32[]{:S(2)}) collective-permute-start(bf16[64,2304]{1,0:T(8,128)(2,1)} %get-tuple-element.179), channel_id=1, source_target_pairs={{0,4},{4,0},{16,20},{20,16},{1,5},{5,1},{17,21},{21,17},{2,6},{6,2... | collective-permute-start | bytes 884744 | tf_op jit(solution)/shard_map/ppermute | solution.py:36
  398.7 170.5 %reduce-scatter.7.cloned.1.call-start = ((), (), s32[]{:S(2)}) async-start(), calls=%async_computation.9 | async-start | bytes 16957440 | tf_op jit(solution)/shard_map/reduce_scatter | solution.py:94
  441.5 200.9 %reduce-scatter.9.cloned.1.call-start = ((), (), s32[]{:S(2)}) async-start(), calls=%async_computation.10 | async-start | bytes 10321920 | tf_op jit(solution)/shard_map/reduce_scatter | solution.py:94
  538.4 254.4 %reduce-scatter.11.cloned.1.call-start = ((), (), s32[]{:S(2)}) async-start(), calls=%async_computation.11 | async-start | bytes 3317760 | tf_op jit(solution)/shard_map/reduce_scatter | solution.py:94
  550.7 26.9 %collective-permute-start.52 = (bf16[64,2304]{1,0:T(8,128)(2,1)S(1)}, bf16[64,2304]{1,0:T(8,128)(2,1)}, u32[]{:S(2)}, u32[]{:S(2)}) collective-permute-start(bf16[64,2304]{1,0:T(8,128)(2,1)S(1)} %get-tuple-element.142), channel_id=1, source_target_pairs={{0,4},{4,0},{16,20},{20,16},{1,5},{5,1},{17,21},{21,17},{2,6},{6,2... | collective-permute-start | bytes 884744 | tf_op jit(solution)/shard_map/ppermute | solution.py:36
  575.2 70.3 %collective-permute-start.70 = (bf16[184,2304]{1,0:T(8,128)(2,1)}, bf16[184,2304]{1,0:T(8,128)(2,1)}, u32[]{:S(2)}, u32[]{:S(2)}) collective-permute-start(bf16[184,2304]{1,0:T(8,128)(2,1)} %get-tuple-element.120), channel_id=1, source_target_pairs={{0,8},{8,0},{1,9},{9,1},{2,10},{10,2},{3,11},{11,3},{4,12},{12,4},... | collective-permute-start | bytes 2543624 | tf_op jit(solution)/shard_map/ppermute | solution.py:103
  586.3 141.8 %collective-permute-start.57 = (bf16[64,2304]{1,0:T(8,128)(2,1)}, bf16[64,2304]{1,0:T(8,128)(2,1)}, u32[]{:S(2)}, u32[]{:S(2)}) collective-permute-start(bf16[64,2304]{1,0:T(8,128)(2,1)} %get-tuple-element.131), channel_id=1, source_target_pairs={{0,16},{4,20},{16,0},{20,4},{1,17},{5,21},{17,1},{21,5},{2,18},{6,... | collective-permute-start | bytes 884744 | tf_op jit(solution)/shard_map/ppermute | solution.py:36
  594.5 27.2 %collective-permute-start.56 = (bf16[64,2304]{1,0:T(8,128)(2,1)S(1)}, bf16[64,2304]{1,0:T(8,128)(2,1)S(1)}, u32[]{:S(2)}, u32[]{:S(2)}) collective-permute-start(bf16[64,2304]{1,0:T(8,128)(2,1)S(1)} %get-tuple-element.135), channel_id=1, source_target_pairs={{0,20},{4,16},{16,4},{20,0},{1,21},{5,17},{17,5},{21,1},{2,22},{6,... | collective-permute-start | bytes 884744 | tf_op jit(solution)/shard_map/ppermute | solution.py:36
  596.3 31.0 %collective-permute-start.55 = (bf16[64,2304]{1,0:T(8,128)(2,1)S(1)}, bf16[64,2304]{1,0:T(8,128)(2,1)S(1)}, u32[]{:S(2)}, u32[]{:S(2)}) collective-permute-start(bf16[64,2304]{1,0:T(8,128)(2,1)S(1)} %get-tuple-element.136), channel_id=1, source_target_pairs={{0,4},{4,0},{16,20},{20,16},{1,5},{5,1},{17,21},{21,17},{2,6},{6,2... | collective-permute-start | bytes 884744 | tf_op jit(solution)/shard_map/ppermute | solution.py:36
  603.3 124.8 %collective-permute-start.60 = (bf16[64,2304]{1,0:T(8,128)(2,1)}, bf16[64,2304]{1,0:T(8,128)(2,1)}, u32[]{:S(2)}, u32[]{:S(2)}) collective-permute-start(bf16[64,2304]{1,0:T(8,128)(2,1)} %get-tuple-element.132), channel_id=1, source_target_pairs={{0,20},{4,16},{16,4},{20,0},{1,21},{5,17},{17,5},{21,1},{2,22},{6,... | collective-permute-start | bytes 884744 | tf_op jit(solution)/shard_map/ppermute | solution.py:36
  621.7 106.4 %collective-permute-start.59 = (bf16[64,2304]{1,0:T(8,128)(2,1)}, bf16[64,2304]{1,0:T(8,128)(2,1)}, u32[]{:S(2)}, u32[]{:S(2)}) collective-permute-start(bf16[64,2304]{1,0:T(8,128)(2,1)} %get-tuple-element.133), channel_id=1, source_target_pairs={{0,4},{4,0},{16,20},{20,16},{1,5},{5,1},{17,21},{21,17},{2,6},{6,2... | collective-permute-start | bytes 884744 | tf_op jit(solution)/shard_map/ppermute | solution.py:36
  627.3 97.8 %collective-permute-start.58 = (bf16[288,2944]{1,0:T(8,128)(2,1)}, bf16[288,2944]{1,0:T(8,128)(2,1)}, u32[]{:S(2)}, u32[]{:S(2)}) collective-permute-start(bf16[288,2944]{1,0:T(8,128)(2,1)} %get-tuple-element.108), channel_id=1, source_target_pairs={{0,8},{8,0},{1,9},{9,1},{2,10},{10,2},{3,11},{11,3},{4,12},{12,4},... | collective-permute-start | bytes 5087240 | tf_op jit(solution)/shard_map/ppermute | solution.py:103
  645.5 117.9 %collective-permute-start.61 = (bf16[288,1792]{1,0:T(8,128)(2,1)}, bf16[288,1792]{1,0:T(8,128)(2,1)}, u32[]{:S(2)}, u32[]{:S(2)}) collective-permute-start(bf16[288,1792]{1,0:T(8,128)(2,1)} %get-tuple-element.110), channel_id=1, source_target_pairs={{0,8},{8,0},{1,9},{9,1},{2,10},{10,2},{3,11},{11,3},{4,12},{12,4},... | collective-permute-start | bytes 3096584 | tf_op jit(solution)/shard_map/ppermute | solution.py:103
  (146 other events, 1308.9 us)
Sparse Core Ops, SparseCore 0:
  83.2 57.7 all-gather.4
  143.1 29.5 all-gather.6
  207.1 85.5 all-gather.8
  294.7 49.1 all-gather.10
  398.8 61.1 reduce-scatter.4
  462.6 106.5 reduce-scatter.6
  571.8 70.5 reduce-scatter.8
  645.0 34.7 reduce-scatter.10

commit v9 on v8

--- a/solution.py
+++ b/solution.py
@@ -333,8 +333,6 @@
         own_branch1.append((BRANCH_SCALE * grad_mid).astype(BF16))
         branch1.append(plane_gather(own_branch1[s]))
 
-    y_terms = [dot(after(mixes[s], gu_terms, *own_branch1), w_down).astype(BF16) for s in range(count)]
-
     grad_qkv = []
     input_grads = []
     for s in range(count):
@@ -360,29 +358,29 @@
     all_grads = jnp.concatenate(grad_qkv, axis=0)
     qkv_terms = dot(all_normed, all_grads, TN).astype(BF16)
     qkv_part = line_scatter(qkv_terms)
+    all_in_terms = [dot(after(g, qkv_terms), w_qkv, NT).astype(BF16) for g in grad_qkv]
     all_attended = after(jnp.concatenate([k[4] for k in kept], axis=0), qkv_terms, gu_part)
     out_terms = dot(all_attended, jnp.concatenate(branch1, axis=0), TN).astype(BF16)
     out_part = line_scatter(out_terms)
-    outputs = []
-    for s in range(count):
-        y_sum = plane_scatter(y_terms[s], out_terms)
-        outputs.append((mids[s] + BRANCH_SCALE * y_sum).astype(BF16))
-
-    all_in_terms = [dot(after(g, out_terms), w_qkv, NT).astype(BF16) for g in grad_qkv]
     factor_one = [norm_factor(v) for v in x_float]
 
-    def input_grad_of(s, *late):
-        grad_norm = plane_scatter(all_in_terms[s], *late)
+    input_grads = []
+    for s in range(count):
+        grad_norm = plane_scatter(all_in_terms[s], gu_part)
         grad_norm = from_line(grad_norm, rows) * gain_one
-        return (grad_mids[s] + norm_back(x_float[s], factor_one[s], grad_norm)).astype(BF16)
-
-    input_grads = [input_grad_of(s) for s in range(count - 1)]
+        input_grads.append(
+            (grad_mids[s] + norm_back(x_float[s], factor_one[s], grad_norm)).astype(BF16)
+        )
+    y_terms = [dot(after(m, out_terms), w_down).astype(BF16) for m in mixes]
     gu_mine = half_scatter(gu_part, BF16, qkv_part, *input_grads)
     gu_raw = plane_exchange(gu_mine.reshape(4, rows, 2 * hidden))
-    input_grads.append(input_grad_of(count - 1, gu_mine))
-    qkv_mine = half_scatter(qkv_part, BF16, input_grads[-1])
+    outputs = []
+    for s in range(count):
+        y_sum = plane_scatter(y_terms[s], gu_raw)
+        outputs.append((mids[s] + BRANCH_SCALE * y_sum).astype(BF16))
+    qkv_mine = half_scatter(qkv_part, BF16, gu_mine)
     qkv_raw = plane_exchange(qkv_mine.reshape(4, rows, 3 * part + spare))
-    out_part = after(out_part, input_grads[-1])
+    out_part = after(out_part, gu_mine)
     own = out_part.shape[0] // halves
     if halves == 2:
         h = lax.axis_index("h")

time: 828 us -> 822 us (level)
    reduce_scatter x4, waiting for transfers between devices: 12 us -> 26.4 us  [line_scatter(): return lax.psum_scatter(partial, LINE, scatter_dimension=0, tiled=True)]
    ppermute x3, waiting for transfers between devices: 74.7 us -> 65 us  [half_scatter(): other = lax.ppermute(other, 'h', [(0, 1), (1, 0)])]
    unnamed x189 -> x205, local copies, waits for them, and re-layouts: 20.3 us -> 21.5 us
  transfers between devices with their start and end apart: 79 -> 79, of which waited for: 41 -> 42; matrix products, arithmetic and copies ran while one was open for 37% -> 36% of each run, Pallas kernels for 0% -> 0%
where the time goes in v9:
time: 822 us; the launch traced here: 814 us
  waiting for transfers between devices  383 us (47%)
  local copies, waits for them, and re-layouts  132 us (16%)
  matrix products  125 us (15%)
  starting transfers between devices  86 us (10%)
  other arithmetic  71 us (9%)
  between operations  16.2 us (2%)
    ppermute x60, waiting for transfers between devices, flip_send(): return lax.ppermute(block, PLANE, [(p, p ^ flip) for p in range(4)])  157 us
    ppermute x2, waiting for transfers between devices, half_gather(): other = lax.ppermute(block, 'h', [(0, 1), (1, 0)])  120 us
    dot_general x21, matrix products, dot(): lax.dot_general(left, right, (contract, ((), ())), preferred_element_type...  117 us
    ppermute x60, starting transfers between devices, flip_send(): return lax.ppermute(block, PLANE, [(p, p ^ flip) for p in range(4)])  67.2 us
    ppermute x3, waiting for transfers between devices, half_scatter(): other = lax.ppermute(other, 'h', [(0, 1), (1, 0)])  65 us
    reduce_scatter x4, waiting for transfers between devices, line_scatter(): return lax.psum_scatter(partial, LINE, scatter_dimension=0, tiled=True)  26.4 us
    unnamed x205, local copies, waits for them, and re-layouts  21.5 us
    reshape x12, local copies, waits for them, and re-layouts, from_line(): blocks = tokens.reshape(count, 2, 2, -1, 2, 2, rows)  21.4 us
  transfers between devices with their start and end apart: 79, of which 42 were waited for; matrix products, arithmetic and copies ran while one was open for 36% of the time, Pallas kernels for 0%

profile of v9, /device:TPU:0, one launch (start us, length us, event | category | flops | bytes accessed | tf_op | source)
XLA Modules:
  0.0 814.0 jit_solution(11796603029815999321)
XLA Ops:
  21.4 6.5 collective-permute-done.5
  35.9 45.0 %collective-permute-done.6 = bf16[288,1792]{1,0:T(8,128)(2,1)S(1)} collective-permute-done((bf16[288,1792]{1,0:T(8,128)(2,1)S(1)}, bf16[288,1792]{1,0:T(8,128)(2,1)S(1)}, u32[]{:S(2)}, u32[]{:S(2)}) %collective-permute-start.6) | collective-permute-done | bytes 1032224 | tf_op jit(solution)/shard_map/ppermute | solution.py:88
  110.3 7.3 collective-permute-done.9
  117.6 9.7 %collective-permute-done.8 = bf16[72,2944]{1,0:T(8,128)(2,1)S(1)} collective-permute-done((bf16[72,2944]{1,0:T(8,128)(2,1)S(1)}, bf16[72,2944]{1,0:T(8,128)(2,1)S(1)}, u32[]{:S(2)}, u32[]{:S(2)}) %collective-permute-start.8) | collective-permute-done | bytes 423968 | tf_op jit(solution)/shard_map/ppermute | solution.py:36
  129.6 75.0 %collective-permute-done.10 = bf16[288,2944]{1,0:T(8,128)(2,1)S(1)} collective-permute-done((bf16[288,2944]{1,0:T(8,128)(2,1)S(1)}, bf16[288,2944]{1,0:T(8,128)(2,1)S(1)}, u32[]{:S(2)}, u32[]{:S(2)}) %collective-permute-start.10) | collective-permute-done | bytes 1695776 | tf_op jit(solution)/shard_map/ppermute | solution.py:88
  232.6 8.6 %collective-permute-done.22 = bf16[64,2304]{1,0:T(8,128)(2,1)S(1)} collective-permute-done((bf16[64,2304]{1,0:T(8,128)(2,1)S(1)}, bf16[64,2304]{1,0:T(8,128)(2,1)S(1)}, u32[]{:S(2)}, u32[]{:S(2)}) %collective-permute-start.22) | collective-permute-done | bytes 294944 | tf_op jit(solution)/shard_map/ppermute | solution.py:36
  250.8 7.4 fusion.174
  262.2 7.4 fusion.176
  302.9 9.4 %collective-permute-done.24 = bf16[64,2304]{1,0:T(8,128)(2,1)S(1)} collective-permute-done((bf16[64,2304]{1,0:T(8,128)(2,1)S(1)}, bf16[64,2304]{1,0:T(8,128)(2,1)S(1)}, u32[]{:S(2)}, u32[]{:S(2)}) %collective-permute-start.24) | collective-permute-done | bytes 294944 | tf_op jit(solution)/shard_map/ppermute | solution.py:36
  363.7 6.5 collective-permute-done.31
  374.6 7.6 fusion.175
  401.4 8.0 multiply_convert_fusion.1
  414.8 7.3 convolution_convert_fusion.9
  422.1 8.8 %convolution_convert_fusion.8 = bf16[256,2304]{1,0:T(8,128)(2,1)} fusion(bf16[256,2944]{1,0:T(8,128)(2,1)S(1)} %pad_maximum_fusion.5, bf16[2304,2944]{1,0:T(8,128)(2,1)} %all-gather.9.cloned.1.call-done), kind=kOutput, calls=%fused_computation.10 | convolution fusion | flops 3473473536 | bytes 16252928 | tf_op jit(solution)/shard_map/dot_general | solution.py:28
  430.9 10.1 %convolution_convert_fusion = bf16[2304,2944]{1,0:T(8,128)(2,1)} fusion(bf16[512,2304]{1,0:T(8,128)(2,1)S(1)} %copy-done.26, bf16[256,2944]{1,0:T(8,128)(2,1)S(1)} %pad_maximum_fusion.5, bf16[256,2944]{1,0:T(8,128)(2,1)S(1)} %pad_maximum_fusion.4), kind=kOutput, calls=%fused_computation.2 | convolution fusion | flops 6958579712 | bytes 18939904 | tf_op jit(solution)/shard_map/dot_general | solution.py:28
  448.6 13.1 %collective-permute-done.42 = bf16[64,2304]{1,0:T(8,128)(2,1)S(1)} collective-permute-done((bf16[64,2304]{1,0:T(8,128)(2,1)S(1)}, bf16[64,2304]{1,0:T(8,128)(2,1)S(1)}, u32[]{:S(2)}, u32[]{:S(2)}) %collective-permute-start.42) | collective-permute-done | bytes 294944 | tf_op jit(solution)/shard_map/ppermute | solution.py:36
  532.0 6.7 convolution_convert_fusion.1
  620.7 21.5 %reduce-scatter.9.cloned.1.call-done = bf16[576,1792]{1,0:T(8,128)(2,1)} async-done(((bf16[2304,1792]{1,0:T(8,128)(2,1)}), bf16[576,1792]{1,0:T(8,128)(2,1)}) %reduce-scatter.9.cloned.1.call-update) | async-done | bytes 2064400 | tf_op jit(solution)/shard_map/reduce_scatter | solution.py:94
  642.1 45.0 %collective-permute-done.55 = bf16[288,2944]{1,0:T(8,128)(2,1)} collective-permute-done((bf16[288,2944]{1,0:T(8,128)(2,1)}, bf16[288,2944]{1,0:T(8,128)(2,1)}, u32[]{:S(2)}, u32[]{:S(2)}) %collective-permute-start.55) | collective-permute-done | bytes 1695776 | tf_op jit(solution)/shard_map/ppermute | solution.py:103
  696.0 7.3 collective-permute-done.58
  703.4 6.4 collective-permute-done.57
  719.4 17.1 %collective-permute-done.60 = bf16[64,2304]{1,0:T(8,128)(2,1)S(1)} collective-permute-done((bf16[64,2304]{1,0:T(8,128)(2,1)S(1)}, bf16[64,2304]{1,0:T(8,128)(2,1)S(1)}, u32[]{:S(2)}, u32[]{:S(2)}) %collective-permute-start.60) | collective-permute-done | bytes 294944 | tf_op jit(solution)/shard_map/ppermute | solution.py:36
  743.3 20.0 %collective-permute-done.64 = bf16[288,1792]{1,0:T(8,128)(2,1)S(1)} collective-permute-done((bf16[288,1792]{1,0:T(8,128)(2,1)S(1)}, bf16[288,1792]{1,0:T(8,128)(2,1)S(1)}, u32[]{:S(2)}, u32[]{:S(2)}) %collective-permute-start.64) | collective-permute-done | bytes 1032224 | tf_op jit(solution)/shard_map/ppermute | solution.py:103
  795.7 10.3 %collective-permute-done.69 = bf16[72,2304]{1,0:T(8,128)(2,1)S(1)} collective-permute-done((bf16[72,2304]{1,0:T(8,128)(2,1)S(1)}, bf16[72,2304]{1,0:T(8,128)(2,1)S(1)}, u32[]{:S(2)}, u32[]{:S(2)}) %collective-permute-start.69) | collective-permute-done | bytes 331808 | tf_op jit(solution)/shard_map/ppermute | solution.py:388
  (576 shorter events, 425.7 us)
Async XLA Ops:
  7.2 240.1 %all-gather.5.cloned.1.call-start = ((), (), s32[]{:S(2)}) async-start(), calls=%async_computation.4 | async-start | bytes 10321920 | tf_op jit(solution)/shard_map/all_gather | solution.py:75
  33.2 47.7 %collective-permute-start.6 = (bf16[288,1792]{1,0:T(8,128)(2,1)S(1)}, bf16[288,1792]{1,0:T(8,128)(2,1)S(1)}, u32[]{:S(2)}, u32[]{:S(2)}) collective-permute-start(bf16[288,1792]{1,0:T(8,128)(2,1)S(1)} %bitcast.287), channel_id=1, source_target_pairs={{0,8},{8,0},{1,9},{9,1},{2,10},{10,2},{3,11},{11,3},{4,12},{12,4},... | collective-permute-start | bytes 3096584 | tf_op jit(solution)/shard_map/ppermute | solution.py:88
  83.1 206.9 %all-gather.7.cloned.1.call-start = ((), (), s32[]{:S(2)}) async-start(), calls=%async_computation.5 | async-start | bytes 3317760 | tf_op jit(solution)/shard_map/all_gather | solution.py:75
  83.1 25.0 %collective-permute-start.13 = (bf16[72,2304]{1,0:T(8,128)(2,1)}, bf16[72,2304]{1,0:T(8,128)(2,1)S(1)}, u32[]{:S(2)}, u32[]{:S(2)}) collective-permute-start(bf16[72,2304]{1,0:T(8,128)(2,1)} %param.17), channel_id=1, source_target_pairs={{0,8},{2,9},{4,10},{6,11},{8,12},{10,13},{12,14},{14,15},{1,0},{3,... | collective-permute-start | bytes 995336 | tf_op jit(solution)/shard_map/ppermute | solution.py:217
  83.2 24.9 %collective-permute-start.12 = (bf16[72,2304]{1,0:T(8,128)(2,1)}, bf16[72,2304]{1,0:T(8,128)(2,1)}, u32[]{:S(2)}, u32[]{:S(2)}) collective-permute-start(bf16[72,2304]{1,0:T(8,128)(2,1)} %param.17), channel_id=1, source_target_pairs={{0,0},{2,1},{4,2},{6,3},{8,4},{10,5},{12,6},{14,7},{1,8},{3,9},{5,... | collective-permute-start | bytes 995336 | tf_op jit(solution)/shard_map/ppermute | solution.py:217
  110.2 264.4 %all-gather.9.cloned.1.call-start = ((), (), s32[]{:S(2)}) async-start(), calls=%async_computation.6 | async-start | bytes 16957440 | tf_op jit(solution)/shard_map/all_gather | solution.py:75
  128.1 76.5 %collective-permute-start.10 = (bf16[288,2944]{1,0:T(8,128)(2,1)S(1)}, bf16[288,2944]{1,0:T(8,128)(2,1)S(1)}, u32[]{:S(2)}, u32[]{:S(2)}) collective-permute-start(bf16[288,2944]{1,0:T(8,128)(2,1)S(1)} %bitcast.278), channel_id=1, source_target_pairs={{0,8},{8,0},{1,9},{9,1},{2,10},{10,2},{3,11},{11,3},{4,12},{12,4},... | collective-permute-start | bytes 5087240 | tf_op jit(solution)/shard_map/ppermute | solution.py:88
  207.0 194.3 %all-gather.11.cloned.1.call-start = ((), (), s32[]{:S(2)}) async-start(), calls=%async_computation.7 | async-start | bytes 8478720 | tf_op jit(solution)/shard_map/all_gather | solution.py:75
  216.2 24.9 %collective-permute-start.22 = (bf16[64,2304]{1,0:T(8,128)(2,1)S(1)}, bf16[64,2304]{1,0:T(8,128)(2,1)S(1)}, u32[]{:S(2)}, u32[]{:S(2)}) collective-permute-start(bf16[64,2304]{1,0:T(8,128)(2,1)S(1)} %reshape.455), channel_id=1, source_target_pairs={{0,20},{4,16},{16,4},{20,0},{1,21},{5,17},{17,5},{21,1},{2,22},{6,... | collective-permute-start | bytes 884744 | tf_op jit(solution)/shard_map/ppermute | solution.py:36
  229.3 54.2 %collective-permute-start.35 = (bf16[184,2304]{1,0:T(8,128)(2,1)}, bf16[184,2304]{1,0:T(8,128)(2,1)}, u32[]{:S(2)}, u32[]{:S(2)}) collective-permute-start(bf16[184,2304]{1,0:T(8,128)(2,1)} %pad.20), channel_id=1, source_target_pairs={{0,8},{8,0},{1,9},{9,1},{2,10},{10,2},{3,11},{11,3},{4,12},{12,4},... | collective-permute-start | bytes 2543624 | tf_op jit(solution)/shard_map/ppermute | solution.py:232
  287.1 223.5 %reduce-scatter.5.cloned.1.call-start = ((), (), s32[]{:S(2)}) async-start(), calls=%async_computation.8 | async-start | bytes 8478720 | tf_op jit(solution)/shard_map/reduce_scatter | solution.py:94
  324.9 25.5 %collective-permute-start.27 = (bf16[64,2304]{1,0:T(8,128)(2,1)}, bf16[64,2304]{1,0:T(8,128)(2,1)}, u32[]{:S(2)}, u32[]{:S(2)}) collective-permute-start(bf16[64,2304]{1,0:T(8,128)(2,1)} %get-tuple-element.190), channel_id=1, source_target_pairs={{0,4},{4,0},{16,20},{20,16},{1,5},{5,1},{17,21},{21,17},{2,6},{6,2... | collective-permute-start | bytes 884744 | tf_op jit(solution)/shard_map/ppermute | solution.py:36
  338.5 24.5 %collective-permute-start.18 = (bf16[64,2304]{1,0:T(8,128)(2,1)S(1)}, bf16[64,2304]{1,0:T(8,128)(2,1)S(1)}, u32[]{:S(2)}, u32[]{:S(2)}) collective-permute-start(bf16[64,2304]{1,0:T(8,128)(2,1)S(1)} %reshape.454), channel_id=1, source_target_pairs={{0,4},{4,0},{16,20},{20,16},{1,5},{5,1},{17,21},{21,17},{2,6},{6,2... | collective-permute-start | bytes 884744 | tf_op jit(solution)/shard_map/ppermute | solution.py:36
  398.5 170.4 %reduce-scatter.7.cloned.1.call-start = ((), (), s32[]{:S(2)}) async-start(), calls=%async_computation.9 | async-start | bytes 16957440 | tf_op jit(solution)/shard_map/reduce_scatter | solution.py:94
  441.1 201.1 %reduce-scatter.9.cloned.1.call-start = ((), (), s32[]{:S(2)}) async-start(), calls=%async_computation.10 | async-start | bytes 10321920 | tf_op jit(solution)/shard_map/reduce_scatter | solution.py:94
  538.7 251.1 %reduce-scatter.11.cloned.1.call-start = ((), (), s32[]{:S(2)}) async-start(), calls=%async_computation.11 | async-start | bytes 3317760 | tf_op jit(solution)/shard_map/reduce_scatter | solution.py:94
  550.5 26.8 %collective-permute-start.52 = (bf16[64,2304]{1,0:T(8,128)(2,1)}, bf16[64,2304]{1,0:T(8,128)(2,1)S(1)}, u32[]{:S(2)}, u32[]{:S(2)}) collective-permute-start(bf16[64,2304]{1,0:T(8,128)(2,1)} %get-tuple-element.146), channel_id=1, source_target_pairs={{0,16},{4,20},{16,0},{20,4},{1,17},{5,21},{17,1},{21,5},{2,18},{6,... | collective-permute-start | bytes 884744 | tf_op jit(solution)/shard_map/ppermute | solution.py:36
  574.9 116.5 %collective-permute-start.70 = (bf16[184,2304]{1,0:T(8,128)(2,1)}, bf16[184,2304]{1,0:T(8,128)(2,1)}, u32[]{:S(2)}, u32[]{:S(2)}) collective-permute-start(bf16[184,2304]{1,0:T(8,128)(2,1)} %get-tuple-element.129), channel_id=1, source_target_pairs={{0,8},{8,0},{1,9},{9,1},{2,10},{10,2},{3,11},{11,3},{4,12},{12,4},... | collective-permute-start | bytes 2543624 | tf_op jit(solution)/shard_map/ppermute | solution.py:103
  607.1 112.3 %collective-permute-start.61 = (bf16[64,2304]{1,0:T(8,128)(2,1)}, bf16[64,2304]{1,0:T(8,128)(2,1)}, u32[]{:S(2)}, u32[]{:S(2)}) collective-permute-start(bf16[64,2304]{1,0:T(8,128)(2,1)} %get-tuple-element.143), channel_id=1, source_target_pairs={{0,16},{4,20},{16,0},{20,4},{1,17},{5,21},{17,1},{21,5},{2,18},{6,... | collective-permute-start | bytes 884744 | tf_op jit(solution)/shard_map/ppermute | solution.py:36
  609.2 103.9 %collective-permute-start.63 = (bf16[64,2304]{1,0:T(8,128)(2,1)}, bf16[64,2304]{1,0:T(8,128)(2,1)}, u32[]{:S(2)}, u32[]{:S(2)}) collective-permute-start(bf16[64,2304]{1,0:T(8,128)(2,1)} %get-tuple-element.144), channel_id=1, source_target_pairs={{0,20},{4,16},{16,4},{20,0},{1,21},{5,17},{17,5},{21,1},{2,22},{6,... | collective-permute-start | bytes 884744 | tf_op jit(solution)/shard_map/ppermute | solution.py:36
  610.7 76.4 %collective-permute-start.55 = (bf16[288,2944]{1,0:T(8,128)(2,1)}, bf16[288,2944]{1,0:T(8,128)(2,1)}, u32[]{:S(2)}, u32[]{:S(2)}) collective-permute-start(bf16[288,2944]{1,0:T(8,128)(2,1)} %get-tuple-element.117), channel_id=1, source_target_pairs={{0,8},{8,0},{1,9},{9,1},{2,10},{10,2},{3,11},{11,3},{4,12},{12,4},... | collective-permute-start | bytes 5087240 | tf_op jit(solution)/shard_map/ppermute | solution.py:103
  709.8 30.1 %collective-permute-start.48 = (bf16[64,2304]{1,0:T(8,128)(2,1)S(1)}, bf16[64,2304]{1,0:T(8,128)(2,1)S(1)}, u32[]{:S(2)}, u32[]{:S(2)}) collective-permute-start(bf16[64,2304]{1,0:T(8,128)(2,1)S(1)} %get-tuple-element.140), channel_id=1, source_target_pairs={{0,16},{4,20},{16,0},{20,4},{1,17},{5,21},{17,1},{21,5},{2,18},{6,... | collective-permute-start | bytes 884744 | tf_op jit(solution)/shard_map/ppermute | solution.py:36
  713.1 26.9 %collective-permute-start.59 = (bf16[64,2304]{1,0:T(8,128)(2,1)S(1)}, bf16[64,2304]{1,0:T(8,128)(2,1)S(1)}, u32[]{:S(2)}, u32[]{:S(2)}) collective-permute-start(bf16[64,2304]{1,0:T(8,128)(2,1)S(1)} %get-tuple-element.142), channel_id=1, source_target_pairs={{0,4},{4,0},{16,20},{20,16},{1,5},{5,1},{17,21},{21,17},{2,6},{6,2... | collective-permute-start | bytes 884744 | tf_op jit(solution)/shard_map/ppermute | solution.py:36
  718.8 44.6 %collective-permute-start.64 = (bf16[288,1792]{1,0:T(8,128)(2,1)S(1)}, bf16[288,1792]{1,0:T(8,128)(2,1)S(1)}, u32[]{:S(2)}, u32[]{:S(2)}) collective-permute-start(bf16[288,1792]{1,0:T(8,128)(2,1)S(1)} %get-tuple-element.119), channel_id=1, source_target_pairs={{0,8},{8,0},{1,9},{9,1},{2,10},{10,2},{3,11},{11,3},{4,12},{12,4},... | collective-permute-start | bytes 3096584 | tf_op jit(solution)/shard_map/ppermute | solution.py:103
  (154 other events, 1525.6 us)
Sparse Core Ops, SparseCore 0:
  83.2 57.7 all-gather.4
  143.1 29.5 all-gather.6
  207.1 85.5 all-gather.8
  294.7 49.1 all-gather.10
  398.6 61.1 reduce-scatter.4
  462.3 106.5 reduce-scatter.6
  571.5 70.5 reduce-scatter.8
  644.7 34.7 reduce-scatter.10

commit v10 on v9

--- a/solution.py
+++ b/solution.py
@@ -333,8 +333,9 @@
         own_branch1.append((BRANCH_SCALE * grad_mid).astype(BF16))
         branch1.append(plane_gather(own_branch1[s]))
 
+    y_terms = [dot(after(m, gu_terms, *own_branch1), w_down).astype(BF16) for m in mixes]
+
     grad_qkv = []
-    input_grads = []
     for s in range(count):
         queries, keys, values, probs, attended = kept[s]
         grad_att = dot(after(branch1[s], down_part), w_out, NT).astype(BF16)
@@ -364,6 +365,10 @@
     out_part = line_scatter(out_terms)
     factor_one = [norm_factor(v) for v in x_float]
 
+    outputs = []
+    for s in range(count):
+        y_sum = plane_scatter(y_terms[s], out_terms)
+        outputs.append((mids[s] + BRANCH_SCALE * y_sum).astype(BF16))
     input_grads = []
     for s in range(count):
         grad_norm = plane_scatter(all_in_terms[s], gu_part)
@@ -371,13 +376,8 @@
         input_grads.append(
             (grad_mids[s] + norm_back(x_float[s], factor_one[s], grad_norm)).astype(BF16)
         )
-    y_terms = [dot(after(m, out_terms), w_down).astype(BF16) for m in mixes]
     gu_mine = half_scatter(gu_part, BF16, qkv_part, *input_grads)
     gu_raw = plane_exchange(gu_mine.reshape(4, rows, 2 * hidden))
-    outputs = []
-    for s in range(count):
-        y_sum = plane_scatter(y_terms[s], gu_raw)
-        outputs.append((mids[s] + BRANCH_SCALE * y_sum).astype(BF16))
     qkv_mine = half_scatter(qkv_part, BF16, gu_mine)
     qkv_raw = plane_exchange(qkv_mine.reshape(4, rows, 3 * part + spare))
     out_part = after(out_part, gu_mine)

time: 822 us -> 845 us (1.028)
  waiting for transfers between devices: 383 us -> 418 us
    ppermute x3, waiting for transfers between devices: 65 us -> 99.3 us  [half_scatter(): other = lax.ppermute(other, 'h', [(0, 1), (1, 0)])]
    reduce_scatter x4, waiting for transfers between devices: 26.4 us -> 10.5 us  [line_scatter(): return lax.psum_scatter(partial, LINE, scatter_dimension=0, tiled=True)]
    ppermute x60, waiting for transfers between devices: 157 us -> 170 us  [flip_send(): return lax.ppermute(block, PLANE, [(p, p ^ flip) for p in range(4)])]
    unnamed x205 -> x219, local copies, waits for them, and re-layouts: 21.5 us -> 19.8 us
  transfers between devices with their start and end apart: 79 -> 79, of which waited for: 42 -> 41; matrix products, arithmetic and copies ran while one was open for 36% -> 34% of each run, Pallas kernels for 0% -> 0%
where the time goes in v10:
time: 845 us; the launch traced here: 840 us
  waiting for transfers between devices  418 us (49%)
  local copies, waits for them, and re-layouts  131 us (16%)
  matrix products  118 us (14%)
  starting transfers between devices  85.4 us (10%)
  other arithmetic  71.4 us (8%)
  between operations  16.3 us (2%)
    ppermute x60, waiting for transfers between devices, flip_send(): return lax.ppermute(block, PLANE, [(p, p ^ flip) for p in range(4)])  170 us
    ppermute x2, waiting for transfers between devices, half_gather(): other = lax.ppermute(block, 'h', [(0, 1), (1, 0)])  120 us
    dot_general x21, matrix products, dot(): lax.dot_general(left, right, (contract, ((), ())), preferred_element_type...  111 us
    ppermute x3, waiting for transfers between devices, half_scatter(): other = lax.ppermute(other, 'h', [(0, 1), (1, 0)])  99.3 us
    ppermute x60, starting transfers between devices, flip_send(): return lax.ppermute(block, PLANE, [(p, p ^ flip) for p in range(4)])  64.3 us
    unnamed x219, local copies, waits for them, and re-layouts  19.8 us
    reshape x12, local copies, waits for them, and re-layouts, from_line(): blocks = tokens.reshape(count, 2, 2, -1, 2, 2, rows)  18.4 us
  transfers between devices with their start and end apart: 79, of which 41 were waited for; matrix products, arithmetic and copies ran while one was open for 34% of the time, Pallas kernels for 0%

profile of v10, /device:TPU:0, one launch (start us, length us, event | category | flops | bytes accessed | tf_op | source)
XLA Modules:
  0.0 839.6 jit_solution(14427853954572401017)
XLA Ops:
  21.4 6.5 collective-permute-done.5
  35.9 45.0 %collective-permute-done.6 = bf16[288,1792]{1,0:T(8,128)(2,1)S(1)} collective-permute-done((bf16[288,1792]{1,0:T(8,128)(2,1)S(1)}, bf16[288,1792]{1,0:T(8,128)(2,1)S(1)}, u32[]{:S(2)}, u32[]{:S(2)}) %collective-permute-start.6) | collective-permute-done | bytes 1032224 | tf_op jit(solution)/shard_map/ppermute | solution.py:88
  110.3 7.2 collective-permute-done.9
  117.6 9.7 %collective-permute-done.8 = bf16[72,2944]{1,0:T(8,128)(2,1)S(1)} collective-permute-done((bf16[72,2944]{1,0:T(8,128)(2,1)S(1)}, bf16[72,2944]{1,0:T(8,128)(2,1)S(1)}, u32[]{:S(2)}, u32[]{:S(2)}) %collective-permute-start.8) | collective-permute-done | bytes 423968 | tf_op jit(solution)/shard_map/ppermute | solution.py:36
  129.6 75.0 %collective-permute-done.10 = bf16[288,2944]{1,0:T(8,128)(2,1)S(1)} collective-permute-done((bf16[288,2944]{1,0:T(8,128)(2,1)S(1)}, bf16[288,2944]{1,0:T(8,128)(2,1)S(1)}, u32[]{:S(2)}, u32[]{:S(2)}) %collective-permute-start.10) | collective-permute-done | bytes 1695776 | tf_op jit(solution)/shard_map/ppermute | solution.py:88
  232.6 8.5 %collective-permute-done.22 = bf16[64,2304]{1,0:T(8,128)(2,1)S(1)} collective-permute-done((bf16[64,2304]{1,0:T(8,128)(2,1)S(1)}, bf16[64,2304]{1,0:T(8,128)(2,1)S(1)}, u32[]{:S(2)}, u32[]{:S(2)}) %collective-permute-start.22) | collective-permute-done | bytes 294944 | tf_op jit(solution)/shard_map/ppermute | solution.py:36
  250.9 7.4 fusion.174
  262.3 7.5 fusion.176
  303.0 9.6 %collective-permute-done.23 = bf16[64,2304]{1,0:T(8,128)(2,1)S(1)} collective-permute-done((bf16[64,2304]{1,0:T(8,128)(2,1)S(1)}, bf16[64,2304]{1,0:T(8,128)(2,1)S(1)}, u32[]{:S(2)}, u32[]{:S(2)}) %collective-permute-start.23) | collective-permute-done | bytes 294944 | tf_op jit(solution)/shard_map/ppermute | solution.py:36
  363.6 6.6 collective-permute-done.28
  374.7 7.6 fusion.175
  392.4 6.2 convolution_convert_fusion.2
  401.5 8.1 multiply_convert_fusion.1
  415.1 7.5 convolution_convert_fusion.9
  422.7 8.8 %convolution_convert_fusion.8 = bf16[256,2304]{1,0:T(8,128)(2,1)} fusion(bf16[256,2944]{1,0:T(8,128)(2,1)S(1)} %pad_maximum_fusion.5, bf16[2304,2944]{1,0:T(8,128)(2,1)} %all-gather.9.cloned.1.call-done), kind=kOutput, calls=%fused_computation.10 | convolution fusion | flops 3473473536 | bytes 16252928 | tf_op jit(solution)/shard_map/dot_general | solution.py:28
  431.5 10.1 %convolution_convert_fusion = bf16[2304,2944]{1,0:T(8,128)(2,1)} fusion(bf16[512,2304]{1,0:T(8,128)(2,1)S(1)} %copy-done.25, bf16[256,2944]{1,0:T(8,128)(2,1)S(1)} %pad_maximum_fusion.5, bf16[256,2944]{1,0:T(8,128)(2,1)S(1)} %pad_maximum_fusion.4), kind=kOutput, calls=%fused_computation.2 | convolution fusion | flops 6958579712 | bytes 18939904 | tf_op jit(solution)/shard_map/dot_general | solution.py:28
  449.0 12.5 %collective-permute-done.39 = bf16[64,2304]{1,0:T(8,128)(2,1)S(1)} collective-permute-done((bf16[64,2304]{1,0:T(8,128)(2,1)S(1)}, bf16[64,2304]{1,0:T(8,128)(2,1)S(1)}, u32[]{:S(2)}, u32[]{:S(2)}) %collective-permute-start.39) | collective-permute-done | bytes 294944 | tf_op jit(solution)/shard_map/ppermute | solution.py:36
  530.2 6.7 convolution_convert_fusion.1
  613.1 6.9 collective-permute-done.49
  631.5 10.5 %reduce-scatter.9.cloned.1.call-done = bf16[576,1792]{1,0:T(8,128)(2,1)} async-done(((bf16[2304,1792]{1,0:T(8,128)(2,1)}), bf16[576,1792]{1,0:T(8,128)(2,1)}) %reduce-scatter.9.cloned.1.call-update) | async-done | bytes 2064400 | tf_op jit(solution)/shard_map/reduce_scatter | solution.py:94
  646.0 99.3 %collective-permute-done.60 = bf16[288,2944]{1,0:T(8,128)(2,1)} collective-permute-done((bf16[288,2944]{1,0:T(8,128)(2,1)}, bf16[288,2944]{1,0:T(8,128)(2,1)}, u32[]{:S(2)}, u32[]{:S(2)}) %collective-permute-start.60) | collective-permute-done | bytes 1695776 | tf_op jit(solution)/shard_map/ppermute | solution.py:103
  754.1 22.2 %collective-permute-done.69 = bf16[72,2944]{1,0:T(8,128)(2,1)S(1)} collective-permute-done((bf16[72,2944]{1,0:T(8,128)(2,1)S(1)}, bf16[72,2944]{1,0:T(8,128)(2,1)S(1)}, u32[]{:S(2)}, u32[]{:S(2)}) %collective-permute-start.69) | collective-permute-done | bytes 423968 | tf_op jit(solution)/shard_map/ppermute | solution.py:36
  776.3 7.9 collective-permute-done.67
  818.5 13.1 %collective-permute-done.66 = bf16[72,2304]{1,0:T(8,128)(2,1)S(1)} collective-permute-done((bf16[72,2304]{1,0:T(8,128)(2,1)S(1)}, bf16[72,2304]{1,0:T(8,128)(2,1)S(1)}, u32[]{:S(2)}, u32[]{:S(2)}) %collective-permute-start.66) | collective-permute-done | bytes 331808 | tf_op jit(solution)/shard_map/ppermute | solution.py:388
  (591 shorter events, 413.1 us)
Async XLA Ops:
  7.2 240.2 %all-gather.5.cloned.1.call-start = ((), (), s32[]{:S(2)}) async-start(), calls=%async_computation.4 | async-start | bytes 10321920 | tf_op jit(solution)/shard_map/all_gather | solution.py:75
  33.2 47.7 %collective-permute-start.6 = (bf16[288,1792]{1,0:T(8,128)(2,1)S(1)}, bf16[288,1792]{1,0:T(8,128)(2,1)S(1)}, u32[]{:S(2)}, u32[]{:S(2)}) collective-permute-start(bf16[288,1792]{1,0:T(8,128)(2,1)S(1)} %bitcast.287), channel_id=1, source_target_pairs={{0,8},{8,0},{1,9},{9,1},{2,10},{10,2},{3,11},{11,3},{4,12},{12,4},... | collective-permute-start | bytes 3096584 | tf_op jit(solution)/shard_map/ppermute | solution.py:88
  83.1 207.0 %all-gather.7.cloned.1.call-start = ((), (), s32[]{:S(2)}) async-start(), calls=%async_computation.5 | async-start | bytes 3317760 | tf_op jit(solution)/shard_map/all_gather | solution.py:75
  83.1 25.0 %collective-permute-start.13 = (bf16[72,2304]{1,0:T(8,128)(2,1)}, bf16[72,2304]{1,0:T(8,128)(2,1)S(1)}, u32[]{:S(2)}, u32[]{:S(2)}) collective-permute-start(bf16[72,2304]{1,0:T(8,128)(2,1)} %param.17), channel_id=1, source_target_pairs={{0,8},{2,9},{4,10},{6,11},{8,12},{10,13},{12,14},{14,15},{1,0},{3,... | collective-permute-start | bytes 995336 | tf_op jit(solution)/shard_map/ppermute | solution.py:217
  110.3 264.4 %all-gather.9.cloned.1.call-start = ((), (), s32[]{:S(2)}) async-start(), calls=%async_computation.6 | async-start | bytes 16957440 | tf_op jit(solution)/shard_map/all_gather | solution.py:75
  128.1 76.5 %collective-permute-start.10 = (bf16[288,2944]{1,0:T(8,128)(2,1)S(1)}, bf16[288,2944]{1,0:T(8,128)(2,1)S(1)}, u32[]{:S(2)}, u32[]{:S(2)}) collective-permute-start(bf16[288,2944]{1,0:T(8,128)(2,1)S(1)} %bitcast.278), channel_id=1, source_target_pairs={{0,8},{8,0},{1,9},{9,1},{2,10},{10,2},{3,11},{11,3},{4,12},{12,4},... | collective-permute-start | bytes 5087240 | tf_op jit(solution)/shard_map/ppermute | solution.py:88
  207.0 194.4 %all-gather.11.cloned.1.call-start = ((), (), s32[]{:S(2)}) async-start(), calls=%async_computation.7 | async-start | bytes 8478720 | tf_op jit(solution)/shard_map/all_gather | solution.py:75
  229.3 54.2 %collective-permute-start.35 = (bf16[184,2304]{1,0:T(8,128)(2,1)}, bf16[184,2304]{1,0:T(8,128)(2,1)}, u32[]{:S(2)}, u32[]{:S(2)}) collective-permute-start(bf16[184,2304]{1,0:T(8,128)(2,1)} %pad.20), channel_id=1, source_target_pairs={{0,8},{8,0},{1,9},{9,1},{2,10},{10,2},{3,11},{11,3},{4,12},{12,4},... | collective-permute-start | bytes 2543624 | tf_op jit(solution)/shard_map/ppermute | solution.py:232
  287.1 222.9 %reduce-scatter.5.cloned.1.call-start = ((), (), s32[]{:S(2)}) async-start(), calls=%async_computation.8 | async-start | bytes 8478720 | tf_op jit(solution)/shard_map/reduce_scatter | solution.py:94
  325.0 25.5 %collective-permute-start.30 = (bf16[64,2304]{1,0:T(8,128)(2,1)}, bf16[64,2304]{1,0:T(8,128)(2,1)}, u32[]{:S(2)}, u32[]{:S(2)}) collective-permute-start(bf16[64,2304]{1,0:T(8,128)(2,1)} %get-tuple-element.188), channel_id=1, source_target_pairs={{0,4},{4,0},{16,20},{20,16},{1,5},{5,1},{17,21},{21,17},{2,6},{6,2... | collective-permute-start | bytes 884744 | tf_op jit(solution)/shard_map/ppermute | solution.py:36
  398.5 170.1 %reduce-scatter.7.cloned.1.call-start = ((), (), s32[]{:S(2)}) async-start(), calls=%async_computation.9 | async-start | bytes 16957440 | tf_op jit(solution)/shard_map/reduce_scatter | solution.py:94
  441.6 200.3 %reduce-scatter.9.cloned.1.call-start = ((), (), s32[]{:S(2)}) async-start(), calls=%async_computation.10 | async-start | bytes 10321920 | tf_op jit(solution)/shard_map/reduce_scatter | solution.py:94
  537.0 274.5 %reduce-scatter.11.cloned.1.call-start = ((), (), s32[]{:S(2)}) async-start(), calls=%async_computation.11 | async-start | bytes 3317760 | tf_op jit(solution)/shard_map/reduce_scatter | solution.py:94
  572.6 37.8 %collective-permute-start.51 = (bf16[64,2304]{1,0:T(8,128)(2,1)}, bf16[64,2304]{1,0:T(8,128)(2,1)}, u32[]{:S(2)}, u32[]{:S(2)}) collective-permute-start(bf16[64,2304]{1,0:T(8,128)(2,1)} %get-tuple-element.147), channel_id=1, source_target_pairs={{0,16},{4,20},{16,0},{20,4},{1,17},{5,21},{17,1},{21,5},{2,18},{6,... | collective-permute-start | bytes 884744 | tf_op jit(solution)/shard_map/ppermute | solution.py:36
  574.0 38.6 %collective-permute-start.53 = (bf16[64,2304]{1,0:T(8,128)(2,1)}, bf16[64,2304]{1,0:T(8,128)(2,1)}, u32[]{:S(2)}, u32[]{:S(2)}) collective-permute-start(bf16[64,2304]{1,0:T(8,128)(2,1)} %get-tuple-element.148), channel_id=1, source_target_pairs={{0,20},{4,16},{16,4},{20,0},{1,21},{5,17},{17,5},{21,1},{2,22},{6,... | collective-permute-start | bytes 884744 | tf_op jit(solution)/shard_map/ppermute | solution.py:36
  579.8 33.3 %collective-permute-start.52 = (bf16[64,2304]{1,0:T(8,128)(2,1)}, bf16[64,2304]{1,0:T(8,128)(2,1)}, u32[]{:S(2)}, u32[]{:S(2)}) collective-permute-start(bf16[64,2304]{1,0:T(8,128)(2,1)} %get-tuple-element.149), channel_id=1, source_target_pairs={{0,4},{4,0},{16,20},{20,16},{1,5},{5,1},{17,21},{21,17},{2,6},{6,2... | collective-permute-start | bytes 884744 | tf_op jit(solution)/shard_map/ppermute | solution.py:36
  585.4 27.7 %collective-permute-start.42 = (bf16[64,2304]{1,0:T(8,128)(2,1)}, bf16[64,2304]{1,0:T(8,128)(2,1)}, u32[]{:S(2)}, u32[]{:S(2)}) collective-permute-start(bf16[64,2304]{1,0:T(8,128)(2,1)} %get-tuple-element.144), channel_id=1, source_target_pairs={{0,16},{4,20},{16,0},{20,4},{1,17},{5,21},{17,1},{21,5},{2,18},{6,... | collective-permute-start | bytes 884744 | tf_op jit(solution)/shard_map/ppermute | solution.py:36
  586.8 26.3 %collective-permute-start.50 = (bf16[64,2304]{1,0:T(8,128)(2,1)}, bf16[64,2304]{1,0:T(8,128)(2,1)}, u32[]{:S(2)}, u32[]{:S(2)}) collective-permute-start(bf16[64,2304]{1,0:T(8,128)(2,1)} %get-tuple-element.145), channel_id=1, source_target_pairs={{0,20},{4,16},{16,4},{20,0},{1,21},{5,17},{17,5},{21,1},{2,22},{6,... | collective-permute-start | bytes 884744 | tf_op jit(solution)/shard_map/ppermute | solution.py:36
  612.6 138.9 %collective-permute-start.70 = (bf16[184,2304]{1,0:T(8,128)(2,1)}, bf16[184,2304]{1,0:T(8,128)(2,1)}, u32[]{:S(2)}, u32[]{:S(2)}) collective-permute-start(bf16[184,2304]{1,0:T(8,128)(2,1)} %get-tuple-element.127), channel_id=1, source_target_pairs={{0,8},{8,0},{1,9},{9,1},{2,10},{10,2},{3,11},{11,3},{4,12},{12,4},... | collective-permute-start | bytes 2543624 | tf_op jit(solution)/shard_map/ppermute | solution.py:103
  623.5 121.9 %collective-permute-start.60 = (bf16[288,2944]{1,0:T(8,128)(2,1)}, bf16[288,2944]{1,0:T(8,128)(2,1)}, u32[]{:S(2)}, u32[]{:S(2)}) collective-permute-start(bf16[288,2944]{1,0:T(8,128)(2,1)} %get-tuple-element.115), channel_id=1, source_target_pairs={{0,8},{8,0},{1,9},{9,1},{2,10},{10,2},{3,11},{11,3},{4,12},{12,4},... | collective-permute-start | bytes 5087240 | tf_op jit(solution)/shard_map/ppermute | solution.py:103
  643.6 141.4 %collective-permute-start.61 = (bf16[288,1792]{1,0:T(8,128)(2,1)S(1)}, bf16[288,1792]{1,0:T(8,128)(2,1)S(1)}, u32[]{:S(2)}, u32[]{:S(2)}) collective-permute-start(bf16[288,1792]{1,0:T(8,128)(2,1)S(1)} %get-tuple-element.117), channel_id=1, source_target_pairs={{0,8},{8,0},{1,9},{9,1},{2,10},{10,2},{3,11},{11,3},{4,12},{12,4},... | collective-permute-start | bytes 3096584 | tf_op jit(solution)/shard_map/ppermute | solution.py:103
  748.0 28.3 %collective-permute-start.69 = (bf16[72,2944]{1,0:T(8,128)(2,1)S(1)}, bf16[72,2944]{1,0:T(8,128)(2,1)S(1)}, u32[]{:S(2)}, u32[]{:S(2)}) collective-permute-start(bf16[72,2944]{1,0:T(8,128)(2,1)S(1)} %get-tuple-element.131), channel_id=1, source_target_pairs={{0,20},{4,16},{16,4},{20,0},{1,21},{5,17},{17,5},{21,1},{2,22},{6,... | collective-permute-start | bytes 1271816 | tf_op jit(solution)/shard_map/ppermute | solution.py:36
  749.5 26.8 %collective-permute-start.68 = (bf16[72,2944]{1,0:T(8,128)(2,1)S(1)}, bf16[72,2944]{1,0:T(8,128)(2,1)S(1)}, u32[]{:S(2)}, u32[]{:S(2)}) collective-permute-start(bf16[72,2944]{1,0:T(8,128)(2,1)S(1)} %get-tuple-element.132), channel_id=1, source_target_pairs={{0,16},{4,20},{16,0},{20,4},{1,17},{5,21},{17,1},{21,5},{2,18},{6,... | collective-permute-start | bytes 1271816 | tf_op jit(solution)/shard_map/ppermute | solution.py:36
  749.8 34.3 %collective-permute-start.67 = (bf16[72,2944]{1,0:T(8,128)(2,1)S(1)}, bf16[72,2944]{1,0:T(8,128)(2,1)S(1)}, u32[]{:S(2)}, u32[]{:S(2)}) collective-permute-start(bf16[72,2944]{1,0:T(8,128)(2,1)S(1)} %get-tuple-element.133), channel_id=1, source_target_pairs={{0,4},{4,0},{16,20},{20,16},{1,5},{5,1},{17,21},{21,17},{2,6},{6,2... | collective-permute-start | bytes 1271816 | tf_op jit(solution)/shard_map/ppermute | solution.py:36
  (161 other events, 1607.1 us)
Sparse Core Ops, SparseCore 0:
  83.2 57.7 all-gather.4
  143.1 29.5 all-gather.6
  207.1 85.5 all-gather.8
  294.8 49.1 all-gather.10
  398.7 61.0 reduce-scatter.4
  462.2 106.3 reduce-scatter.6
  571.3 70.6 reduce-scatter.8
  644.5 34.7 reduce-scatter.10
